TPU v7x, 128 devices: a whole 4x4x4 slice. The times are simulated.
128 devices in a mesh: row: 16 (over z_hi, y, core), col: 8 (over x, z_lo).
Axes of the slice: x: 4, y: 4, z: 4 (z_hi: 2, z_lo: 2; z = z_hi * 2 + z_lo), core: 2. Of those that a mesh axis runs over, the one named last changes fastest.
Arguments:
- observed: float32 [2048, 4096], P('row', 'col'), may hold values from -6 to 6
- psf_table: bfloat16 [64, 31, 31], replicated, may hold values from 0.049804688 to 1
- psf_index: int32 [16, 32], P('row', 'col'), may hold values from 0 to 63
- start_image: float32 [2048, 4096], P('row', 'col'), may hold values from -6 to 6
- blur_dual: float32 [2048, 4096], P('row', 'col'), may hold values from -6 to 6
- tv_dual: float32 [2, 2048, 4096], P(None, 'row', 'col'), may hold values from -1.8 to 1.8
Outputs:
- restored: float32 [2048, 4096], P('row', 'col')
- blur_dual_out: float32 [2048, 4096], P('row', 'col')
Inputs may be any that keep to these rules, and one draw needn't show every extreme that they name: `psf_index`: each entry names a row of psf_table.
All inputs are finite; a program needn't handle non-finite values.
Results may differ from a plain program's by a relative error of at most 0.0003.
Values may be sent and summed in bfloat16 or wider, within the bound.
No kernel may reach another device: no remote copies, remote signals or barrier semaphores. Data moves between devices by JAX's collectives and lax.ppermute only.
A program may use at most 128 MiB of HBM per device.

v0:
```python
import jax
import jax.numpy as jnp
from jax import lax
from jax.sharding import PartitionSpec as P

ITERS = 2


sigma_step = 0.15
tau_step = 0.6
tv_weight = 0.5
group_size = 4


def for_sending(value):

    def short(part):
        return part.astype(jnp.bfloat16) if part.dtype == jnp.float32 else part

    return jax.tree.map(short, value)


def from_behind(block, axis, distance):
    devices = range(lax.axis_size(axis))
    route = [(i - distance, i) for i in devices if i - distance in devices]
    return lax.ppermute(block, axis, route)


def extended_2(cells, sides, width):
    for axis, dim in sides:
        count = lax.axis_size(axis)
        ends = count - 1
        head = lax.slice_in_dim(cells, 0, width, axis=dim)
        tail = lax.slice_in_dim(cells, cells.shape[dim] - width, cells.shape[dim], axis=dim)
        cells = jnp.concatenate(
            [
                lax.ppermute(tail, axis, [(i, (i + 1) % count) for i in range(ends)]),
                cells,
                lax.ppermute(head, axis, [((i + 1) % count, i) for i in range(ends)]),
            ],
            axis=dim,
        )
    return cells


def make_select(kernel_size, patch_cols):
    half_width = kernel_size // 2
    column_in = jnp.arange(patch_cols + 2 * half_width, dtype=jnp.int32)[None, :, None]
    column_out = jnp.arange(patch_cols, dtype=jnp.int32)[None, None, :]
    tap_index = jnp.arange(kernel_size, dtype=jnp.int32)[:, None, None]
    return (column_in - column_out == tap_index).astype(jnp.bfloat16)


def strip_pass(strip_in, observed_s, dual_s, index_s, kern_flat, select):
    kernel_size = select.shape[0]
    patch_cols = select.shape[2]
    half_width = (select.shape[1] - patch_cols) // 2
    patch_rows, width = observed_s.shape
    group_span = group_size * patch_cols
    group_count = width // group_span
    table_size = kern_flat.shape[0]

    def one_group(spread_sum, group_id):
        pieces = jnp.stack(
            [
                strip_in[:, member * patch_cols : member * patch_cols + patch_cols + 2 * half_width]
                for member in range(group_size)
            ]
        )
        stacked = jnp.stack(
            [pieces[:, tap_row : tap_row + patch_rows, :] for tap_row in range(kernel_size)], axis=2
        )
        onehot = (index_s[:, None] == jnp.arange(table_size, dtype=jnp.int32)[None, :]).astype(
            jnp.bfloat16
        )
        kernels = jnp.dot(onehot, kern_flat, preferred_element_type=jnp.float32).astype(
            jnp.bfloat16
        )
        kernels = kernels.reshape(group_size, kernel_size, kernel_size)
        toeplitz = jnp.einsum(
            "pab,bkj->pakj", kernels, select, preferred_element_type=jnp.float32
        ).astype(jnp.bfloat16)
        blurred = jnp.einsum(
            "piak,pakj->pij", stacked, toeplitz, preferred_element_type=jnp.float32
        )
        blurred = blurred.transpose(1, 0, 2).reshape(patch_rows, group_span)
        dual_new = (dual_s + sigma_step * (blurred - observed_s)) / (1.0 + sigma_step)
        rounded = (
            dual_new.astype(jnp.bfloat16)
            .reshape(patch_rows, group_size, patch_cols)
            .transpose(1, 0, 2)
        )
        padded_dual = jnp.pad(rounded, ((0, 0), (kernel_size - 1, kernel_size - 1), (0, 0)))
        shifted = jnp.stack(
            [
                padded_dual[
                    :,
                    kernel_size
                    - 1
                    - tap_row : kernel_size
                    - 1
                    - tap_row
                    + patch_rows
                    + 2 * half_width,
                    :,
                ]
                for tap_row in range(kernel_size)
            ],
            axis=2,
        )
        spread = jnp.einsum("praj,pakj->prk", shifted, toeplitz, preferred_element_type=jnp.float32)
        merged = jnp.zeros((patch_rows + 2 * half_width, group_span + 2 * half_width), jnp.float32)
        for member in range(group_size):
            merged = merged.at[
                :, member * patch_cols : member * patch_cols + patch_cols + 2 * half_width
            ].add(spread[member])
        previous = spread_sum
        spread_sum = previous + merged
        return (spread_sum, dual_new)

    start_sum = jnp.zeros((patch_rows + 2 * half_width, width + 2 * half_width), jnp.float32)
    spread_sum, duals = lax.scan(one_group, start_sum, jnp.arange(group_count, dtype=jnp.int32))
    return (duals.transpose(1, 0, 2).reshape(patch_rows, width), spread_sum)


def fold_rows(extended, extra, half_width):
    above_rim, above_extra = (
        from_behind(extended[-half_width:].astype(jnp.bfloat16), "row", 1).astype(jnp.float32),
        from_behind(for_sending(extra), "row", 1).astype(extra.dtype),
    )
    below_rim = from_behind(extended[:half_width], "row", -1)
    middle = extended[half_width:-half_width]
    middle = middle.at[:half_width].add(above_rim)
    middle = middle.at[-half_width:].add(below_rim)
    return (middle, above_extra)


def fold_cols(extended, extra, half_width):
    left_rim, left_extra = from_behind((extended[:, -half_width:], extra), "col", 1)
    right_rim = from_behind(extended[:, :half_width], "col", -1)
    middle = extended[:, half_width:-half_width]
    middle = middle.at[:, :half_width].add(left_rim)
    middle = middle.at[:, -half_width:].add(right_rim)
    return (middle, left_extra)


def per_device(observed, psf_table, psf_index, start_image, blur_dual, tv_dual):
    kernel_size = psf_table.shape[1]
    half_width = kernel_size // 2
    tile_rows, tile_cols = observed.shape
    table_size = psf_table.shape[0]
    table = psf_table.astype(jnp.float32)
    normed = table / jnp.sum(table, axis=(1, 2), keepdims=True)
    kern_flat = normed.astype(jnp.bfloat16).reshape(table_size, kernel_size * kernel_size)
    patch_cols = tile_cols // psf_index.shape[1]
    select = make_select(kernel_size, patch_cols)
    row_place = lax.axis_index("row") * tile_rows + jnp.arange(tile_rows, dtype=jnp.int32)
    col_place = lax.axis_index("col") * tile_cols + jnp.arange(tile_cols, dtype=jnp.int32)
    keep_rows = (row_place < tile_rows * lax.axis_size("row") - 1)[:, None]
    keep_cols = (col_place < tile_cols * lax.axis_size("col") - 1)[None, :]
    restored = start_image
    extrapolated = start_image
    dual_now = blur_dual
    tv_rows = tv_dual[0]
    tv_cols = tv_dual[1]
    for step in range(ITERS):
        padded = extended_2(extrapolated, (("row", 0), ("col", 1)), half_width)
        strip_in = padded.astype(jnp.bfloat16)
        below = padded[
            half_width + 1 : half_width + 1 + tile_rows, half_width : half_width + tile_cols
        ]
        right = padded[
            half_width : half_width + tile_rows, half_width + 1 : half_width + 1 + tile_cols
        ]
        grad_rows = jnp.where(keep_rows, below - extrapolated, 0.0)
        grad_cols = jnp.where(keep_cols, right - extrapolated, 0.0)
        dual_now, spread_sum = strip_pass(
            strip_in, observed, dual_now, psf_index[0], kern_flat, select
        )
        moved_rows = tv_rows + sigma_step * grad_rows
        moved_cols = tv_cols + sigma_step * grad_cols
        shrink = jnp.maximum(
            1.0, jnp.sqrt(moved_rows * moved_rows + moved_cols * moved_cols) / tv_weight
        )
        tv_rows = moved_rows / shrink
        tv_cols = moved_cols / shrink
        masked_rows = jnp.where(keep_rows, tv_rows, 0.0)
        masked_cols = jnp.where(keep_cols, tv_cols, 0.0)
        middle, edge_col = fold_cols(spread_sum, masked_cols[:, -1:], half_width)
        adjoint, edge_row = fold_rows(middle, masked_rows[-1:], half_width)
        diverge = masked_rows - jnp.concatenate([edge_row, masked_rows[:-1]], axis=0)
        diverge = diverge + masked_cols - jnp.concatenate([edge_col, masked_cols[:, :-1]], axis=1)
        next_image = restored - tau_step * (adjoint - diverge)
        extrapolated = 2.0 * next_image - restored
        restored = next_image
    return (restored, dual_now)


def solution(mesh):
    placed = (
        P("row", "col"),
        P(),
        P("row", "col"),
        P("row", "col"),
        P("row", "col"),
        P(None, "row", "col"),
    )
    return jax.shard_map(
        per_device,
        mesh=mesh,
        in_specs=placed,
        out_specs=(P("row", "col"), P("row", "col")),
        check_vma=False,
    )
```

profile of v0, /device:TPU:96, one launch (start us, length us, event | category | flops | bytes accessed | tf_op | source)
XLA Modules:
  0.0 168.6 jit_solution(8009175019211469860)
XLA Ops:
  1.6 1.9 %collective-permute-start = (f32[15,512]{0,1:T(8,128)S(1)}, f32[15,512]{0,1:T(8,128)S(1)}, u32[]{:S(2)}, u32[]{:S(2)}) collective-permute-start(f32[15,512]{0,1:T(8,128)S(1)} %copy.248), channel_id=1, source_target_pairs={{0,8},{8,16},{16,24},{24,32},{32,40},{40,48},{48,56},{56,64},{64,7... | collective-permute-start | bytes 92168 | tf_op jit(solution)/shard_map/ppermute | solution.py:37
  3.7 7.3 %collective-permute-start.1 = (f32[15,512]{0,1:T(8,128)S(1)}, f32[15,512]{0,1:T(8,128)S(1)}, u32[]{:S(2)}, u32[]{:S(2)}) collective-permute-start(f32[15,512]{0,1:T(8,128)S(1)} %copy.249), channel_id=1, source_target_pairs={{8,0},{16,8},{24,16},{32,24},{40,32},{48,40},{56,48},{64,56},{72,6... | collective-permute-start | bytes 92168 | tf_op jit(solution)/shard_map/ppermute | solution.py:39
  14.2 3.8 %convolution_convert_fusion = bf16[4,31,158,128]{3,1,2,0:T(8,128)(2,1)} fusion(s32[158,128]{1,0:T(8,128)S(1)} %iota_subtract_fusion, bf16[4,31,31,1]{2,1,0,3:T(8,128)(2,1)S(1)} %reshape.545), kind=kOutput, calls=%fused_computation.8 | convolution fusion | flops 158616832 | bytes 5104136 | tf_op jit(solution)/shard_map/while/body/eval_jaxpr/pab,bkj->pakj/dot_general | solution.py:80
  18.5 2.3 %collective-permute-start.3 = (f32[158,15]{0,1:T(8,128)S(1)}, f32[158,15]{0,1:T(8,128)S(1)}, u32[]{:S(2)}, u32[]{:S(2)}) collective-permute-start(f32[158,15]{0,1:T(8,128)S(1)} %slice.1229), channel_id=1, source_target_pairs={{1,0},{2,1},{3,2},{4,3},{5,4},{6,5},{7,6},{9,8},{10,9},{11,10},{12... | collective-permute-start | bytes 28448 | tf_op jit(solution)/shard_map/ppermute | solution.py:39
  20.9 4.4 %collective-permute-start.2 = (bf16[158,15]{0,1:T(8,128)(2,1)S(1)}, bf16[158,15]{0,1:T(8,128)(2,1)S(1)}, u32[]{:S(2)}, u32[]{:S(2)}) collective-permute-start(bf16[158,15]{0,1:T(8,128)(2,1)S(1)} %slice.1226), channel_id=1, source_target_pairs={{0,1},{1,2},{2,3},{3,4},{4,5},{5,6},{6,7},{8,9},{9,10},{10,11},{11... | collective-permute-start | bytes 14228 | tf_op jit(solution)/shard_map/ppermute | solution.py:37
  25.4 8.8 %copy.382 = bf16[4,31,158,128]{3,0,2,1:T(4,128)(2,1)} copy(bf16[4,31,158,128]{3,1,2,0:T(8,128)(2,1)} %convolution_convert_fusion) | data formatting | bytes 10031104
  41.3 1.9 %fusion.6 = f32[4,128,128,1]{1,2,3,0:T(8,128)S(1)} fusion(bf16[4,128,31,158]{1,3,2,0:T(8,128)(2,1)S(1)} %constant_dynamic-update-slice_fusion, bf16[4,31,158,128]{3,0,2,1:T(4,128)(2,1)S(1)} %copy-done), kind=kOutput, calls=%fused_computation.6 | convolution fusion | flops 641990656 | bytes 10293248 | tf_op jit(solution)/shard_map/while/body/eval_jaxpr/piak,pakj->pij/dot_general | solution.py:83
  45.2 4.0 %fusion.11 = f32[4,158,158]{1,2,0:T(8,128)S(1)} fusion(bf16[4,158,31,128]{3,1,2,0:T(8,128)(2,1)S(1)} %constant_dynamic-update-slice_fusion.31, bf16[4,31,158,128]{3,0,2,1:T(4,128)(2,1)} %copy.382), kind=kOutput, calls=%fused_computation.12 | convolution fusion | flops 792457216 | bytes 10430528 | tf_op jit(solution)/shard_map/while/body/eval_jaxpr/praj,pakj->prk/dot_general | solution.py:111
  53.6 2.3 %collective-permute-start.4 = (f32[158,15]{0,1:T(8,128)S(1)}, f32[158,15]{0,1:T(8,128)S(1)}, u32[]{:S(2)}, u32[]{:S(2)}) collective-permute-start(f32[158,15]{0,1:T(8,128)S(1)} %slice.1269), channel_id=1, source_target_pairs={{0,1},{1,2},{2,3},{3,4},{4,5},{5,6},{6,7},{8,9},{9,10},{10,11},{11... | collective-permute-start | bytes 28448 | tf_op jit(solution)/shard_map/ppermute | solution.py:26
  56.0 3.3 %collective-permute-done.4 = f32[158,15]{0,1:T(8,128)S(1)} collective-permute-done((f32[158,15]{0,1:T(8,128)S(1)}, f32[158,15]{0,1:T(8,128)S(1)}, u32[]{:S(2)}, u32[]{:S(2)}) %collective-permute-start.4) | collective-permute-done | bytes 9512 | tf_op jit(solution)/shard_map/ppermute | solution.py:26
  59.8 1.9 %collective-permute-start.5 = (f32[158,15]{0,1:T(8,128)S(1)}, f32[158,15]{0,1:T(8,128)S(1)}, u32[]{:S(2)}, u32[]{:S(2)}) collective-permute-start(f32[158,15]{0,1:T(8,128)S(1)} %get-tuple-element.309), channel_id=1, source_target_pairs={{1,0},{2,1},{3,2},{4,3},{5,4},{6,5},{7,6},{9,8},{10,9},{11,10},{12... | collective-permute-start | bytes 28448 | tf_op jit(solution)/shard_map/ppermute | solution.py:26
  62.3 4.0 %collective-permute-done.5 = f32[158,15]{0,1:T(8,128)S(1)} collective-permute-done((f32[158,15]{0,1:T(8,128)S(1)}, f32[158,15]{0,1:T(8,128)S(1)}, u32[]{:S(2)}, u32[]{:S(2)}) %collective-permute-start.5) | collective-permute-done | bytes 9512 | tf_op jit(solution)/shard_map/ppermute | solution.py:26
  66.6 1.9 %collective-permute-start.6 = (bf16[15,512]{0,1:T(8,128)(2,1)S(1)}, bf16[15,512]{0,1:T(8,128)(2,1)S(1)}, u32[]{:S(2)}, u32[]{:S(2)}) collective-permute-start(bf16[15,512]{0,1:T(8,128)(2,1)S(1)} %slice.1883), channel_id=1, source_target_pairs={{0,8},{8,16},{16,24},{24,32},{32,40},{40,48},{48,56},{56,64},{64,7... | collective-permute-start | bytes 46088 | tf_op jit(solution)/shard_map/ppermute | solution.py:26
  70.0 1.9 %collective-permute-start.8 = (bf16[1,512]{0,1:T(8,128)(2,1)S(1)}, bf16[1,512]{0,1:T(8,128)(2,1)S(1)}, u32[]{:S(2)}, u32[]{:S(2)}) collective-permute-start(bf16[1,512]{0,1:T(8,128)(2,1)S(1)} %slice.1882), channel_id=1, source_target_pairs={{0,8},{8,16},{16,24},{24,32},{32,40},{40,48},{48,56},{56,64},{64,7... | collective-permute-start | bytes 3080 | tf_op jit(solution)/shard_map/ppermute | solution.py:26
  72.0 4.6 %collective-permute-done.6 = bf16[15,512]{0,1:T(8,128)(2,1)S(1)} collective-permute-done((bf16[15,512]{0,1:T(8,128)(2,1)S(1)}, bf16[15,512]{0,1:T(8,128)(2,1)S(1)}, u32[]{:S(2)}, u32[]{:S(2)}) %collective-permute-start.6) | collective-permute-done | bytes 15392 | tf_op jit(solution)/shard_map/ppermute | solution.py:26
  77.3 2.7 %collective-permute-start.7 = (f32[15,512]{0,1:T(8,128)}, f32[15,512]{0,1:T(8,128)S(1)}, u32[]{:S(2)}, u32[]{:S(2)}) collective-permute-start(f32[15,512]{0,1:T(8,128)} %get-tuple-element.315), channel_id=1, source_target_pairs={{8,0},{16,8},{24,16},{32,24},{40,32},{48,40},{56,48},{64,56},{72,6... | collective-permute-start | bytes 92168 | tf_op jit(solution)/shard_map/ppermute | solution.py:26
  80.1 2.4 %collective-permute-start.9 = (f32[128,1]{0,1:T(1,128)S(1)}, f32[128,1]{0,1:T(1,128)S(1)}, u32[]{:S(2)}, u32[]{:S(2)}) collective-permute-start(f32[128,1]{0,1:T(1,128)S(1)} %slice.1279), channel_id=1, source_target_pairs={{0,1},{1,2},{2,3},{3,4},{4,5},{5,6},{6,7},{8,9},{9,10},{10,11},{11... | collective-permute-start | bytes 1544 | tf_op jit(solution)/shard_map/ppermute | solution.py:26
  86.1 2.2 %collective-permute-start.10 = (f32[15,512]{0,1:T(8,128)S(1)}, f32[15,512]{0,1:T(8,128)S(1)}, u32[]{:S(2)}, u32[]{:S(2)}) collective-permute-start(f32[15,512]{0,1:T(8,128)S(1)} %get-tuple-element.321), channel_id=1, source_target_pairs={{0,8},{8,16},{16,24},{24,32},{32,40},{40,48},{48,56},{56,64},{64,7... | collective-permute-start | bytes 92168 | tf_op jit(solution)/shard_map/ppermute | solution.py:37
  88.3 7.3 %collective-permute-start.11 = (f32[15,512]{0,1:T(8,128)S(1)}, f32[15,512]{0,1:T(8,128)S(1)}, u32[]{:S(2)}, u32[]{:S(2)}) collective-permute-start(f32[15,512]{0,1:T(8,128)S(1)} %get-tuple-element.322), channel_id=1, source_target_pairs={{8,0},{16,8},{24,16},{32,24},{40,32},{48,40},{56,48},{64,56},{72,6... | collective-permute-start | bytes 92168 | tf_op jit(solution)/shard_map/ppermute | solution.py:39
  95.6 2.2 %collective-permute-done.10 = f32[15,512]{0,1:T(8,128)S(1)} collective-permute-done((f32[15,512]{0,1:T(8,128)S(1)}, f32[15,512]{0,1:T(8,128)S(1)}, u32[]{:S(2)}, u32[]{:S(2)}) %collective-permute-start.10) | collective-permute-done | bytes 30752 | tf_op jit(solution)/shard_map/ppermute | solution.py:37
  99.8 3.0 %collective-permute-start.13 = (f32[158,15]{0,1:T(8,128)S(1)}, f32[158,15]{0,1:T(8,128)S(1)}, u32[]{:S(2)}, u32[]{:S(2)}) collective-permute-start(f32[158,15]{0,1:T(8,128)S(1)} %slice.1286), channel_id=1, source_target_pairs={{1,0},{2,1},{3,2},{4,3},{5,4},{6,5},{7,6},{9,8},{10,9},{11,10},{12... | collective-permute-start | bytes 28448 | tf_op jit(solution)/shard_map/ppermute | solution.py:39
  102.8 3.9 %collective-permute-start.12 = (bf16[158,15]{0,1:T(8,128)(2,1)S(1)}, bf16[158,15]{0,1:T(8,128)(2,1)S(1)}, u32[]{:S(2)}, u32[]{:S(2)}) collective-permute-start(bf16[158,15]{0,1:T(8,128)(2,1)S(1)} %slice.1283), channel_id=1, source_target_pairs={{0,1},{1,2},{2,3},{3,4},{4,5},{5,6},{6,7},{8,9},{9,10},{10,11},{11... | collective-permute-start | bytes 14228 | tf_op jit(solution)/shard_map/ppermute | solution.py:37
  117.6 4.0 %fusion.14 = f32[4,158,158]{1,2,0:T(8,128)S(1)} fusion(bf16[4,158,31,128]{3,1,2,0:T(8,128)(2,1)S(1)} %constant_dynamic-update-slice_fusion.93, bf16[4,31,158,128]{3,0,2,1:T(4,128)(2,1)} %copy.382), kind=kOutput, calls=%fused_computation.13 | convolution fusion | flops 792457216 | bytes 10430528 | tf_op jit(solution)/shard_map/while/body/eval_jaxpr/praj,pakj->prk/dot_general | solution.py:111
  127.9 4.6 %collective-permute-start.14 = (f32[158,15]{0,1:T(8,128)S(1)}, f32[158,15]{0,1:T(8,128)S(1)}, u32[]{:S(2)}, u32[]{:S(2)}) collective-permute-start(f32[158,15]{0,1:T(8,128)S(1)} %slice.1326), channel_id=1, source_target_pairs={{0,1},{1,2},{2,3},{3,4},{4,5},{5,6},{6,7},{8,9},{9,10},{10,11},{11... | collective-permute-start | bytes 28448 | tf_op jit(solution)/shard_map/ppermute | solution.py:26
  134.6 1.9 %collective-permute-start.15 = (f32[158,15]{0,1:T(8,128)S(1)}, f32[158,15]{0,1:T(8,128)S(1)}, u32[]{:S(2)}, u32[]{:S(2)}) collective-permute-start(f32[158,15]{0,1:T(8,128)S(1)} %get-tuple-element.307), channel_id=1, source_target_pairs={{1,0},{2,1},{3,2},{4,3},{5,4},{6,5},{7,6},{9,8},{10,9},{11,10},{12... | collective-permute-start | bytes 28448 | tf_op jit(solution)/shard_map/ppermute | solution.py:26
  136.8 4.6 %collective-permute-done.15 = f32[158,15]{0,1:T(8,128)S(1)} collective-permute-done((f32[158,15]{0,1:T(8,128)S(1)}, f32[158,15]{0,1:T(8,128)S(1)}, u32[]{:S(2)}, u32[]{:S(2)}) %collective-permute-start.15) | collective-permute-done | bytes 9512 | tf_op jit(solution)/shard_map/ppermute | solution.py:26
  141.7 1.9 %collective-permute-start.16 = (bf16[15,512]{0,1:T(8,128)(2,1)S(1)}, bf16[15,512]{0,1:T(8,128)(2,1)S(1)}, u32[]{:S(2)}, u32[]{:S(2)}) collective-permute-start(bf16[15,512]{0,1:T(8,128)(2,1)S(1)} %slice.1881), channel_id=1, source_target_pairs={{0,8},{8,16},{16,24},{24,32},{32,40},{40,48},{48,56},{56,64},{64,7... | collective-permute-start | bytes 46088 | tf_op jit(solution)/shard_map/ppermute | solution.py:26
  143.6 8.0 %collective-permute-done.16 = bf16[15,512]{0,1:T(8,128)(2,1)S(1)} collective-permute-done((bf16[15,512]{0,1:T(8,128)(2,1)S(1)}, bf16[15,512]{0,1:T(8,128)(2,1)S(1)}, u32[]{:S(2)}, u32[]{:S(2)}) %collective-permute-start.16) | collective-permute-done | bytes 15392 | tf_op jit(solution)/shard_map/ppermute | solution.py:26
  152.3 1.9 %collective-permute-start.17 = (f32[15,512]{0,1:T(8,128)}, f32[15,512]{0,1:T(8,128)S(1)}, u32[]{:S(2)}, u32[]{:S(2)}) collective-permute-start(f32[15,512]{0,1:T(8,128)} %get-tuple-element.311), channel_id=1, source_target_pairs={{8,0},{16,8},{24,16},{32,24},{40,32},{48,40},{56,48},{64,56},{72,6... | collective-permute-start | bytes 92168 | tf_op jit(solution)/shard_map/ppermute | solution.py:26
  154.8 2.4 %collective-permute-start.18 = (bf16[1,512]{0,1:T(8,128)(2,1)S(1)}, bf16[1,512]{0,1:T(8,128)(2,1)S(1)}, u32[]{:S(2)}, u32[]{:S(2)}) collective-permute-start(bf16[1,512]{0,1:T(8,128)(2,1)S(1)} %slice.1880), channel_id=1, source_target_pairs={{0,8},{8,16},{16,24},{24,32},{32,40},{40,48},{48,56},{56,64},{64,7... | collective-permute-start | bytes 3080 | tf_op jit(solution)/shard_map/ppermute | solution.py:26
  157.2 3.9 %collective-permute-start.19 = (f32[128,1]{0,1:T(1,128)S(1)}, f32[128,1]{0,1:T(1,128)S(1)}, u32[]{:S(2)}, u32[]{:S(2)}) collective-permute-start(f32[128,1]{0,1:T(1,128)S(1)} %slice.1336), channel_id=1, source_target_pairs={{0,1},{1,2},{2,3},{3,4},{4,5},{5,6},{6,7},{8,9},{9,10},{10,11},{11... | collective-permute-start | bytes 1544 | tf_op jit(solution)/shard_map/ppermute | solution.py:26
  162.0 2.7 %collective-permute-done.18 = bf16[1,512]{0,1:T(8,128)(2,1)S(1)} collective-permute-done((bf16[1,512]{0,1:T(8,128)(2,1)S(1)}, bf16[1,512]{0,1:T(8,128)(2,1)S(1)}, u32[]{:S(2)}, u32[]{:S(2)}) %collective-permute-start.18) | collective-permute-done | bytes 1056 | tf_op jit(solution)/shard_map/ppermute | solution.py:26
  (253 shorter events, 52.3 us)
Async XLA Ops:
  0.6 17.4 %copy-start.7 = (f32[128,512]{1,0:T(8,128)S(1)}, f32[128,512]{1,0:T(8,128)}, u32[]{:S(2)}) copy-start(f32[128,512]{1,0:T(8,128)} %param.41) | copy-start | bytes 786436
  0.6 17.4 %copy-start.6 = (f32[2,128,512]{2,1,0:T(8,128)S(1)}, f32[2,128,512]{2,1,0:T(8,128)}, u32[]{:S(2)}) copy-start(f32[2,128,512]{2,1,0:T(8,128)} %param.43) | copy-start | bytes 1572868
  1.6 16.6 %collective-permute-start = (f32[15,512]{0,1:T(8,128)S(1)}, f32[15,512]{0,1:T(8,128)S(1)}, u32[]{:S(2)}, u32[]{:S(2)}) collective-permute-start(f32[15,512]{0,1:T(8,128)S(1)} %copy.248), channel_id=1, source_target_pairs={{0,8},{8,16},{16,24},{24,32},{32,40},{40,48},{48,56},{56,64},{64,7... | collective-permute-start | bytes 92168 | tf_op jit(solution)/shard_map/ppermute | solution.py:37
  3.7 14.5 %collective-permute-start.1 = (f32[15,512]{0,1:T(8,128)S(1)}, f32[15,512]{0,1:T(8,128)S(1)}, u32[]{:S(2)}, u32[]{:S(2)}) collective-permute-start(f32[15,512]{0,1:T(8,128)S(1)} %copy.249), channel_id=1, source_target_pairs={{8,0},{16,8},{24,16},{32,24},{40,32},{48,40},{56,48},{64,56},{72,6... | collective-permute-start | bytes 92168 | tf_op jit(solution)/shard_map/ppermute | solution.py:39
  18.2 7.1 %copy-start.4 = (f32[15,512]{0,1:T(8,128)}, f32[15,512]{0,1:T(8,128)S(1)}, u32[]{:S(2)}) copy-start(f32[15,512]{0,1:T(8,128)S(1)} %collective-permute-done.1) | copy-start | bytes 92164
  18.5 18.1 %collective-permute-start.3 = (f32[158,15]{0,1:T(8,128)S(1)}, f32[158,15]{0,1:T(8,128)S(1)}, u32[]{:S(2)}, u32[]{:S(2)}) collective-permute-start(f32[158,15]{0,1:T(8,128)S(1)} %slice.1229), channel_id=1, source_target_pairs={{1,0},{2,1},{3,2},{4,3},{5,4},{6,5},{7,6},{9,8},{10,9},{11,10},{12... | collective-permute-start | bytes 28448 | tf_op jit(solution)/shard_map/ppermute | solution.py:39
  20.9 15.8 %collective-permute-start.2 = (bf16[158,15]{0,1:T(8,128)(2,1)S(1)}, bf16[158,15]{0,1:T(8,128)(2,1)S(1)}, u32[]{:S(2)}, u32[]{:S(2)}) collective-permute-start(bf16[158,15]{0,1:T(8,128)(2,1)S(1)} %slice.1226), channel_id=1, source_target_pairs={{0,1},{1,2},{2,3},{3,4},{4,5},{5,6},{6,7},{8,9},{9,10},{10,11},{11... | collective-permute-start | bytes 14228 | tf_op jit(solution)/shard_map/ppermute | solution.py:37
  25.3 8.8 %copy-start.8 = (f32[128,512]{1,0:T(8,128)S(1)}, f32[128,512]{1,0:T(8,128)}, u32[]{:S(2)}) copy-start(f32[128,512]{1,0:T(8,128)} %param.38) | copy-start | bytes 786436
  25.3 8.9 %copy-start.9 = (f32[128,512]{1,0:T(8,128)S(1)}, f32[128,512]{1,0:T(8,128)}, u32[]{:S(2)}) copy-start(f32[128,512]{1,0:T(8,128)} %param.42) | copy-start | bytes 786436
  36.8 4.5 %copy-start = (bf16[4,31,158,128]{3,0,2,1:T(4,128)(2,1)S(1)}, bf16[4,31,158,128]{3,0,2,1:T(4,128)(2,1)}, u32[]{:S(2)}) copy-start(bf16[4,31,158,128]{3,0,2,1:T(4,128)(2,1)} %copy.382) | copy-start | bytes 15046660
  43.3 1.9 %copy-start.1 = (f32[4,128,128,1]{1,2,3,0:T(8,128)}, f32[4,128,128,1]{1,2,3,0:T(8,128)S(1)}, u32[]{:S(2)}) copy-start(f32[4,128,128,1]{1,2,3,0:T(8,128)S(1)} %fusion.6) | copy-start | bytes 786436
  53.6 5.6 %collective-permute-start.4 = (f32[158,15]{0,1:T(8,128)S(1)}, f32[158,15]{0,1:T(8,128)S(1)}, u32[]{:S(2)}, u32[]{:S(2)}) collective-permute-start(f32[158,15]{0,1:T(8,128)S(1)} %slice.1269), channel_id=1, source_target_pairs={{0,1},{1,2},{2,3},{3,4},{4,5},{5,6},{6,7},{8,9},{9,10},{10,11},{11... | collective-permute-start | bytes 28448 | tf_op jit(solution)/shard_map/ppermute | solution.py:26
  59.8 6.5 %collective-permute-start.5 = (f32[158,15]{0,1:T(8,128)S(1)}, f32[158,15]{0,1:T(8,128)S(1)}, u32[]{:S(2)}, u32[]{:S(2)}) collective-permute-start(f32[158,15]{0,1:T(8,128)S(1)} %get-tuple-element.309), channel_id=1, source_target_pairs={{1,0},{2,1},{3,2},{4,3},{5,4},{6,5},{7,6},{9,8},{10,9},{11,10},{12... | collective-permute-start | bytes 28448 | tf_op jit(solution)/shard_map/ppermute | solution.py:26
  66.6 9.9 %collective-permute-start.6 = (bf16[15,512]{0,1:T(8,128)(2,1)S(1)}, bf16[15,512]{0,1:T(8,128)(2,1)S(1)}, u32[]{:S(2)}, u32[]{:S(2)}) collective-permute-start(bf16[15,512]{0,1:T(8,128)(2,1)S(1)} %slice.1883), channel_id=1, source_target_pairs={{0,8},{8,16},{16,24},{24,32},{32,40},{40,48},{48,56},{56,64},{64,7... | collective-permute-start | bytes 46088 | tf_op jit(solution)/shard_map/ppermute | solution.py:26
  70.0 12.5 %collective-permute-start.8 = (bf16[1,512]{0,1:T(8,128)(2,1)S(1)}, bf16[1,512]{0,1:T(8,128)(2,1)S(1)}, u32[]{:S(2)}, u32[]{:S(2)}) collective-permute-start(bf16[1,512]{0,1:T(8,128)(2,1)S(1)} %slice.1882), channel_id=1, source_target_pairs={{0,8},{8,16},{16,24},{24,32},{32,40},{40,48},{48,56},{56,64},{64,7... | collective-permute-start | bytes 3080 | tf_op jit(solution)/shard_map/ppermute | solution.py:26
  77.3 6.9 %collective-permute-start.7 = (f32[15,512]{0,1:T(8,128)}, f32[15,512]{0,1:T(8,128)S(1)}, u32[]{:S(2)}, u32[]{:S(2)}) collective-permute-start(f32[15,512]{0,1:T(8,128)} %get-tuple-element.315), channel_id=1, source_target_pairs={{8,0},{16,8},{24,16},{32,24},{40,32},{48,40},{56,48},{64,56},{72,6... | collective-permute-start | bytes 92168 | tf_op jit(solution)/shard_map/ppermute | solution.py:26
  80.1 5.6 %collective-permute-start.9 = (f32[128,1]{0,1:T(1,128)S(1)}, f32[128,1]{0,1:T(1,128)S(1)}, u32[]{:S(2)}, u32[]{:S(2)}) collective-permute-start(f32[128,1]{0,1:T(1,128)S(1)} %slice.1279), channel_id=1, source_target_pairs={{0,1},{1,2},{2,3},{3,4},{4,5},{5,6},{6,7},{8,9},{9,10},{10,11},{11... | collective-permute-start | bytes 1544 | tf_op jit(solution)/shard_map/ppermute | solution.py:26
  85.8 27.2 %slice-start = ((s8[5015552]{0:T(1024)(128)(4,1)}), s8[4194304]{0:T(1024)(128)(4,1)S(1)}, s32[]{:S(2)}) async-start(s8[5015552]{0:T(1024)(128)(4,1)} %bitcast.853), calls=%async_computation | async-start | bytes 8388608
  86.1 11.7 %collective-permute-start.10 = (f32[15,512]{0,1:T(8,128)S(1)}, f32[15,512]{0,1:T(8,128)S(1)}, u32[]{:S(2)}, u32[]{:S(2)}) collective-permute-start(f32[15,512]{0,1:T(8,128)S(1)} %get-tuple-element.321), channel_id=1, source_target_pairs={{0,8},{8,16},{16,24},{24,32},{32,40},{40,48},{48,56},{56,64},{64,7... | collective-permute-start | bytes 92168 | tf_op jit(solution)/shard_map/ppermute | solution.py:37
  88.3 11.2 %collective-permute-start.11 = (f32[15,512]{0,1:T(8,128)S(1)}, f32[15,512]{0,1:T(8,128)S(1)}, u32[]{:S(2)}, u32[]{:S(2)}) collective-permute-start(f32[15,512]{0,1:T(8,128)S(1)} %get-tuple-element.322), channel_id=1, source_target_pairs={{8,0},{16,8},{24,16},{32,24},{40,32},{48,40},{56,48},{64,56},{72,6... | collective-permute-start | bytes 92168 | tf_op jit(solution)/shard_map/ppermute | solution.py:39
  99.8 7.0 %collective-permute-start.13 = (f32[158,15]{0,1:T(8,128)S(1)}, f32[158,15]{0,1:T(8,128)S(1)}, u32[]{:S(2)}, u32[]{:S(2)}) collective-permute-start(f32[158,15]{0,1:T(8,128)S(1)} %slice.1286), channel_id=1, source_target_pairs={{1,0},{2,1},{3,2},{4,3},{5,4},{6,5},{7,6},{9,8},{10,9},{11,10},{12... | collective-permute-start | bytes 28448 | tf_op jit(solution)/shard_map/ppermute | solution.py:39
  102.8 5.5 %collective-permute-start.12 = (bf16[158,15]{0,1:T(8,128)(2,1)S(1)}, bf16[158,15]{0,1:T(8,128)(2,1)S(1)}, u32[]{:S(2)}, u32[]{:S(2)}) collective-permute-start(bf16[158,15]{0,1:T(8,128)(2,1)S(1)} %slice.1283), channel_id=1, source_target_pairs={{0,1},{1,2},{2,3},{3,4},{4,5},{5,6},{6,7},{8,9},{9,10},{10,11},{11... | collective-permute-start | bytes 14228 | tf_op jit(solution)/shard_map/ppermute | solution.py:37
  109.1 3.8 %slice-start.1 = ((s8[5015552]{0:T(1024)(128)(4,1)}), s8[821248]{0:T(1024)(128)(4,1)S(1)}, s32[]{:S(2)}) async-start(s8[5015552]{0:T(1024)(128)(4,1)} %bitcast.853), calls=%async_computation.1 | async-start | bytes 1642496
  113.0 1.9 %copy-start.2 = (f32[4,128,128,1]{1,2,3,0:T(8,128)S(1)}, f32[4,128,128,1]{1,2,3,0:T(8,128)}, u32[]{:S(2)}) copy-start(f32[4,128,128,1]{1,2,3,0:T(8,128)} %copy-done.1) | copy-start | bytes 786436
  121.5 1.5 copy-start.5
  121.5 39.6 %copy-start.3 = (f32[128,512]{0,1:T(8,128)S(1)}, f32[128,512]{0,1:T(8,128)}, u32[]{:S(2)}) copy-start(f32[128,512]{0,1:T(8,128)} %get-tuple-element.295) | copy-start | bytes 786436
  127.9 6.0 %collective-permute-start.14 = (f32[158,15]{0,1:T(8,128)S(1)}, f32[158,15]{0,1:T(8,128)S(1)}, u32[]{:S(2)}, u32[]{:S(2)}) collective-permute-start(f32[158,15]{0,1:T(8,128)S(1)} %slice.1326), channel_id=1, source_target_pairs={{0,1},{1,2},{2,3},{3,4},{4,5},{5,6},{6,7},{8,9},{9,10},{10,11},{11... | collective-permute-start | bytes 28448 | tf_op jit(solution)/shard_map/ppermute | solution.py:26
  134.6 6.8 %collective-permute-start.15 = (f32[158,15]{0,1:T(8,128)S(1)}, f32[158,15]{0,1:T(8,128)S(1)}, u32[]{:S(2)}, u32[]{:S(2)}) collective-permute-start(f32[158,15]{0,1:T(8,128)S(1)} %get-tuple-element.307), channel_id=1, source_target_pairs={{1,0},{2,1},{3,2},{4,3},{5,4},{6,5},{7,6},{9,8},{10,9},{11,10},{12... | collective-permute-start | bytes 28448 | tf_op jit(solution)/shard_map/ppermute | solution.py:26
  141.7 9.9 %collective-permute-start.16 = (bf16[15,512]{0,1:T(8,128)(2,1)S(1)}, bf16[15,512]{0,1:T(8,128)(2,1)S(1)}, u32[]{:S(2)}, u32[]{:S(2)}) collective-permute-start(bf16[15,512]{0,1:T(8,128)(2,1)S(1)} %slice.1881), channel_id=1, source_target_pairs={{0,8},{8,16},{16,24},{24,32},{32,40},{40,48},{48,56},{56,64},{64,7... | collective-permute-start | bytes 46088 | tf_op jit(solution)/shard_map/ppermute | solution.py:26
  152.3 13.6 %collective-permute-start.17 = (f32[15,512]{0,1:T(8,128)}, f32[15,512]{0,1:T(8,128)S(1)}, u32[]{:S(2)}, u32[]{:S(2)}) collective-permute-start(f32[15,512]{0,1:T(8,128)} %get-tuple-element.311), channel_id=1, source_target_pairs={{8,0},{16,8},{24,16},{32,24},{40,32},{48,40},{56,48},{64,56},{72,6... | collective-permute-start | bytes 92168 | tf_op jit(solution)/shard_map/ppermute | solution.py:26
  154.8 9.9 %collective-permute-start.18 = (bf16[1,512]{0,1:T(8,128)(2,1)S(1)}, bf16[1,512]{0,1:T(8,128)(2,1)S(1)}, u32[]{:S(2)}, u32[]{:S(2)}) collective-permute-start(bf16[1,512]{0,1:T(8,128)(2,1)S(1)} %slice.1880), channel_id=1, source_target_pairs={{0,8},{8,16},{16,24},{24,32},{32,40},{40,48},{48,56},{56,64},{64,7... | collective-permute-start | bytes 3080 | tf_op jit(solution)/shard_map/ppermute | solution.py:26
  157.2 10.3 %collective-permute-start.19 = (f32[128,1]{0,1:T(1,128)S(1)}, f32[128,1]{0,1:T(1,128)S(1)}, u32[]{:S(2)}, u32[]{:S(2)}) collective-permute-start(f32[128,1]{0,1:T(1,128)S(1)} %slice.1336), channel_id=1, source_target_pairs={{0,1},{1,2},{2,3},{3,4},{4,5},{5,6},{6,7},{8,9},{9,10},{10,11},{11... | collective-permute-start | bytes 1544 | tf_op jit(solution)/shard_map/ppermute | solution.py:26
where the time goes:
time: 170 us; the launch traced here: 169 us
  starting transfers between devices  62.2 us (37%)
  local copies, waits for them, and re-layouts  36 us (21%)
  waiting for transfers between devices  34.4 us (20%)
  other arithmetic  17.3 us (10%)
  matrix products  16.5 us (10%)
  between operations  2.16 us (1%)
    ppermute x12, starting transfers between devices, from_behind(): return lax.ppermute(block, axis, route)  29.9 us
    ppermute x12, waiting for transfers between devices, from_behind(): return lax.ppermute(block, axis, route)  28.9 us
    unnamed x152, local copies, waits for them, and re-layouts  22.4 us
    ppermute x4, starting transfers between devices, extended_2(): lax.ppermute(head, axis, [((i + 1) % count, i) for i in range(ends)])  19.9 us
    ppermute x4, starting transfers between devices, extended_2(): lax.ppermute(tail, axis, [(i, (i + 1) % count) for i in range(ends)])  12.5 us
    dot_general x2, matrix products, one_group(): jnp.einsum('praj,pakj->prk', shifted, toeplitz, preferred_element_type=jn...  7.94 us
    another operation x13, other arithmetic  7.76 us
    scatter-add x8, local copies, waits for them, and re-layouts, one_group(): merged = merged.at[:, member * patch_cols:member * patch_cols + patch_col...  4.82 us
  transfers between devices with their start and end apart: 20, of which 11 were waited for; matrix products, arithmetic and copies ran while one was open for 17% of the time, Pallas kernels for 0%

commit v1 on v0

v1 whole, which is shorter than its diff:
```python
import jax
import jax.numpy as jnp
from jax import lax
from jax.experimental import pallas as pl
from jax.experimental.pallas import tpu as pltpu
from jax.sharding import PartitionSpec as P

SIGMA = 0.15
TAU = 0.6
TV = 0.5
F32 = jnp.float32
BF16 = jnp.bfloat16

ROWS = 128
COLS = 512
XO = 48
YO = 32
WIDE = 640
SEGS = ((0, 16, 32), (16, 128, 144), (144, 16, 32))
PATCHES = ((0,), (1, 2, 3, 4), (5, 6, 7, 8), (9, 10, 11, 12), (13, 14, 15, 16), (17,))


def iota(shape, dim):
    return lax.broadcasted_iota(jnp.int32, shape, dim)


def split(value):
    hi = value.astype(BF16).astype(F32)
    return hi, value - hi


def lanes(value, shift):
    shift = shift % value.shape[1]
    return pltpu.roll(value, shift, 1) if shift else value


def rows(value, shift):
    shift = shift % value.shape[0]
    return pltpu.roll(value, shift, 0) if shift else value


def between(shape, lo, hi):
    lane = iota(shape, 1)
    return (lane >= lo) & (lane < hi)


def flags():
    row = lax.axis_index("row")
    col = lax.axis_index("col")
    return (
        row > 0,
        row < lax.axis_size("row") - 1,
        col > 0,
        col < lax.axis_size("col") - 1,
    )


def pack_rows_kernel(x_ref, y_ref, o_ref, q_ref, idx_ref, down_ref, up_ref):
    for out, near, far, edge in ((down_ref, 112, 96, 127), (up_ref, 0, 0, 0)):
        out[0:32] = x_ref[far : far + 32].astype(BF16)
        seen = o_ref[near : near + 16]
        hi, lo = split(y_ref[near : near + 16] - SIGMA * seen)
        out[32:48] = hi.astype(BF16)
        out[48:64] = lo.astype(BF16)
        out[64:80] = seen.astype(BF16)
        a_hi, a_lo = split(q_ref[0, edge : edge + 1])
        b_hi, b_lo = split(q_ref[1, edge : edge + 1])
        x_lo = split(x_ref[edge : edge + 1])[1]
        row = iota((16, COLS), 0)
        misc = jnp.zeros((16, COLS), F32)
        for place, part in enumerate((x_lo, a_hi, a_lo, b_hi, b_lo, idx_ref[0:1])):
            misc = jnp.where(row == place, part, misc)
        out[80:96] = misc.astype(BF16)


def pack_cols_kernel(x_ref, y_ref, o_ref, q_ref, idx_ref, top_ref, bot_ref, right_ref, left_ref):
    for out, base, spots in (
        (right_ref, 384, (48, 64, 80, 96, (97, 98, 99, 100, 101))),
        (left_ref, 0, (48, 0, 16, 32, (96, 97, 98, 99, 100))),
    ):
        own = slice(base, base + 128)
        top = top_ref[:, own].astype(F32)
        bot = bot_ref[:, own].astype(F32)
        seen = o_ref[:, own]
        x = x_ref[:, own]
        c_hi, c_lo = split(y_ref[:, own] - SIGMA * seen)
        x_hi, x_lo = split(x)

        def rolled(middle, section, shift, size):
            first = lanes(top[section : section + size], shift)
            last = lanes(bot[section : section + size], shift)
            return jnp.concatenate([first, lanes(middle, shift), last], axis=0)

        shape = (192, 128)
        fill = jnp.zeros((32, 128), F32)
        buf = rolled(x_hi, 0, spots[0], 32)
        right = base > 0
        x_at = 16 if right else 48
        buf = jnp.where(between(shape, x_at, x_at + 32), buf, 0.0)
        at = 48 if right else 0
        for which, (middle, section) in enumerate(((c_hi, 32), (c_lo, 48), (seen, 64))):
            part = jnp.concatenate([rolled(middle, section, spots[1 + which], 16), fill], axis=0)
            start = at + 16 * which
            buf = jnp.where(between(shape, start, start + 16), part, buf)
        a_hi, a_lo = split(q_ref[0, :, own])
        b_hi, b_lo = split(q_ref[1, :, own])
        rix = iota((32, 128), 0)
        for which, middle in enumerate((x_lo, a_hi, a_lo, b_hi, b_lo)):
            shift = spots[4][which]
            first = jnp.where(rix == 31, top[80 + which : 81 + which], 0.0)
            last = jnp.where(rix == 0, bot[80 + which : 81 + which], 0.0)
            part = jnp.concatenate(
                [lanes(first, shift), lanes(middle, shift), lanes(last, shift)], axis=0
            )
            buf = jnp.where(between(shape, 96 + which, 97 + which), part, buf)
        spot = 4 if right else 1
        row = iota((192, 1), 0)
        mine = idx_ref[0:1, spot : spot + 1]
        above = top_ref[85:86, spot : spot + 1].astype(F32)
        below = bot_ref[85:86, spot : spot + 1].astype(F32)
        entry = jnp.where(row == 0, above, jnp.where(row == 1, mine, below))
        buf = jnp.where(between(shape, 101, 102), entry, buf)
        out[...] = buf.astype(BF16)


def pack_cols2_kernel(xb_ref, top_ref, bot_ref, right_ref, left_ref):
    for out, tile, at in ((right_ref, 4, 16), (left_ref, 0, 48)):
        own = slice(128 * tile, 128 * tile + 128)
        hi, lo = split(xb_ref[:, own])
        top = top_ref[:, own].astype(F32)
        bot = bot_ref[:, own].astype(F32)
        shape = (192, 128)
        buf = jnp.concatenate([top[0:32], hi, bot[0:32]], axis=0)
        rix = iota((32, 128), 0)
        low = jnp.concatenate(
            [
                jnp.where(rix == 31, top[32:33], 0.0),
                lo,
                jnp.where(rix == 0, bot[32:33], 0.0),
            ],
            axis=0,
        )
        source = 47 if tile == 4 else 48
        buf = jnp.where(between(shape, at, at + 32), buf, 0.0)
        buf = jnp.where(between(shape, 96, 97), lanes(low, 96 - source), buf)
        out[...] = buf.astype(BF16)


def build_taps(tab_ref, t_ref):
    k = iota((32, 128), 0)
    j = iota((32, 128), 1) % 32
    lower = j <= k
    for patch in range(18):
        at = 8 * (patch // 6) + patch % 6
        for a1 in range(4):
            for half in range(2):
                e = 2 * a1 + half
                line = tab_ref[at : at + 1, 128 * e : 128 * e + 128]
                spread = jnp.broadcast_to(line, (32, 128))
                low = pltpu.roll(spread, 97, 1, stride=1, stride_axis=0)
                high = pltpu.roll(low, 32, 1)
                block = jnp.concatenate(
                    [jnp.where(lower, low, 0.0), jnp.where(lower, 0.0, high)], axis=0
                )
                t_ref[patch, 64 * a1 : 64 * a1 + 64, 128 * half : 128 * half + 128] = block.astype(
                    BF16
                )


def windows(xe_ref, p_ref):
    low = between((192, 128), 0, 64)
    tail = between((192, 128), 96, 128)
    for tile in range(5):
        here = slice(128 * tile, 128 * tile + 128)
        x0 = xe_ref[0:192, here]
        x8 = xe_ref[8:200, here]
        p_ref[4 * tile] = jnp.where(low, x0, lanes(x8, 64)).astype(BF16)
        p_ref[4 * tile + 1] = jnp.where(low, lanes(x0, 96), lanes(x8, 32)).astype(BF16)
        if tile < 4:
            after = slice(128 * tile + 128, 128 * tile + 256)
            p_ref[4 * tile + 2] = jnp.where(low, lanes(x0, 64), x8).astype(BF16)
            w0 = jnp.where(tail, x0, xe_ref[0:192, after])
            w8 = jnp.where(tail, x8, xe_ref[8:200, after])
            p_ref[4 * tile + 3] = jnp.where(low, lanes(w0, 32), lanes(w8, 96)).astype(BF16)


def blur(p_ref, t_ref, a_ref, c_ref, y_ref, row_ok, col_ok):
    for seg, (first, size, padded) in enumerate(SEGS):
        for patch, blocks in enumerate(PATCHES):
            lhs = jnp.concatenate(
                [
                    jnp.concatenate(
                        [
                            p_ref[b, first : first + padded],
                            p_ref[b, first + 16 : first + 16 + padded],
                        ],
                        axis=1,
                    )
                    for b in blocks
                ],
                axis=0,
            )
            v = jnp.dot(lhs, t_ref[6 * seg + patch], preferred_element_type=F32)
            for place, b in enumerate(blocks):
                part = v[place * padded : place * padded + padded]
                a_ref[b, 0:padded] = part[:, :128] + rows(part[:, 128:], -4)
        low = between((padded, 128), 0, 64)
        even = iota((padded, 128), 1) % 64 < 32
        for tile in range(5):
            a = [a_ref[4 * tile + p, 0:padded] for p in range(2 if tile == 4 else 4)]
            if tile == 4:
                a += [jnp.zeros_like(a[0])] * 2
            e = []
            for p in range(2):
                z = lanes(jnp.where(low, a[p + 2], a[p]), 64)
                e.append(jnp.where(low, a[p], z) + rows(jnp.where(low, z, a[p + 2]), -2))
            m1 = jnp.where(even, e[0], lanes(e[1], 32))
            m2 = jnp.where(even, lanes(e[0], 96), e[1])
            blurred = (m1 + rows(m2, -1))[0:size]
            here = slice(128 * tile, 128 * tile + 128)
            new = (c_ref[first : first + size, here] + SIGMA * blurred) / (1.0 + SIGMA)
            keep = col_ok(tile, size) & row_ok(seg)
            y_ref[first : first + size, here] = jnp.where(keep, new, 0.0)


def adjoint(y_ref, t_ref, l_ref, f_ref, z_ref):
    z_ref[...] = jnp.zeros_like(z_ref)
    for seg, (first, size, padded) in enumerate(SEGS):
        low = between((padded, 128), 0, 64)
        even = iota((padded, 128), 1) % 64 < 32
        for tile in range(5):
            here = slice(128 * tile, 128 * tile + 128)
            o = jnp.concatenate(
                [y_ref[first : first + size, here], jnp.zeros((padded - size, 128), F32)], axis=0
            )
            o1 = rows(o, 1)
            e = [jnp.where(even, o, lanes(o1, 32)), jnp.where(even, lanes(o, 96), o1)]
            for p in range(2):
                s = rows(e[p], 2)
                parts = [(p, jnp.where(low, e[p], lanes(s, 64)))]
                if tile < 4:
                    parts.append((p + 2, jnp.where(low, lanes(e[p], 64), s)))
                for place, part in parts:
                    b = 4 * tile + place
                    l_ref[b, 0:padded, 0:128] = part.astype(BF16)
                    l_ref[b, 0:padded, 128:256] = rows(part, 4).astype(BF16)
        for patch, blocks in enumerate(PATCHES):
            lhs = jnp.concatenate([l_ref[b, 0:padded] for b in blocks], axis=0)
            g = lax.dot_general(
                lhs, t_ref[6 * seg + patch], (((1,), (1,)), ((), ())), preferred_element_type=F32
            )
            zero = jnp.zeros((16, 128), F32)
            for place, b in enumerate(blocks):
                part = g[place * padded : place * padded + padded]
                f_ref[b, 0 : padded + 16] = jnp.concatenate(
                    [part[:, :128], zero], axis=0
                ) + jnp.concatenate([zero, part[:, 128:]], axis=0)
        tall = padded + 24
        low = between((tall, 128), 0, 64)
        head = between((tall, 128), 0, 32)
        pad8 = jnp.zeros((8, 128), F32)
        for tile in range(5):
            both = []
            for p in range(2):
                fa = f_ref[4 * tile + p, 0 : padded + 16]
                a0 = jnp.concatenate([fa, pad8], axis=0)
                a8 = jnp.concatenate([pad8, fa], axis=0)
                if tile < 4:
                    fb = f_ref[4 * tile + p + 2, 0 : padded + 16]
                    b0 = jnp.concatenate([fb, pad8], axis=0)
                    b8 = jnp.concatenate([pad8, fb], axis=0)
                    both.append(jnp.where(low, a0, b8) + lanes(jnp.where(low, b0, a8), 64))
                else:
                    both.append(jnp.where(low, a0 + lanes(a8, 64), 0.0))
            turned = lanes(both[1], 32)
            here = slice(128 * tile, 128 * tile + 128)
            span = slice(first, first + tall)
            z_ref[span, here] += both[0] + jnp.where(head, 0.0, turned)
            if tile < 4:
                after = slice(128 * tile + 128, 128 * tile + 256)
                z_ref[span, after] += jnp.where(head, turned, 0.0)


def total_variation(xe_ref, q1_ref, q2_ref, q1o_ref, q2o_ref, place_row, place_col, limit_row, limit_col):
    for chunk in range(9):
        start = 16 * chunk
        x = xe_ref[24 + start : 40 + start, 0:WIDE]
        tall = xe_ref[24 + start : 48 + start, 0:WIDE]
        below = rows(tall, -1)[0:16]
        right = lanes(x, -1)
        r = place_row - 8 + start + iota((16, WIDE), 0)
        c = place_col - XO + iota((16, WIDE), 1)
        g1 = jnp.where(r < limit_row, below - x, 0.0)
        g2 = jnp.where(c < limit_col, right - x, 0.0)
        span = slice(start, start + 16)
        u1 = q1_ref[span] + SIGMA * g1
        u2 = q2_ref[span] + SIGMA * g2
        shrink = jnp.maximum(1.0, jnp.sqrt(u1 * u1 + u2 * u2) / TV)
        inv = 1.0 / shrink
        q1o_ref[span] = u1 * inv
        q2o_ref[span] = u2 * inv


def divergence(q1_ref, q2_ref, chunk, place_row, place_col, limit_row, limit_col):
    start = 8 + 16 * chunk
    m1 = q1_ref[start - 8 : start + 16]
    m2 = q2_ref[start : start + 16]
    r = place_row + 16 * chunk - 8 + iota((24, WIDE), 0)
    c = place_col - XO + iota((16, WIDE), 1)
    m1 = jnp.where((r >= 0) & (r < limit_row), m1, 0.0)
    m2 = jnp.where((c >= 0) & (c < limit_col), m2, 0.0)
    return (m1 - rows(m1, 1))[8:24] + (m2 - lanes(m2, 1))


def places():
    row = lax.axis_index("row")
    col = lax.axis_index("col")
    return (
        row * ROWS,
        col * COLS,
        lax.axis_size("row") * ROWS - 1,
        lax.axis_size("col") * COLS - 1,
    )


def masks():
    top, bot, left, right = flags()

    def row_ok(seg):
        if seg == 1:
            return jnp.bool_(True)
        return top if seg == 0 else bot

    def col_ok(tile, size):
        lane = iota((size, 128), 1)
        if tile == 0:
            return (lane >= YO) | left
        if tile == 4:
            return (lane < YO) | right
        return jnp.ones((size, 128), jnp.bool_)

    return row_ok, col_ok


def widen(value, shift):
    pad = jnp.zeros((value.shape[0], WIDE - COLS), F32)
    return lanes(jnp.concatenate([value, pad], axis=1), shift)


def select_tables(table_ref, idx_ref, top_ref, bot_ref, lf_ref, rt_ref, tab_ref):
    lane = iota((1, 128), 1)
    total = jnp.full((1, 128), -1.0, F32)
    lines = (top_ref[80:96, 0:128].astype(F32)[5:6], idx_ref[0:1, 0:128], bot_ref[80:96, 0:128].astype(F32)[5:6])
    lf = lf_ref[0:16].astype(F32)
    rt = rt_ref[0:16].astype(F32)
    for r in range(3):
        line = jnp.where(lane == 0, lf[r : r + 1, 101:102], lines[r])
        line = jnp.where(lane == 5, rt[r : r + 1, 101:102], line)
        line = lanes(line, 8 * r) if r else line
        total = jnp.where((lane >= 8 * r) & (lane < 8 * r + 6), line, total)
    onehot = jnp.where(total == iota((64, 128), 0).astype(F32), 1.0, 0.0).astype(BF16)
    picked = lax.dot_general(
        onehot, table_ref[...], (((0,), (0,)), ((), ())), preferred_element_type=F32
    )
    tab_ref[...] = picked[0:24]


def first_kernel(
    x_ref, y_ref, o_ref, q_ref, idx_ref, table_ref, top_ref, bot_ref, lf_ref, rt_ref,
    x1_ref, xb_ref, c2_ref, q1o_ref, q2o_ref, tab_ref, down_ref, up_ref,
    xe_ref, c_ref, ob_ref, ys_ref, q1_ref, q2_ref, t_ref, p_ref, a_ref, l_ref, f_ref, z_ref,
):
    top_ok, bot_ok, left_ok, right_ok = flags()
    row0, col0, limit_row, limit_col = places()
    select_tables(table_ref, idx_ref, top_ref, bot_ref, lf_ref, rt_ref, tab_ref)
    build_taps(tab_ref, t_ref)
    misc_t = top_ref[80:96].astype(F32)
    misc_b = bot_ref[80:96].astype(F32)
    rix = iota((32, COLS), 0)
    above = top_ref[0:32].astype(F32) + jnp.where(rix == 31, misc_t[0:1], 0.0)
    below = bot_ref[0:32].astype(F32) + jnp.where(rix == 0, misc_b[0:1], 0.0)
    own = widen(x_ref[...], XO)
    xe_ref[0:32, 0:WIDE] = widen(jnp.where(top_ok, above, 0.0), XO)
    xe_ref[32:160, 0:WIDE] = own
    xe_ref[160:192, 0:WIDE] = widen(jnp.where(bot_ok, below, 0.0), XO)
    xe_ref[192:208, :] = jnp.zeros((16, 768), F32)
    xe_ref[0:208, 640:768] = jnp.zeros((208, 128), F32)
    rr = iota((192, 128), 0)
    rows_ok = ((rr >= 32) | top_ok) & ((rr < 160) | bot_ok)
    lf = jnp.where(rows_ok & left_ok, lf_ref[...].astype(F32), 0.0)
    rt = jnp.where(rows_ok & right_ok, rt_ref[...].astype(F32), 0.0)
    shape = (192, 128)
    add = jnp.where(between(shape, 16, 48), lf, 0.0)
    xe_ref[0:192, 0:128] += add + jnp.where(between(shape, 47, 48), lanes(lf, 79), 0.0)
    add = jnp.where(between(shape, 48, 80), rt, 0.0)
    xe_ref[0:192, 512:640] += add + jnp.where(between(shape, 48, 49), lanes(rt, 80), 0.0)
    seen = o_ref[...]
    c_ref[16:144] = widen(y_ref[...] - SIGMA * seen, YO)
    ob_ref[16:144] = widen(seen, YO)
    for ref, span in ((top_ref, slice(0, 16)), (bot_ref, slice(144, 160))):
        c_ref[span] = widen(ref[32:48].astype(F32) + ref[48:64].astype(F32), YO)
        ob_ref[span] = widen(ref[64:80].astype(F32), YO)
    lf = lf_ref[0:160].astype(F32)
    rt = rt_ref[0:160].astype(F32)
    shape = (160, 128)
    at = between(shape, 16, 32)
    c_ref[:, 0:128] = jnp.where(at, lanes(lf, 96) + lanes(lf, 80), c_ref[:, 0:128])
    ob_ref[:, 0:128] = jnp.where(at, lanes(lf, 64), ob_ref[:, 0:128])
    at = between(shape, 32, 48)
    c_ref[:, 512:640] = jnp.where(at, lanes(rt, 32) + lanes(rt, 16), c_ref[:, 512:640])
    ob_ref[:, 512:640] = jnp.where(at, rt, ob_ref[:, 512:640])
    lf = lf_ref[24:168].astype(F32)
    edge = between((144, 128), 47, 48)
    r8 = iota((8, COLS), 0)
    for comp, ref in ((0, q1_ref), (1, q2_ref)):
        line = misc_t[1 + 2 * comp : 2 + 2 * comp] + misc_t[2 + 2 * comp : 3 + 2 * comp]
        ref[0:8] = widen(jnp.where(r8 == 7, line, 0.0), XO)
        ref[8:136] = widen(q_ref[comp], XO)
        ref[136:144] = jnp.zeros((8, WIDE), F32)
        side = lanes(lf, 78 - 2 * comp) + lanes(lf, 77 - 2 * comp)
        ref[:, 0:128] = jnp.where(edge, side, ref[:, 0:128])
    row_ok, col_ok = masks()
    windows(xe_ref, p_ref)
    blur(p_ref, t_ref, a_ref, c_ref, ys_ref, row_ok, col_ok)
    total_variation(xe_ref, q1_ref, q2_ref, q1o_ref, q2o_ref, row0, col0, limit_row, limit_col)
    adjoint(ys_ref, t_ref, l_ref, f_ref, z_ref)
    c2_ref[...] = ys_ref[...] - SIGMA * ob_ref[...]
    for chunk in range(8):
        span = slice(16 * chunk, 16 * chunk + 16)
        ext = slice(32 + 16 * chunk, 48 + 16 * chunk)
        div = divergence(q1o_ref, q2o_ref, chunk, row0, col0, limit_row, limit_col)
        x = xe_ref[ext, 0:WIDE]
        new = x - TAU * (z_ref[ext, 0:WIDE] - div)
        x1_ref[span] = new
        xb_ref[span] = 2.0 * new - x
    row = iota((16, WIDE), 0)
    down_ref[0:32] = xb_ref[96:128].astype(BF16)
    up_ref[0:32] = xb_ref[0:32].astype(BF16)
    down_ref[32:48] = jnp.where(row == 0, split(xb_ref[127:128])[1], 0.0).astype(BF16)
    up_ref[32:48] = jnp.where(row == 0, split(xb_ref[0:1])[1], 0.0).astype(BF16)


def second_kernel(
    x1_ref, xb_ref, c2_ref, q1i_ref, q2i_ref, tab_ref, top_ref, bot_ref, lf_ref, rt_ref,
    x2_ref, y2_ref,
    xe_ref, ys_ref, q1_ref, q2_ref, t_ref, p_ref, a_ref, l_ref, f_ref, z_ref,
):
    top_ok, bot_ok, left_ok, right_ok = flags()
    row0, col0, limit_row, limit_col = places()
    build_taps(tab_ref, t_ref)
    lane = iota((32, WIDE), 1)
    own_lane = (lane >= XO) & (lane < XO + COLS)
    rix = iota((32, WIDE), 0)
    above = top_ref[0:32].astype(F32) + jnp.where(rix == 31, top_ref[32:48].astype(F32)[0:1], 0.0)
    below = bot_ref[0:32].astype(F32) + jnp.where(rix == 0, bot_ref[32:48].astype(F32)[0:1], 0.0)
    xe_ref[0:32, 0:WIDE] = jnp.where(own_lane & top_ok, above, 0.0)
    for chunk in range(4):
        span = slice(32 * chunk, 32 * chunk + 32)
        xe_ref[32 + 32 * chunk : 64 + 32 * chunk, 0:WIDE] = jnp.where(own_lane, xb_ref[span], 0.0)
    xe_ref[160:192, 0:WIDE] = jnp.where(own_lane & bot_ok, below, 0.0)
    xe_ref[192:208, :] = jnp.zeros((16, 768), F32)
    xe_ref[0:208, 640:768] = jnp.zeros((208, 128), F32)
    rr = iota((192, 128), 0)
    rows_ok = ((rr >= 32) | top_ok) & ((rr < 160) | bot_ok)
    lf = jnp.where(rows_ok & left_ok, lf_ref[...].astype(F32), 0.0)
    rt = jnp.where(rows_ok & right_ok, rt_ref[...].astype(F32), 0.0)
    shape = (192, 128)
    add = jnp.where(between(shape, 16, 48), lf, 0.0)
    xe_ref[0:192, 0:128] += add + jnp.where(between(shape, 47, 48), lanes(lf, 79), 0.0)
    add = jnp.where(between(shape, 48, 80), rt, 0.0)
    xe_ref[0:192, 512:640] += add + jnp.where(between(shape, 48, 49), lanes(rt, 80), 0.0)
    row_ok, col_ok = masks()
    windows(xe_ref, p_ref)
    blur(p_ref, t_ref, a_ref, c2_ref, ys_ref, row_ok, col_ok)
    total_variation(xe_ref, q1i_ref, q2i_ref, q1_ref, q2_ref, row0, col0, limit_row, limit_col)
    adjoint(ys_ref, t_ref, l_ref, f_ref, z_ref)
    for chunk in range(8):
        span = slice(16 * chunk, 16 * chunk + 16)
        ext = slice(32 + 16 * chunk, 48 + 16 * chunk)
        div = divergence(q1_ref, q2_ref, chunk, row0, col0, limit_row, limit_col)
        new = x1_ref[span] - TAU * (z_ref[ext, 0:WIDE] - div)
        x2_ref[span] = lanes(new, -XO)[:, :COLS]
        y2_ref[span] = lanes(ys_ref[16 + 16 * chunk : 32 + 16 * chunk], -YO)[:, :COLS]


def work_scratch():
    return [
        pltpu.VMEM((18, 256, 256), BF16),
        pltpu.VMEM((18, 192, 128), BF16),
        pltpu.VMEM((18, 144, 128), F32),
        pltpu.VMEM((18, 144, 256), BF16),
        pltpu.VMEM((18, 160, 128), F32),
        pltpu.VMEM((208, WIDE), F32),
    ]


def field(*shape, dtype=F32):
    return jax.ShapeDtypeStruct(shape, dtype)


def call(kernel, outs, scratch, *args, name):
    return pl.pallas_call(
        kernel,
        out_shape=outs,
        scratch_shapes=scratch,
        compiler_params=pltpu.CompilerParams(vmem_limit_bytes=56 * 1024 * 1024),
        name=name,
    )(*args)


def ring(block, axis, distance):
    count = lax.axis_size(axis)
    return lax.ppermute(block, axis, [(i, (i + distance) % count) for i in range(count)])


def per_device(observed, psf_table, psf_index, start_image, blur_dual, tv_dual):
    table = psf_table.astype(F32)
    normed = (table / jnp.sum(table, axis=(1, 2), keepdims=True)).astype(BF16)
    normed = jnp.pad(normed[:, :, ::-1], ((0, 0), (1, 0), (0, 1))).reshape(64, 1024)
    idx = jnp.pad(psf_index.astype(F32), ((0, 0), (1, COLS - 5)))
    strip = field(96, COLS, dtype=BF16)
    side = field(192, 128, dtype=BF16)
    down, up = call(
        pack_rows_kernel, (strip, strip), [], start_image, blur_dual, observed, tv_dual, idx,
        name="pack_rows",
    )
    top = ring(down, "row", 1)
    bot = ring(up, "row", -1)
    to_right, to_left = call(
        pack_cols_kernel, (side, side), [],
        start_image, blur_dual, observed, tv_dual, idx, top, bot, name="pack_cols",
    )
    lf = ring(to_right, "col", 1)
    rt = ring(to_left, "col", -1)
    q_ext = field(144, WIDE)
    strip2 = field(48, WIDE, dtype=BF16)
    x1, xb, c2, q1, q2, tab, down, up = call(
        first_kernel,
        (
            field(ROWS, WIDE), field(ROWS, WIDE), field(160, WIDE), q_ext, q_ext,
            field(24, 1024), strip2, strip2,
        ),
        [
            pltpu.VMEM((208, 768), F32), pltpu.VMEM((160, WIDE), F32),
            pltpu.VMEM((160, WIDE), F32), pltpu.VMEM((160, WIDE), F32),
            pltpu.VMEM((144, WIDE), F32), pltpu.VMEM((144, WIDE), F32),
        ] + work_scratch(),
        start_image, blur_dual, observed, tv_dual, idx, normed, top, bot, lf, rt,
        name="first",
    )
    top = ring(down, "row", 1)
    bot = ring(up, "row", -1)
    to_right, to_left = call(pack_cols2_kernel, (side, side), [], xb, top, bot, name="pack_cols2")
    lf = ring(to_right, "col", 1)
    rt = ring(to_left, "col", -1)
    return call(
        second_kernel,
        (field(ROWS, COLS), field(ROWS, COLS)),
        [
            pltpu.VMEM((208, 768), F32), pltpu.VMEM((160, WIDE), F32),
            pltpu.VMEM((144, WIDE), F32), pltpu.VMEM((144, WIDE), F32),
        ] + work_scratch(),
        x1, xb, c2, q1, q2, tab, top, bot, lf, rt, name="second",
    )


def solution(mesh):
    placed = (
        P("row", "col"),
        P(),
        P("row", "col"),
        P("row", "col"),
        P("row", "col"),
        P(None, "row", "col"),
    )
    return jax.shard_map(
        per_device,
        mesh=mesh,
        in_specs=placed,
        out_specs=(P("row", "col"), P("row", "col")),
        check_vma=False,
    )
```

time: 170 us -> 66.2 us (0.39)
  the two profiles are of different devices: /device:TPU:96 before, /device:TPU:25 now
where the time goes in v1:
time: 66.2 us; the launch traced here: 66 us
  Pallas kernels  29.2 us (44%)
  waiting for transfers between devices  17.5 us (26%)
  starting transfers between devices  12.9 us (19%)
  local copies, waits for them, and re-layouts  4.82 us (7%)
  other arithmetic  0.86 us (1%)
  between operations  0.67 us (1%)
    pallas_call x5, Pallas kernels, call(): pl.pallas_call(kernel, out_shape=outs, scratch_shapes=scratch, compiler_p...  29.2 us
    ppermute x8, waiting for transfers between devices, ring(): lax.ppermute(block, axis, [(i, (i + distance) % count) for i in range(cou...  17.5 us
    ppermute x8, starting transfers between devices, ring(): lax.ppermute(block, axis, [(i, (i + distance) % count) for i in range(cou...  12.9 us
    unnamed x18, local copies, waits for them, and re-layouts  3.12 us
  transfers between devices with their start and end apart: 8, of which 6 were waited for; matrix products, arithmetic and copies ran while one was open for 2% of the time, Pallas kernels for 0%

profile of v1, /device:TPU:25, one launch (start us, length us, event | category | flops | bytes accessed | tf_op | source)
XLA Modules:
  0.0 66.0 jit_solution(16700281720558756673)
XLA Ops:
  0.6 0.7 convert_element_type.13
  1.3 0.7 pad.8.idx_ref
  1.9 2.0 %pack_rows.1 = (bf16[96,512]{1,0:T(8,128)(2,1)}, bf16[96,512]{1,0:T(8,128)(2,1)}) custom-call(f32[128,512]{1,0:T(8,128)} %x_ref.5, f32[128,512]{1,0:T(8,128)} %y_ref.5, f32[128,512]{1,0:T(8,128)} %o_ref.5, f32[2,128,512]{2,1,0:T(8,128)} %q_ref.5, f32[1,512]{1,0:T(1,128)} %pad.8.idx_ref), custom_call_target="tpu_custom_call" | custom-call | tf_op jit(solution)/shard_map/pack_rows/pallas_call | solution.py:502
  4.0 3.8 %collective-permute-start = (bf16[96,512]{1,0:T(8,128)(2,1)}, bf16[96,512]{1,0:T(8,128)(2,1)S(1)}, u32[]{:S(2)}, u32[]{:S(2)}) collective-permute-start(bf16[96,512]{1,0:T(8,128)(2,1)} %get-tuple-element.16), channel_id=1, source_target_pairs={{0,8},{8,16},{16,24},{24,32},{32,40},{40,48},{48,56},{56,64},{64,7... | collective-permute-start | bytes 294920 | tf_op jit(solution)/shard_map/ppermute | solution.py:513
  7.8 0.0 collective-permute-start.1
  7.8 0.1 convert_reduce_fusion
  7.9 1.8 %collective-permute-done.top_ref = bf16[96,512]{1,0:T(8,128)(2,1)S(1)} collective-permute-done((bf16[96,512]{1,0:T(8,128)(2,1)}, bf16[96,512]{1,0:T(8,128)(2,1)S(1)}, u32[]{:S(2)}, u32[]{:S(2)}) %collective-permute-start) | collective-permute-done | bytes 98336 | tf_op jit(solution)/shard_map/ppermute | solution.py:513
  9.7 5.9 %collective-permute-done.1.bot_ref = bf16[96,512]{1,0:T(8,128)(2,1)S(1)} collective-permute-done((bf16[96,512]{1,0:T(8,128)(2,1)}, bf16[96,512]{1,0:T(8,128)(2,1)S(1)}, u32[]{:S(2)}, u32[]{:S(2)}) %collective-permute-start.1) | collective-permute-done | bytes 98336 | tf_op jit(solution)/shard_map/ppermute | solution.py:513
  15.6 0.6 copy-done.2
  16.3 2.3 %pack_cols.1 = (bf16[192,128]{1,0:T(8,128)(2,1)}, bf16[192,128]{1,0:T(8,128)(2,1)}) custom-call(f32[128,512]{1,0:T(8,128)} %x_ref.5, f32[128,512]{1,0:T(8,128)} %y_ref.5, f32[128,512]{1,0:T(8,128)} %o_ref.5, f32[2,128,512]{2,1,0:T(8,128)} %q_ref.5, f32[1,512]{1,0:T(1,128)} %pad.8.idx_ref, bf16[96,512]{1,0:T(8,128)(2,1)} %copy-done.1, bf16[96,512]{1,0:T(8,128)(2,1)} %copy-done.2), custom_call_target="tpu_custom_call" | custom-call | tf_op jit(solution)/shard_map/pack_cols/pallas_call | solution.py:502
  18.6 0.7 %collective-permute-start.2 = (bf16[192,128]{1,0:T(8,128)(2,1)}, bf16[192,128]{1,0:T(8,128)(2,1)S(1)}, u32[]{:S(2)}, u32[]{:S(2)}) collective-permute-start(bf16[192,128]{1,0:T(8,128)(2,1)} %get-tuple-element.18), channel_id=1, source_target_pairs={{0,1},{1,2},{2,3},{3,4},{4,5},{5,6},{6,7},{7,0},{8,9},{9,10},{10,1... | collective-permute-start | bytes 147464 | tf_op jit(solution)/shard_map/ppermute | solution.py:513
  19.3 2.8 %collective-permute-start.3 = (bf16[192,128]{1,0:T(8,128)(2,1)}, bf16[192,128]{1,0:T(8,128)(2,1)S(1)}, u32[]{:S(2)}, u32[]{:S(2)}) collective-permute-start(bf16[192,128]{1,0:T(8,128)(2,1)} %get-tuple-element.19), channel_id=1, source_target_pairs={{0,7},{1,0},{2,1},{3,2},{4,3},{5,4},{6,5},{7,6},{8,15},{9,8},{10,9... | collective-permute-start | bytes 147464 | tf_op jit(solution)/shard_map/ppermute | solution.py:513
  22.1 0.1 fusion
  22.2 0.2 rev.3
  22.4 0.1 pad.9
  22.5 0.8 %copy.9.table_ref = bf16[64,1024]{1,0:T(8,128)(2,1)} copy(bf16[64,1024]{0,1:T(8,128)(2,1)S(1)} %bitcast.1) | data formatting | bytes 262144 | tf_op jit(solution)/shard_map/reshape | solution.py:519
  23.2 0.6 collective-permute-done.2.lf_ref
  23.8 0.6 copy-done.5
  24.4 0.6 copy-done.6
  25.0 10.4 %first.1 = (f32[128,640]{1,0:T(8,128)}, f32[128,640]{1,0:T(8,128)}, f32[160,640]{1,0:T(8,128)}, f32[144,640]{1,0:T(8,128)}, f32[144,640]{1,0:T(8,128)}, /*index=...) custom-call(f32[128,512]{1,0:T(8,128)} %x_ref.5, f32[128,512]{1,0:T(8,128)} %y_ref.5, ...), custom_call_target="tpu_custom_call" | custom-call | tf_op jit(solution)/shard_map/first/pallas_call | solution.py:502
  35.5 1.9 %collective-permute-start.4 = (bf16[48,640]{1,0:T(8,128)(2,1)}, bf16[48,640]{1,0:T(8,128)(2,1)S(1)}, u32[]{:S(2)}, u32[]{:S(2)}) collective-permute-start(bf16[48,640]{1,0:T(8,128)(2,1)} %get-tuple-element.26), channel_id=1, source_target_pairs={{0,8},{8,16},{16,24},{24,32},{32,40},{40,48},{48,56},{56,64},{64,7... | collective-permute-start | bytes 184328 | tf_op jit(solution)/shard_map/ppermute | solution.py:513
  37.4 0.0 collective-permute-start.5
  37.4 1.6 %collective-permute-done.4.top_ref = bf16[48,640]{1,0:T(8,128)(2,1)S(1)} collective-permute-done((bf16[48,640]{1,0:T(8,128)(2,1)}, bf16[48,640]{1,0:T(8,128)(2,1)S(1)}, u32[]{:S(2)}, u32[]{:S(2)}) %collective-permute-start.4) | collective-permute-done | bytes 61472 | tf_op jit(solution)/shard_map/ppermute | solution.py:513
  39.0 6.0 %collective-permute-done.5.bot_ref = bf16[48,640]{1,0:T(8,128)(2,1)S(1)} collective-permute-done((bf16[48,640]{1,0:T(8,128)(2,1)}, bf16[48,640]{1,0:T(8,128)(2,1)S(1)}, u32[]{:S(2)}, u32[]{:S(2)}) %collective-permute-start.5) | collective-permute-done | bytes 61472 | tf_op jit(solution)/shard_map/ppermute | solution.py:513
  45.0 0.6 copy-done.4
  45.6 1.7 %pack_cols2.1 = (bf16[192,128]{1,0:T(8,128)(2,1)}, bf16[192,128]{1,0:T(8,128)(2,1)}) custom-call(f32[128,640]{1,0:T(8,128)} %get-tuple-element.21.xb_ref, bf16[48,640]{1,0:T(8,128)(2,1)} %copy-done.3, bf16[48,640]{1,0:T(8,128)(2,1)} %copy-done.4), custom_call_target="tpu_custom_call" | custom-call | tf_op jit(solution)/shard_map/pack_cols2/pallas_call | solution.py:502
  47.3 0.1 collective-permute-start.6
  47.4 3.5 %collective-permute-start.7 = (bf16[192,128]{1,0:T(8,128)(2,1)}, bf16[192,128]{1,0:T(8,128)(2,1)S(1)}, u32[]{:S(2)}, u32[]{:S(2)}) collective-permute-start(bf16[192,128]{1,0:T(8,128)(2,1)} %get-tuple-element.29), channel_id=1, source_target_pairs={{0,7},{1,0},{2,1},{3,2},{4,3},{5,4},{6,5},{7,6},{8,15},{9,8},{10,9... | collective-permute-start | bytes 147464 | tf_op jit(solution)/shard_map/ppermute | solution.py:513
  50.9 1.7 %collective-permute-done.6.lf_ref = bf16[192,128]{1,0:T(8,128)(2,1)S(1)} collective-permute-done((bf16[192,128]{1,0:T(8,128)(2,1)}, bf16[192,128]{1,0:T(8,128)(2,1)S(1)}, u32[]{:S(2)}, u32[]{:S(2)}) %collective-permute-start.6) | collective-permute-done | bytes 49184 | tf_op jit(solution)/shard_map/ppermute | solution.py:513
  52.6 0.6 copy-done.7
  53.2 0.0 copy-done.8
  53.2 12.8 %second.1 = (f32[128,512]{1,0:T(8,128)}, f32[128,512]{1,0:T(8,128)}) custom-call(f32[128,640]{1,0:T(8,128)} %get-tuple-element.20.x1_ref, f32[128,640]{1,0:T(8,128)} %get-tuple-element.21.xb_ref, f32[160,640]{1,0:T(8,128)} %get-tuple-element.22.c2_ref, f32[144,640]{1,0:T(8,128)} %get-tuple-element.23.q1i_ref, f32[144,640]{1,0:T(8,128)} %get-tuple-element.24.q2i_ref, ...), custom_call_target="tpu_custom_call" | custom-call | tf_op jit(solution)/shard_map/second/pallas_call | solution.py:502
  (14 shorter events, 0.0 us)
Async XLA Ops:
  1.9 5.8 %copy-start = (bf16[64,31,31]{0,2,1:T(8,128)(2,1)S(1)}, bf16[64,31,31]{0,2,1:T(8,128)(2,1)}, u32[]{:S(2)}) copy-start(bf16[64,31,31]{0,2,1:T(8,128)(2,1)} %param.7) | copy-start | bytes 369028
  4.0 5.8 %collective-permute-start = (bf16[96,512]{1,0:T(8,128)(2,1)}, bf16[96,512]{1,0:T(8,128)(2,1)S(1)}, u32[]{:S(2)}, u32[]{:S(2)}) collective-permute-start(bf16[96,512]{1,0:T(8,128)(2,1)} %get-tuple-element.16), channel_id=1, source_target_pairs={{0,8},{8,16},{16,24},{24,32},{32,40},{40,48},{48,56},{56,64},{64,7... | collective-permute-start | bytes 294920 | tf_op jit(solution)/shard_map/ppermute | solution.py:513
  7.8 7.9 %collective-permute-start.1 = (bf16[96,512]{1,0:T(8,128)(2,1)}, bf16[96,512]{1,0:T(8,128)(2,1)S(1)}, u32[]{:S(2)}, u32[]{:S(2)}) collective-permute-start(bf16[96,512]{1,0:T(8,128)(2,1)} %get-tuple-element.17), channel_id=1, source_target_pairs={{0,120},{8,0},{16,8},{24,16},{32,24},{40,32},{48,40},{56,48},{64,5... | collective-permute-start | bytes 294920 | tf_op jit(solution)/shard_map/ppermute | solution.py:513
  9.7 5.9 %copy-start.1 = (bf16[96,512]{1,0:T(8,128)(2,1)}, bf16[96,512]{1,0:T(8,128)(2,1)S(1)}, u32[]{:S(2)}) copy-start(bf16[96,512]{1,0:T(8,128)(2,1)S(1)} %collective-permute-done.top_ref) | copy-start | bytes 294916
  15.6 0.6 copy-start.2
  18.6 5.3 %collective-permute-start.2 = (bf16[192,128]{1,0:T(8,128)(2,1)}, bf16[192,128]{1,0:T(8,128)(2,1)S(1)}, u32[]{:S(2)}, u32[]{:S(2)}) collective-permute-start(bf16[192,128]{1,0:T(8,128)(2,1)} %get-tuple-element.18), channel_id=1, source_target_pairs={{0,1},{1,2},{2,3},{3,4},{4,5},{5,6},{6,7},{7,0},{8,9},{9,10},{10,1... | collective-permute-start | bytes 147464 | tf_op jit(solution)/shard_map/ppermute | solution.py:513
  19.3 4.5 %collective-permute-start.3 = (bf16[192,128]{1,0:T(8,128)(2,1)}, bf16[192,128]{1,0:T(8,128)(2,1)S(1)}, u32[]{:S(2)}, u32[]{:S(2)}) collective-permute-start(bf16[192,128]{1,0:T(8,128)(2,1)} %get-tuple-element.19), channel_id=1, source_target_pairs={{0,7},{1,0},{2,1},{3,2},{4,3},{5,4},{6,5},{7,6},{8,15},{9,8},{10,9... | collective-permute-start | bytes 147464 | tf_op jit(solution)/shard_map/ppermute | solution.py:513
  23.8 0.6 copy-start.5
  24.4 0.6 copy-start.6
  35.5 3.5 %collective-permute-start.4 = (bf16[48,640]{1,0:T(8,128)(2,1)}, bf16[48,640]{1,0:T(8,128)(2,1)S(1)}, u32[]{:S(2)}, u32[]{:S(2)}) collective-permute-start(bf16[48,640]{1,0:T(8,128)(2,1)} %get-tuple-element.26), channel_id=1, source_target_pairs={{0,8},{8,16},{16,24},{24,32},{32,40},{40,48},{48,56},{56,64},{64,7... | collective-permute-start | bytes 184328 | tf_op jit(solution)/shard_map/ppermute | solution.py:513
  37.4 7.6 %collective-permute-start.5 = (bf16[48,640]{1,0:T(8,128)(2,1)}, bf16[48,640]{1,0:T(8,128)(2,1)S(1)}, u32[]{:S(2)}, u32[]{:S(2)}) collective-permute-start(bf16[48,640]{1,0:T(8,128)(2,1)} %get-tuple-element.27), channel_id=1, source_target_pairs={{0,120},{8,0},{16,8},{24,16},{32,24},{40,32},{48,40},{56,48},{64,5... | collective-permute-start | bytes 184328 | tf_op jit(solution)/shard_map/ppermute | solution.py:513
  39.0 6.0 %copy-start.3 = (bf16[48,640]{1,0:T(8,128)(2,1)}, bf16[48,640]{1,0:T(8,128)(2,1)S(1)}, u32[]{:S(2)}) copy-start(bf16[48,640]{1,0:T(8,128)(2,1)S(1)} %collective-permute-done.4.top_ref) | copy-start | bytes 184324
  45.0 0.6 copy-start.4
  47.3 5.3 %collective-permute-start.6 = (bf16[192,128]{1,0:T(8,128)(2,1)}, bf16[192,128]{1,0:T(8,128)(2,1)S(1)}, u32[]{:S(2)}, u32[]{:S(2)}) collective-permute-start(bf16[192,128]{1,0:T(8,128)(2,1)} %get-tuple-element.28), channel_id=1, source_target_pairs={{0,1},{1,2},{2,3},{3,4},{4,5},{5,6},{6,7},{7,0},{8,9},{9,10},{10,1... | collective-permute-start | bytes 147464 | tf_op jit(solution)/shard_map/ppermute | solution.py:513
  47.4 5.2 %collective-permute-start.7 = (bf16[192,128]{1,0:T(8,128)(2,1)}, bf16[192,128]{1,0:T(8,128)(2,1)S(1)}, u32[]{:S(2)}, u32[]{:S(2)}) collective-permute-start(bf16[192,128]{1,0:T(8,128)(2,1)} %get-tuple-element.29), channel_id=1, source_target_pairs={{0,7},{1,0},{2,1},{3,2},{4,3},{5,4},{6,5},{7,6},{8,15},{9,8},{10,9... | collective-permute-start | bytes 147464 | tf_op jit(solution)/shard_map/ppermute | solution.py:513
  52.6 0.6 copy-start.7
  52.6 0.6 copy-start.8

commit v2 on v1

--- a/solution.py
+++ b/solution.py
@@ -498,12 +498,12 @@
     return jax.ShapeDtypeStruct(shape, dtype)
 
 
-def call(kernel, outs, scratch, *args, name):
+def call(kernel, outs, scratch, *args, name, room=4):
     return pl.pallas_call(
         kernel,
         out_shape=outs,
         scratch_shapes=scratch,
-        compiler_params=pltpu.CompilerParams(vmem_limit_bytes=56 * 1024 * 1024),
+        compiler_params=pltpu.CompilerParams(vmem_limit_bytes=room * 1024 * 1024),
         name=name,
     )(*args)
 
@@ -546,7 +546,7 @@
             pltpu.VMEM((144, WIDE), F32), pltpu.VMEM((144, WIDE), F32),
         ] + work_scratch(),
         start_image, blur_dual, observed, tv_dual, idx, normed, top, bot, lf, rt,
-        name="first",
+        name="first", room=24,
     )
     top = ring(down, "row", 1)
     bot = ring(up, "row", -1)
@@ -560,7 +560,7 @@
             pltpu.VMEM((208, 768), F32), pltpu.VMEM((160, WIDE), F32),
             pltpu.VMEM((144, WIDE), F32), pltpu.VMEM((144, WIDE), F32),
         ] + work_scratch(),
-        x1, xb, c2, q1, q2, tab, top, bot, lf, rt, name="second",
+        x1, xb, c2, q1, q2, tab, top, bot, lf, rt, name="second", room=24,
     )
 
 

time: 66.2 us -> 55.9 us (0.84)
  Pallas kernels: 29.2 us -> 19.9 us
  waiting for transfers between devices: 17.5 us -> 16.3 us
  other arithmetic: 0.86 us -> 1.81 us
    pallas_call x5, Pallas kernels: 29.2 us -> 19.9 us  [call(): pl.pallas_call(kernel, out_shape=outs, scratch_shapes=scratch, compiler_p...]
    ppermute x8, waiting for transfers between devices: 17.5 us -> 16.3 us  [ring(): lax.ppermute(block, axis, [(i, (i + distance) % count) for i in range(cou...]
    reduce_sum x1, other arithmetic: 0.15 us -> 1.09 us  [per_device(): normed = (table / jnp.sum(table, axis=(1, 2), keepdims=True)).astype(BF16)]
    unnamed x18, local copies, waits for them, and re-layouts: 3.12 us -> 3.91 us
  transfers between devices with their start and end apart: 8 -> 8, of which waited for: 6 -> 6; matrix products, arithmetic and copies ran while one was open for 2% -> 3% of each run, Pallas kernels for 0% -> 0%
where the time goes in v2:
time: 55.9 us; the launch traced here: 55.6 us
  Pallas kernels  19.9 us (36%)
  waiting for transfers between devices  16.3 us (29%)
  starting transfers between devices  12.5 us (22%)
  local copies, waits for them, and re-layouts  4.37 us (8%)
  other arithmetic  1.81 us (3%)
  between operations  0.71 us (1%)
    pallas_call x5, Pallas kernels, call(): pl.pallas_call(kernel, out_shape=outs, scratch_shapes=scratch, compiler_p...  19.9 us
    ppermute x8, waiting for transfers between devices, ring(): lax.ppermute(block, axis, [(i, (i + distance) % count) for i in range(cou...  16.3 us
    ppermute x8, starting transfers between devices, ring(): lax.ppermute(block, axis, [(i, (i + distance) % count) for i in range(cou...  12.5 us
    unnamed x18, local copies, waits for them, and re-layouts  3.91 us
  transfers between devices with their start and end apart: 8, of which 6 were waited for; matrix products, arithmetic and copies ran while one was open for 3% of the time, Pallas kernels for 0%

profile of v2, /device:TPU:25, one launch (start us, length us, event | category | flops | bytes accessed | tf_op | source)
XLA Modules:
  0.0 55.6 jit_solution(14816090585176120817)
XLA Ops:
  0.6 0.7 %convert_element_type.13 = f32[1,4]{1,0:T(1,128)S(1)} convert(s32[1,4]{1,0:T(1,128)} %param.8) | non-fusion elementwise | flops 4 | bytes 32 | tf_op jit(solution)/shard_map/convert_element_type | solution.py:520
  1.3 0.1 pad.8.idx_ref
  1.4 1.0 %copy-done = f32[2,128,512]{2,1,0:T(8,128)S(1)} copy-done((f32[2,128,512]{2,1,0:T(8,128)S(1)}, f32[2,128,512]{2,1,0:T(8,128)}, u32[]{:S(2)}) %copy-start) | copy-done | bytes 524312
  2.4 0.9 %copy-done.2 = f32[128,512]{1,0:T(8,128)S(1)} copy-done((f32[128,512]{1,0:T(8,128)S(1)}, f32[128,512]{1,0:T(8,128)}, u32[]{:S(2)}) %copy-start.2) | copy-done | bytes 262168
  3.4 0.9 %copy-done.4 = f32[128,512]{1,0:T(8,128)S(1)} copy-done((f32[128,512]{1,0:T(8,128)S(1)}, f32[128,512]{1,0:T(8,128)}, u32[]{:S(2)}) %copy-start.4) | copy-done | bytes 262168
  4.3 0.9 %copy-done.6 = f32[128,512]{1,0:T(8,128)S(1)} copy-done((f32[128,512]{1,0:T(8,128)S(1)}, f32[128,512]{1,0:T(8,128)}, u32[]{:S(2)}) %copy-start.6) | copy-done | bytes 262168
  5.3 0.1 pack_rows.1
  5.3 3.9 %collective-permute-start = (bf16[96,512]{1,0:T(8,128)(2,1)S(1)}, bf16[96,512]{1,0:T(8,128)(2,1)S(1)}, u32[]{:S(2)}, u32[]{:S(2)}) collective-permute-start(bf16[96,512]{1,0:T(8,128)(2,1)S(1)} %get-tuple-element.16), channel_id=1, source_target_pairs={{0,8},{8,16},{16,24},{24,32},{32,40},{40,48},{48,56},{56,64},{64,7... | collective-permute-start | bytes 294920 | tf_op jit(solution)/shard_map/ppermute | solution.py:513
  9.2 0.0 collective-permute-start.1
  9.2 1.1 %convert_reduce_fusion = f32[64]{0:T(128)S(1)} fusion(bf16[64,31,31]{0,2,1:T(8,128)(2,1)} %param.7), kind=kLoop, calls=%fused_computation.1 | loop fusion | flops 122944 | bytes 123264 | tf_op jit(solution)/shard_map/reduce_sum | solution.py:518
  10.3 0.5 collective-permute-done.top_ref
  10.9 6.0 %collective-permute-done.1.bot_ref = bf16[96,512]{1,0:T(8,128)(2,1)S(1)} collective-permute-done((bf16[96,512]{1,0:T(8,128)(2,1)S(1)}, bf16[96,512]{1,0:T(8,128)(2,1)S(1)}, u32[]{:S(2)}, u32[]{:S(2)}) %collective-permute-start.1) | collective-permute-done | bytes 98336 | tf_op jit(solution)/shard_map/ppermute | solution.py:513
  16.9 0.3 pack_cols.1
  17.2 0.8 %collective-permute-start.2 = (bf16[192,128]{1,0:T(8,128)(2,1)S(1)}, bf16[192,128]{1,0:T(8,128)(2,1)S(1)}, u32[]{:S(2)}, u32[]{:S(2)}) collective-permute-start(bf16[192,128]{1,0:T(8,128)(2,1)S(1)} %get-tuple-element.18), channel_id=1, source_target_pairs={{0,1},{1,2},{2,3},{3,4},{4,5},{5,6},{6,7},{7,0},{8,9},{9,10},{10,1... | collective-permute-start | bytes 147464 | tf_op jit(solution)/shard_map/ppermute | solution.py:513
  18.0 2.8 %collective-permute-start.3 = (bf16[192,128]{1,0:T(8,128)(2,1)S(1)}, bf16[192,128]{1,0:T(8,128)(2,1)S(1)}, u32[]{:S(2)}, u32[]{:S(2)}) collective-permute-start(bf16[192,128]{1,0:T(8,128)(2,1)S(1)} %get-tuple-element.19), channel_id=1, source_target_pairs={{0,7},{1,0},{2,1},{3,2},{4,3},{5,4},{6,5},{7,6},{8,15},{9,8},{10,9... | collective-permute-start | bytes 147464 | tf_op jit(solution)/shard_map/ppermute | solution.py:513
  20.9 0.1 fusion
  20.9 0.2 rev.3
  21.1 0.1 pad.9
  21.2 0.1 copy.9.table_ref
  21.3 1.0 %collective-permute-done.2.lf_ref = bf16[192,128]{1,0:T(8,128)(2,1)S(1)} collective-permute-done((bf16[192,128]{1,0:T(8,128)(2,1)S(1)}, bf16[192,128]{1,0:T(8,128)(2,1)S(1)}, u32[]{:S(2)}, u32[]{:S(2)}) %collective-permute-start.2) | collective-permute-done | bytes 49184 | tf_op jit(solution)/shard_map/ppermute | solution.py:513
  22.4 0.0 collective-permute-done.3.rt_ref
  22.4 8.0 %first.1 = (f32[128,640]{1,0:T(8,128)S(1)}, f32[128,640]{1,0:T(8,128)S(1)}, f32[160,640]{1,0:T(8,128)S(1)}, f32[144,640]{1,0:T(8,128)S(1)}, f32[144,640]{1,0:T(8...) custom-call(f32[128,512]{1,0:T(8,128)S(1)} %copy-done.3, ...), custom_call_target="tpu_custom_call" | custom-call | tf_op jit(solution)/shard_map/first/pallas_call | solution.py:502
  30.4 1.3 %collective-permute-start.4 = (bf16[48,640]{1,0:T(8,128)(2,1)S(1)}, bf16[48,640]{1,0:T(8,128)(2,1)S(1)}, u32[]{:S(2)}, u32[]{:S(2)}) collective-permute-start(bf16[48,640]{1,0:T(8,128)(2,1)S(1)} %get-tuple-element.26), channel_id=1, source_target_pairs={{0,8},{8,16},{16,24},{24,32},{32,40},{40,48},{48,56},{56,64},{64,7... | collective-permute-start | bytes 184328 | tf_op jit(solution)/shard_map/ppermute | solution.py:513
  31.7 0.0 collective-permute-start.5
  31.7 1.3 %collective-permute-done.4.top_ref = bf16[48,640]{1,0:T(8,128)(2,1)S(1)} collective-permute-done((bf16[48,640]{1,0:T(8,128)(2,1)S(1)}, bf16[48,640]{1,0:T(8,128)(2,1)S(1)}, u32[]{:S(2)}, u32[]{:S(2)}) %collective-permute-start.4) | collective-permute-done | bytes 61472 | tf_op jit(solution)/shard_map/ppermute | solution.py:513
  33.0 6.0 %collective-permute-done.5.bot_ref = bf16[48,640]{1,0:T(8,128)(2,1)S(1)} collective-permute-done((bf16[48,640]{1,0:T(8,128)(2,1)S(1)}, bf16[48,640]{1,0:T(8,128)(2,1)S(1)}, u32[]{:S(2)}, u32[]{:S(2)}) %collective-permute-start.5) | collective-permute-done | bytes 61472 | tf_op jit(solution)/shard_map/ppermute | solution.py:513
  38.9 0.1 pack_cols2.1
  39.0 0.9 %collective-permute-start.6 = (bf16[192,128]{1,0:T(8,128)(2,1)S(1)}, bf16[192,128]{1,0:T(8,128)(2,1)S(1)}, u32[]{:S(2)}, u32[]{:S(2)}) collective-permute-start(bf16[192,128]{1,0:T(8,128)(2,1)S(1)} %get-tuple-element.28), channel_id=1, source_target_pairs={{0,1},{1,2},{2,3},{3,4},{4,5},{5,6},{6,7},{7,0},{8,9},{9,10},{10,1... | collective-permute-start | bytes 147464 | tf_op jit(solution)/shard_map/ppermute | solution.py:513
  39.9 2.8 %collective-permute-start.7 = (bf16[192,128]{1,0:T(8,128)(2,1)S(1)}, bf16[192,128]{1,0:T(8,128)(2,1)S(1)}, u32[]{:S(2)}, u32[]{:S(2)}) collective-permute-start(bf16[192,128]{1,0:T(8,128)(2,1)S(1)} %get-tuple-element.29), channel_id=1, source_target_pairs={{0,7},{1,0},{2,1},{3,2},{4,3},{5,4},{6,5},{7,6},{8,15},{9,8},{10,9... | collective-permute-start | bytes 147464 | tf_op jit(solution)/shard_map/ppermute | solution.py:513
  42.7 1.5 %collective-permute-done.6.lf_ref = bf16[192,128]{1,0:T(8,128)(2,1)S(1)} collective-permute-done((bf16[192,128]{1,0:T(8,128)(2,1)S(1)}, bf16[192,128]{1,0:T(8,128)(2,1)S(1)}, u32[]{:S(2)}, u32[]{:S(2)}) %collective-permute-start.6) | collective-permute-done | bytes 49184 | tf_op jit(solution)/shard_map/ppermute | solution.py:513
  44.2 0.0 collective-permute-done.7.rt_ref
  44.2 11.4 %second.1 = (f32[128,512]{1,0:T(8,128)}, f32[128,512]{1,0:T(8,128)}) custom-call(f32[128,640]{1,0:T(8,128)S(1)} %get-tuple-element.20.x1_ref, f32[128,640]{1,0:T(8,128)S(1)} %get-tuple-element.21.xb_ref, f32[160,640]{1,0:T(8,128)S(1)} %get-tuple-element.22.c2_ref, f32[144,640]{1,0:T(8,128)S(1)} %get-tuple-element.23.q1i_ref, ...), custom_call_target="tpu_custom_call" | custom-call | tf_op jit(solution)/shard_map/second/pallas_call | solution.py:502
  (14 shorter events, 0.0 us)
Async XLA Ops:
  1.4 1.0 %copy-start = (f32[2,128,512]{2,1,0:T(8,128)S(1)}, f32[2,128,512]{2,1,0:T(8,128)}, u32[]{:S(2)}) copy-start(f32[2,128,512]{2,1,0:T(8,128)} %q_ref.5) | copy-start | bytes 1572868
  2.4 0.9 %copy-start.2 = (f32[128,512]{1,0:T(8,128)S(1)}, f32[128,512]{1,0:T(8,128)}, u32[]{:S(2)}) copy-start(f32[128,512]{1,0:T(8,128)} %x_ref.5) | copy-start | bytes 786436
  3.4 0.9 %copy-start.4 = (f32[128,512]{1,0:T(8,128)S(1)}, f32[128,512]{1,0:T(8,128)}, u32[]{:S(2)}) copy-start(f32[128,512]{1,0:T(8,128)} %y_ref.5) | copy-start | bytes 786436
  4.3 0.9 %copy-start.6 = (f32[128,512]{1,0:T(8,128)S(1)}, f32[128,512]{1,0:T(8,128)}, u32[]{:S(2)}) copy-start(f32[128,512]{1,0:T(8,128)} %o_ref.5) | copy-start | bytes 786436
  5.3 11.6 %copy-start.1 = (f32[2,128,512]{2,1,0:T(8,128)S(1)}, f32[2,128,512]{2,1,0:T(8,128)}, u32[]{:S(2)}) copy-start(f32[2,128,512]{2,1,0:T(8,128)} %q_ref.5) | copy-start | bytes 1572868
  5.3 11.6 %copy-start.3 = (f32[128,512]{1,0:T(8,128)S(1)}, f32[128,512]{1,0:T(8,128)}, u32[]{:S(2)}) copy-start(f32[128,512]{1,0:T(8,128)} %x_ref.5) | copy-start | bytes 786436
  5.3 11.6 %copy-start.5 = (f32[128,512]{1,0:T(8,128)S(1)}, f32[128,512]{1,0:T(8,128)}, u32[]{:S(2)}) copy-start(f32[128,512]{1,0:T(8,128)} %y_ref.5) | copy-start | bytes 786436
  5.3 11.6 %copy-start.7 = (f32[128,512]{1,0:T(8,128)S(1)}, f32[128,512]{1,0:T(8,128)}, u32[]{:S(2)}) copy-start(f32[128,512]{1,0:T(8,128)} %o_ref.5) | copy-start | bytes 786436
  5.3 5.5 %collective-permute-start = (bf16[96,512]{1,0:T(8,128)(2,1)S(1)}, bf16[96,512]{1,0:T(8,128)(2,1)S(1)}, u32[]{:S(2)}, u32[]{:S(2)}) collective-permute-start(bf16[96,512]{1,0:T(8,128)(2,1)S(1)} %get-tuple-element.16), channel_id=1, source_target_pairs={{0,8},{8,16},{16,24},{24,32},{32,40},{40,48},{48,56},{56,64},{64,7... | collective-permute-start | bytes 294920 | tf_op jit(solution)/shard_map/ppermute | solution.py:513
  9.2 7.7 %collective-permute-start.1 = (bf16[96,512]{1,0:T(8,128)(2,1)S(1)}, bf16[96,512]{1,0:T(8,128)(2,1)S(1)}, u32[]{:S(2)}, u32[]{:S(2)}) collective-permute-start(bf16[96,512]{1,0:T(8,128)(2,1)S(1)} %get-tuple-element.17), channel_id=1, source_target_pairs={{0,120},{8,0},{16,8},{24,16},{32,24},{40,32},{48,40},{56,48},{64,5... | collective-permute-start | bytes 294920 | tf_op jit(solution)/shard_map/ppermute | solution.py:513
  10.3 10.6 %copy-start.8 = (bf16[64,31,31]{0,2,1:T(8,128)(2,1)S(1)}, bf16[64,31,31]{0,2,1:T(8,128)(2,1)}, u32[]{:S(2)}) copy-start(bf16[64,31,31]{0,2,1:T(8,128)(2,1)} %param.7) | copy-start | bytes 369028
  17.2 5.1 %collective-permute-start.2 = (bf16[192,128]{1,0:T(8,128)(2,1)S(1)}, bf16[192,128]{1,0:T(8,128)(2,1)S(1)}, u32[]{:S(2)}, u32[]{:S(2)}) collective-permute-start(bf16[192,128]{1,0:T(8,128)(2,1)S(1)} %get-tuple-element.18), channel_id=1, source_target_pairs={{0,1},{1,2},{2,3},{3,4},{4,5},{5,6},{6,7},{7,0},{8,9},{9,10},{10,1... | collective-permute-start | bytes 147464 | tf_op jit(solution)/shard_map/ppermute | solution.py:513
  18.0 4.3 %collective-permute-start.3 = (bf16[192,128]{1,0:T(8,128)(2,1)S(1)}, bf16[192,128]{1,0:T(8,128)(2,1)S(1)}, u32[]{:S(2)}, u32[]{:S(2)}) collective-permute-start(bf16[192,128]{1,0:T(8,128)(2,1)S(1)} %get-tuple-element.19), channel_id=1, source_target_pairs={{0,7},{1,0},{2,1},{3,2},{4,3},{5,4},{6,5},{7,6},{8,15},{9,8},{10,9... | collective-permute-start | bytes 147464 | tf_op jit(solution)/shard_map/ppermute | solution.py:513
  30.4 2.6 %collective-permute-start.4 = (bf16[48,640]{1,0:T(8,128)(2,1)S(1)}, bf16[48,640]{1,0:T(8,128)(2,1)S(1)}, u32[]{:S(2)}, u32[]{:S(2)}) collective-permute-start(bf16[48,640]{1,0:T(8,128)(2,1)S(1)} %get-tuple-element.26), channel_id=1, source_target_pairs={{0,8},{8,16},{16,24},{24,32},{32,40},{40,48},{48,56},{56,64},{64,7... | collective-permute-start | bytes 184328 | tf_op jit(solution)/shard_map/ppermute | solution.py:513
  31.7 7.3 %collective-permute-start.5 = (bf16[48,640]{1,0:T(8,128)(2,1)S(1)}, bf16[48,640]{1,0:T(8,128)(2,1)S(1)}, u32[]{:S(2)}, u32[]{:S(2)}) collective-permute-start(bf16[48,640]{1,0:T(8,128)(2,1)S(1)} %get-tuple-element.27), channel_id=1, source_target_pairs={{0,120},{8,0},{16,8},{24,16},{32,24},{40,32},{48,40},{56,48},{64,5... | collective-permute-start | bytes 184328 | tf_op jit(solution)/shard_map/ppermute | solution.py:513
  39.0 5.1 %collective-permute-start.6 = (bf16[192,128]{1,0:T(8,128)(2,1)S(1)}, bf16[192,128]{1,0:T(8,128)(2,1)S(1)}, u32[]{:S(2)}, u32[]{:S(2)}) collective-permute-start(bf16[192,128]{1,0:T(8,128)(2,1)S(1)} %get-tuple-element.28), channel_id=1, source_target_pairs={{0,1},{1,2},{2,3},{3,4},{4,5},{5,6},{6,7},{7,0},{8,9},{9,10},{10,1... | collective-permute-start | bytes 147464 | tf_op jit(solution)/shard_map/ppermute | solution.py:513
  39.9 4.2 %collective-permute-start.7 = (bf16[192,128]{1,0:T(8,128)(2,1)S(1)}, bf16[192,128]{1,0:T(8,128)(2,1)S(1)}, u32[]{:S(2)}, u32[]{:S(2)}) collective-permute-start(bf16[192,128]{1,0:T(8,128)(2,1)S(1)} %get-tuple-element.29), channel_id=1, source_target_pairs={{0,7},{1,0},{2,1},{3,2},{4,3},{5,4},{6,5},{7,6},{8,15},{9,8},{10,9... | collective-permute-start | bytes 147464 | tf_op jit(solution)/shard_map/ppermute | solution.py:513

commit v3 on v2

v3 whole, which is shorter than its diff:
```python
import jax
import jax.numpy as jnp
from jax import lax
from jax.experimental import pallas as pl
from jax.experimental.pallas import tpu as pltpu
from jax.sharding import PartitionSpec as P

SIGMA = 0.15
TAU = 0.6
TV = 0.5
F32 = jnp.float32
BF16 = jnp.bfloat16

ROWS = 128
COLS = 512
XO = 80
YO = 64
WIDE = 640
FULL = 768
SEGS1 = ((0, 48, 64), (48, 128, 144), (176, 48, 64))
SEGS2 = ((0, 16, 32), (16, 128, 144), (144, 16, 32))
PATCHES1 = ((0, 1), (2, 3, 4, 5), (6, 7, 8, 9), (10, 11, 12, 13), (14, 15, 16, 17), (18, 19))
PATCHES2 = ((1,), (2, 3, 4, 5), (6, 7, 8, 9), (10, 11, 12, 13), (14, 15, 16, 17), (18,))
SX, SXL, SC, SCL, SO, S1, S2, SM, STRIP = 0, 64, 80, 128, 144, 160, 192, 224, 240


def iota(shape, dim):
    return lax.broadcasted_iota(jnp.int32, shape, dim)


def split(value):
    hi = value.astype(BF16).astype(F32)
    return hi, value - hi


def lanes(value, shift):
    shift = shift % value.shape[1]
    return pltpu.roll(value, shift, 1) if shift else value


def rows(value, shift):
    shift = shift % value.shape[0]
    return pltpu.roll(value, shift, 0) if shift else value


def between(shape, lo, hi):
    lane = iota(shape, 1)
    return (lane >= lo) & (lane < hi)


def flags():
    row = lax.axis_index("row")
    col = lax.axis_index("col")
    return (
        row > 0,
        row < lax.axis_size("row") - 1,
        col > 0,
        col < lax.axis_size("col") - 1,
    )


def index_line(idx_ref, width):
    lane = iota((1, width), 1)
    line = jnp.zeros((1, width), F32)
    for j in range(4):
        line = jnp.where(lane == 1 + j, idx_ref[0:1, j : j + 1].astype(F32), line)
    return line


def pack_rows_kernel(x_hbm, y_hbm, o_hbm, q_hbm, idx_ref, down_ref, up_ref, x_ref, y_ref, o_ref, q_ref, sems):
    copies = [
        pltpu.make_async_copy(src, dst, sems.at[i])
        for i, (src, dst) in enumerate(((x_hbm, x_ref), (y_hbm, y_ref), (o_hbm, o_ref), (q_hbm, q_ref)))
    ]
    for copy in copies:
        copy.start()
    line = index_line(idx_ref, COLS)
    copies[0].wait()
    for out, x_at, low in ((down_ref, 64, 112), (up_ref, 0, 0)):
        out[SX : SX + 64] = x_ref[x_at : x_at + 64].astype(BF16)
        out[SXL : SXL + 16] = split(x_ref[low : low + 16])[1].astype(BF16)
    copies[1].wait()
    copies[2].wait()
    for out, c_at, low in ((down_ref, 80, 112), (up_ref, 0, 0)):
        out[SC : SC + 48] = (y_ref[c_at : c_at + 48] - SIGMA * o_ref[c_at : c_at + 48]).astype(BF16)
        c = y_ref[low : low + 16] - SIGMA * o_ref[low : low + 16]
        out[SCL : SCL + 16] = split(c)[1].astype(BF16)
        out[SO : SO + 16] = o_ref[low : low + 16].astype(BF16)
    copies[3].wait()
    row = iota((16, COLS), 0)
    for out, q_at, edge in ((down_ref, 96, 127), (up_ref, 0, 0)):
        out[S1 : S1 + 32] = q_ref[0, q_at : q_at + 32].astype(BF16)
        out[S2 : S2 + 32] = q_ref[1, q_at : q_at + 32].astype(BF16)
        misc = jnp.zeros((16, COLS), F32)
        for place in range(2):
            misc = jnp.where(row == place, split(q_ref[place, edge : edge + 1])[1], misc)
        misc = jnp.where(row == 2, line, misc)
        out[SM : SM + 16] = misc.astype(BF16)


def pack_cols_kernel(x_ref, y_ref, o_ref, q_ref, idx_ref, top_ref, bot_ref, right_ref, left_ref):
    for out, base in ((right_ref, 384), (left_ref, 0)):
        right = base > 0
        own = slice(base, base + 128)

        def strip(ref, at, count):
            return ref[at : at + count, own].astype(F32)

        def column(middle, at, count, shift):
            parts = [strip(top_ref, at, count), middle, strip(bot_ref, at, count)]
            return lanes(jnp.concatenate(parts, axis=0), shift)

        seen = o_ref[:, own]
        x_hi, x_lo = split(x_ref[:, own])
        c_hi, c_lo = split(y_ref[:, own] - SIGMA * seen)
        zeros = jnp.zeros((128, 128), F32)
        buf = column(x_hi, SX, 64, 80)
        part = jnp.concatenate([column(c_hi, SC, 48, 0 if right else 16), zeros[:32]], axis=0)
        at = 80 if right else 16
        buf = jnp.where(between((256, 128), at, at + 48), part, buf)
        part = jnp.concatenate([column(seen, SO, 16, 16 if right else 64), zeros[:96]], axis=0)
        at = 0 if right else 64
        buf = jnp.where(between((256, 128), at, at + 16), part, buf)
        out[0] = buf.astype(BF16)
        buf = jnp.concatenate([column(q_ref[0, :, own], S1, 32, 80), zeros[:64]], axis=0)
        part = jnp.concatenate(
            [column(q_ref[1, :, own], S2, 32, 112 if right else 0), zeros[:64]], axis=0
        )
        at = 80 if right else 0
        buf = jnp.where(between((256, 128), at, at + 32), part, buf)
        shift = 0 if right else 32
        part = jnp.concatenate(
            [
                zeros[:48],
                lanes(strip(top_ref, SXL, 16), shift),
                lanes(x_lo, shift),
                lanes(strip(bot_ref, SXL, 16), shift),
                zeros[:48],
            ],
            axis=0,
        )
        at = 112 if right else 32
        buf = jnp.where(between((256, 128), at, at + 16), part, buf)
        shift = 16 if right else 64
        part = jnp.concatenate(
            [
                zeros[:32],
                lanes(strip(top_ref, SCL, 16), shift),
                lanes(c_lo, shift),
                lanes(strip(bot_ref, SCL, 16), shift),
                zeros[:64],
            ],
            axis=0,
        )
        at = 0 if right else 64
        buf = jnp.where(between((256, 128), at, at + 16), part, buf)
        misc_t = strip(top_ref, SM, 16)
        misc_b = strip(bot_ref, SM, 16)
        if right:
            for comp in range(2):
                low = lanes(split(q_ref[comp, :, own])[1], 17 + comp)
                part = jnp.concatenate([zeros[:32], low, zeros[:96]], axis=0)
                buf = jnp.where(between((256, 128), 16 + comp, 17 + comp), part, buf)
        row = iota((256, 1), 0)
        spot = 4 if right else 1
        first = top_ref[SM : SM + 16, 0:128].astype(F32)[2:3, spot : spot + 1]
        last = bot_ref[SM : SM + 16, 0:128].astype(F32)[2:3, spot : spot + 1]
        mine = idx_ref[0:1, spot - 1 : spot].astype(F32)
        entry = jnp.where(row == 0, first, jnp.where(row == 1, mine, last))
        at = 18 if right else 112
        buf = jnp.where(between((256, 128), at, at + 1), entry, buf)
        out[1] = buf.astype(BF16)


def build_taps(tab_ref, t_ref):
    k = iota((32, 128), 0)
    j = iota((32, 128), 1) % 32
    lower = j <= k
    sub = iota((8, 128), 0)
    bits = [(sub // (1 << n)) % 2 == 1 for n in range(3)]
    for patch in range(18):
        at = 8 * (patch // 6) + patch % 6
        for e in range(8):
            skew = jnp.broadcast_to(tab_ref[at : at + 1, 128 * e : 128 * e + 128], (8, 128))
            for n in range(3):
                skew = jnp.where(bits[n], lanes(skew, 1 << n), skew)
            low = jnp.concatenate([lanes(skew, 8 * v - 31) for v in range(4)], axis=0)
            high = jnp.concatenate([lanes(skew, 8 * v + 1) for v in range(4)], axis=0)
            block = jnp.concatenate(
                [jnp.where(lower, low, 0.0), jnp.where(lower, 0.0, high)], axis=0
            )
            a1, half = e // 2, e % 2
            t_ref[patch, 64 * a1 : 64 * a1 + 64, 128 * half : 128 * half + 128] = block.astype(BF16)


def windows(xe_ref, p_ref, count):
    low = between((count, 128), 0, 64)
    tail = between((count, 128), 96, 128)
    for tile in range(5):
        here = slice(128 * tile, 128 * tile + 128)
        after = slice(128 * tile + 128, 128 * tile + 256)
        x0 = xe_ref[0:count, here]
        x8 = xe_ref[8 : count + 8, here]
        w0 = jnp.where(tail, x0, xe_ref[0:count, after])
        w8 = jnp.where(tail, x8, xe_ref[8 : count + 8, after])
        p_ref[4 * tile, 0:count] = jnp.where(low, x0, lanes(x8, 64)).astype(BF16)
        p_ref[4 * tile + 1, 0:count] = jnp.where(low, lanes(x0, 96), lanes(x8, 32)).astype(BF16)
        p_ref[4 * tile + 2, 0:count] = jnp.where(low, lanes(x0, 64), x8).astype(BF16)
        p_ref[4 * tile + 3, 0:count] = jnp.where(low, lanes(w0, 32), lanes(w8, 96)).astype(BF16)


def blur(segs, patches, p_ref, t_ref, a_ref, c_ref, y_ref, row_ok, col_ok):
    present = [b for blocks in patches for b in blocks]
    for seg, (first, size, padded) in enumerate(segs):
        for patch, blocks in enumerate(patches):
            lhs = jnp.concatenate(
                [
                    jnp.concatenate(
                        [
                            p_ref[b, first : first + padded],
                            p_ref[b, first + 16 : first + 16 + padded],
                        ],
                        axis=1,
                    )
                    for b in blocks
                ],
                axis=0,
            )
            v = jnp.dot(lhs, t_ref[6 * seg + patch], preferred_element_type=F32)
            for place, b in enumerate(blocks):
                part = v[place * padded : place * padded + padded]
                a_ref[b, 0:padded] = part[:, :128] + rows(part[:, 128:], -4)
        low = between((padded, 128), 0, 64)
        even = iota((padded, 128), 1) % 64 < 32
        for tile in range(5):
            a = [
                a_ref[4 * tile + p, 0:padded]
                if 4 * tile + p in present
                else jnp.zeros((padded, 128), F32)
                for p in range(4)
            ]
            e = []
            for p in range(2):
                z = lanes(jnp.where(low, a[p + 2], a[p]), 64)
                e.append(jnp.where(low, a[p], z) + rows(jnp.where(low, z, a[p + 2]), -2))
            m1 = jnp.where(even, e[0], lanes(e[1], 32))
            m2 = jnp.where(even, lanes(e[0], 96), e[1])
            blurred = (m1 + rows(m2, -1))[0:size]
            here = slice(128 * tile, 128 * tile + 128)
            new = (c_ref[first : first + size, here] + SIGMA * blurred) / (1.0 + SIGMA)
            keep = col_ok(tile, size) & row_ok(seg)
            y_ref[first : first + size, here] = jnp.where(keep, new, 0.0)


def adjoint(segs, patches, y_ref, t_ref, l_ref, f_ref, z_ref):
    present = [b for blocks in patches for b in blocks]
    z_ref[...] = jnp.zeros_like(z_ref)
    for seg, (first, size, padded) in enumerate(segs):
        low = between((padded, 128), 0, 64)
        even = iota((padded, 128), 1) % 64 < 32
        for tile in range(5):
            here = slice(128 * tile, 128 * tile + 128)
            o = jnp.concatenate(
                [y_ref[first : first + size, here], jnp.zeros((padded - size, 128), F32)], axis=0
            )
            o1 = rows(o, 1)
            e = [jnp.where(even, o, lanes(o1, 32)), jnp.where(even, lanes(o, 96), o1)]
            for p in range(2):
                s = rows(e[p], 2)
                for place in (p, p + 2):
                    b = 4 * tile + place
                    if b not in present:
                        continue
                    if place < 2:
                        part = jnp.where(low, e[p], lanes(s, 64))
                    else:
                        part = jnp.where(low, lanes(e[p], 64), s)
                    l_ref[b, 0:padded, 0:128] = part.astype(BF16)
                    l_ref[b, 0:padded, 128:256] = rows(part, 4).astype(BF16)
        for patch, blocks in enumerate(patches):
            lhs = jnp.concatenate([l_ref[b, 0:padded] for b in blocks], axis=0)
            g = lax.dot_general(
                lhs, t_ref[6 * seg + patch], (((1,), (1,)), ((), ())), preferred_element_type=F32
            )
            zero = jnp.zeros((16, 128), F32)
            for place, b in enumerate(blocks):
                part = g[place * padded : place * padded + padded]
                f_ref[b, 0 : padded + 16] = jnp.concatenate(
                    [part[:, :128], zero], axis=0
                ) + jnp.concatenate([zero, part[:, 128:]], axis=0)
        tall = padded + 24
        low = between((tall, 128), 0, 64)
        head = between((tall, 128), 0, 32)
        pad8 = jnp.zeros((8, 128), F32)

        def both_ways(b):
            if b not in present:
                zero = jnp.zeros((tall, 128), F32)
                return zero, zero
            f = f_ref[b, 0 : padded + 16]
            return jnp.concatenate([f, pad8], axis=0), jnp.concatenate([pad8, f], axis=0)

        for tile in range(5):
            both = []
            for p in range(2):
                a0, a8 = both_ways(4 * tile + p)
                b0, b8 = both_ways(4 * tile + p + 2)
                both.append(jnp.where(low, a0, b8) + lanes(jnp.where(low, b0, a8), 64))
            turned = lanes(both[1], 32)
            here = slice(128 * tile, 128 * tile + 128)
            after = slice(128 * tile + 128, 128 * tile + 256)
            span = slice(first, first + tall)
            z_ref[span, here] += both[0] + jnp.where(head, 0.0, turned)
            z_ref[span, after] += jnp.where(head, turned, 0.0)


def total_variation(x_ref, x_first, q1i_ref, q2i_ref, q1_ref, q2_ref, chunks, place):
    row0, col0, limit_row, limit_col = place
    for chunk in chunks:
        start = 16 * chunk
        tall = x_ref[x_first + start : x_first + start + 24, 0:WIDE]
        x = tall[0:16]
        below = rows(tall, -1)[0:16]
        right = lanes(x, -1)
        r = row0 - 32 + start + iota((16, WIDE), 0)
        c = col0 - XO + iota((16, WIDE), 1)
        g1 = jnp.where(r < limit_row, below - x, 0.0)
        g2 = jnp.where(c < limit_col, right - x, 0.0)
        span = slice(start, start + 16)
        u1 = q1i_ref[span] + SIGMA * g1
        u2 = q2i_ref[span] + SIGMA * g2
        shrink = jnp.maximum(1.0, jnp.sqrt(u1 * u1 + u2 * u2) / TV)
        inv = 1.0 / shrink
        q1_ref[span] = u1 * inv
        q2_ref[span] = u2 * inv


def divergence(q1_ref, q2_ref, start, place):
    row0, col0, limit_row, limit_col = place
    above = max(start - 8, 0)
    m1 = q1_ref[above : start + 16]
    m2 = q2_ref[start : start + 16]
    r = row0 - 32 + above + iota(m1.shape, 0)
    c = col0 - XO + iota((16, WIDE), 1)
    m1 = jnp.where((r >= 0) & (r < limit_row), m1, 0.0)
    m2 = jnp.where((c >= 0) & (c < limit_col), m2, 0.0)
    return (m1 - rows(m1, 1))[start - above :] + (m2 - lanes(m2, 1))


def places():
    row = lax.axis_index("row")
    col = lax.axis_index("col")
    return (
        row * ROWS,
        col * COLS,
        lax.axis_size("row") * ROWS - 1,
        lax.axis_size("col") * COLS - 1,
    )


def masks():
    top, bot, left, right = flags()

    def row_ok(seg):
        if seg == 1:
            return jnp.bool_(True)
        return top if seg == 0 else bot

    def col_ok(tile, size):
        lane = iota((size, 128), 1)
        if tile == 0:
            return (lane >= YO) | left
        if tile == 4:
            return (lane < YO) | right
        return jnp.ones((size, 128), jnp.bool_)

    return row_ok, col_ok


def widen(value, shift, width=WIDE):
    pad = jnp.zeros((value.shape[0], width - COLS), F32)
    return lanes(jnp.concatenate([value, pad], axis=1), shift)


def select_tables(table_ref, idx_ref, top_ref, bot_ref, lf_ref, rt_ref, tab_ref):
    lane = iota((1, 128), 1)
    total = jnp.full((1, 128), -1.0, F32)
    lines = (
        top_ref[SM : SM + 16, 0:128].astype(F32)[2:3],
        index_line(idx_ref, 128),
        bot_ref[SM : SM + 16, 0:128].astype(F32)[2:3],
    )
    lf = lf_ref[1, 0:16].astype(F32)
    rt = rt_ref[1, 0:16].astype(F32)
    for r in range(3):
        line = jnp.where(lane == 0, lf[r : r + 1, 18:19], lines[r])
        line = jnp.where(lane == 5, rt[r : r + 1, 112:113], line)
        line = lanes(line, 8 * r)
        total = jnp.where((lane >= 8 * r) & (lane < 8 * r + 6), line, total)
    onehot = jnp.where(total == iota((64, 128), 0).astype(F32), 1.0, 0.0).astype(BF16)
    picked = lax.dot_general(
        onehot, table_ref[...], (((0,), (0,)), ((), ())), preferred_element_type=F32
    )
    tab_ref[...] = picked[0:24]


def main_kernel(
    x_ref, y_ref, o_ref, q_ref, idx_ref, table_ref, top_ref, bot_ref, lf_ref, rt_ref,
    x2_ref, y2_ref,
    xe_ref, c_ref, ob_ref, ys_ref, q1_ref, q2_ref, tab_ref, t_ref, p_ref, a_ref, l_ref, f_ref,
    z_ref, xb_ref, x1_ref,
):
    top_ok, bot_ok, left_ok, right_ok = flags()
    place = places()
    select_tables(table_ref, idx_ref, top_ref, bot_ref, lf_ref, rt_ref, tab_ref)
    build_taps(tab_ref, t_ref)

    def f32(ref, at, count):
        return ref[at : at + count].astype(F32)

    zero = jnp.zeros((48, COLS), F32)
    above = f32(top_ref, SX, 64) + jnp.concatenate([zero, f32(top_ref, SXL, 16)], axis=0)
    below = f32(bot_ref, SX, 64) + jnp.concatenate([f32(bot_ref, SXL, 16), zero], axis=0)
    xe_ref[0:64] = widen(jnp.where(top_ok, above, 0.0), XO, FULL)
    xe_ref[64:192] = widen(x_ref[...], XO, FULL)
    xe_ref[192:256] = widen(jnp.where(bot_ok, below, 0.0), XO, FULL)
    xe_ref[256:272] = jnp.zeros((16, FULL), F32)
    rr = iota((256, 128), 0)
    rows_ok = ((rr >= 64) | top_ok) & ((rr < 192) | bot_ok)
    lf0 = lf_ref[0].astype(F32)
    lf1 = lf_ref[1].astype(F32)
    rt0 = rt_ref[0].astype(F32)
    rt1 = rt_ref[1].astype(F32)
    shape = (256, 128)
    side = jnp.where(between(shape, 16, 80), lf0, 0.0)
    side += jnp.where(between(shape, 64, 80), lanes(lf1, 80), 0.0)
    xe_ref[0:256, 0:128] += jnp.where(rows_ok & left_ok, side, 0.0)
    side = jnp.where(between(shape, 80, 128), rt0, 0.0)
    side += jnp.where(between(shape, 80, 96), lanes(rt1, 48), 0.0)
    xe_ref[0:256, 512:640] += jnp.where(rows_ok & right_ok, side, 0.0)
    side = jnp.where(between(shape, 0, 16), rt0, 0.0)
    xe_ref[0:256, 640:768] += jnp.where(rows_ok & right_ok, side, 0.0)
    seen = o_ref[...]
    c_ref[48:176] = widen(y_ref[...] - SIGMA * seen, YO)
    ob_ref[16:144] = widen(seen, YO)
    zero = jnp.zeros((32, COLS), F32)
    above = f32(top_ref, SC, 48) + jnp.concatenate([zero, f32(top_ref, SCL, 16)], axis=0)
    below = f32(bot_ref, SC, 48) + jnp.concatenate([f32(bot_ref, SCL, 16), zero], axis=0)
    c_ref[0:48] = widen(above, YO)
    c_ref[176:224] = widen(below, YO)
    ob_ref[0:16] = widen(f32(top_ref, SO, 16), YO)
    ob_ref[144:160] = widen(f32(bot_ref, SO, 16), YO)
    shape = (224, 128)
    side = lanes(lf0[0:224], 64) + jnp.where(between(shape, 48, 64), lanes(lf1[0:224], 48), 0.0)
    c_ref[:, 0:128] = jnp.where(between(shape, 16, 64), side, c_ref[:, 0:128])
    side = lanes(rt0[0:224], 48) + jnp.where(between(shape, 64, 80), rt1[0:224], 0.0)
    c_ref[:, 512:640] = jnp.where(between(shape, 64, 112), side, c_ref[:, 512:640])
    shape = (160, 128)
    at = between(shape, 48, 64)
    ob_ref[:, 0:128] = jnp.where(at, lanes(lf0[0:160], 48), ob_ref[:, 0:128])
    ob_ref[:, 512:640] = jnp.where(between(shape, 64, 80), rt0[0:160], ob_ref[:, 512:640])
    rix = iota((32, COLS), 0)
    misc = f32(top_ref, SM, 16)
    shape = (192, 128)
    for comp, (ref, section) in enumerate(((q1_ref, S1), (q2_ref, S2))):
        above = f32(top_ref, section, 32) + jnp.where(rix == 31, misc[comp : comp + 1], 0.0)
        ref[0:32] = widen(above, XO)
        ref[32:160] = widen(q_ref[comp], XO)
        ref[160:192] = widen(f32(bot_ref, section, 32), XO)
        side = lanes(lf1[0:192], 96 * comp)
        side += jnp.where(between(shape, 79, 80), lanes(lf1[0:192], 63 - comp), 0.0)
        ref[:, 0:128] = jnp.where(between(shape, 48, 80), side, ref[:, 0:128])
        side = lanes(rt1[0:192], 80 * comp)
        ref[:, 512:640] = jnp.where(between(shape, 80, 112), side, ref[:, 512:640])
    row_ok, col_ok = masks()
    windows(xe_ref, p_ref, 256)
    blur(SEGS1, PATCHES1, p_ref, t_ref, a_ref, c_ref, ys_ref, row_ok, col_ok)
    total_variation(xe_ref, 32, q1_ref, q2_ref, q1_ref, q2_ref, range(12), place)
    adjoint(SEGS1, PATCHES1, ys_ref, t_ref, l_ref, f_ref, z_ref)
    lane = iota((16, WIDE), 1)
    inside = ((lane >= XO) | left_ok) & ((lane < XO + COLS) | right_ok)
    for chunk in range(12):
        start = 16 * chunk
        ext = slice(32 + start, 48 + start)
        x = xe_ref[ext, 0:WIDE]
        new = x - TAU * (z_ref[ext, 0:WIDE] - divergence(q1_ref, q2_ref, start, place))
        keep = inside & (top_ok if chunk < 2 else bot_ok) if chunk < 2 or chunk >= 10 else inside
        xb_ref[start : start + 16, 0:WIDE] = jnp.where(keep, 2.0 * new - x, 0.0)
        if 2 <= chunk < 10:
            x1_ref[start - 32 : start - 16] = new
    xb_ref[192:208, 0:WIDE] = jnp.zeros((16, WIDE), F32)
    xb_ref[:, WIDE:FULL] = jnp.zeros((208, FULL - WIDE), F32)
    c_ref[0:160] = ys_ref[32:192] - SIGMA * ob_ref[...]
    windows(xb_ref, p_ref, 192)
    blur(SEGS2, PATCHES2, p_ref, t_ref, a_ref, c_ref, ys_ref, row_ok, col_ok)
    total_variation(xb_ref, 0, q1_ref, q2_ref, q1_ref, q2_ref, range(1, 10), place)
    adjoint(SEGS2, PATCHES2, ys_ref, t_ref, l_ref, f_ref, z_ref)
    for chunk in range(8):
        span = slice(16 * chunk, 16 * chunk + 16)
        ext = slice(32 + 16 * chunk, 48 + 16 * chunk)
        div = divergence(q1_ref, q2_ref, 32 + 16 * chunk, place)
        new = x1_ref[span] - TAU * (z_ref[ext, 0:WIDE] - div)
        x2_ref[span] = lanes(new, -XO)[:, :COLS]
        y2_ref[span] = lanes(ys_ref[16 + 16 * chunk : 32 + 16 * chunk], -YO)[:, :COLS]


def field(*shape, dtype=F32):
    return jax.ShapeDtypeStruct(shape, dtype)


def call(kernel, outs, scratch, *args, name, room=4, far=0):
    spaces = [pltpu.HBM] * far + [pltpu.VMEM] * (len(args) - far)
    return pl.pallas_call(
        kernel,
        out_shape=outs,
        in_specs=[pl.BlockSpec(memory_space=space) for space in spaces],
        scratch_shapes=scratch,
        compiler_params=pltpu.CompilerParams(vmem_limit_bytes=room * 1024 * 1024),
        name=name,
    )(*args)


def ring(block, axis, distance):
    count = lax.axis_size(axis)
    return lax.ppermute(block, axis, [(i, (i + distance) % count) for i in range(count)])


def per_device(observed, psf_table, psf_index, start_image, blur_dual, tv_dual):
    own = (start_image, blur_dual, observed, tv_dual)
    block = pltpu.VMEM((ROWS, COLS), F32)
    strip = field(STRIP, COLS, dtype=BF16)
    side = field(2, 256, 128, dtype=BF16)
    down, up = call(
        pack_rows_kernel, (strip, strip),
        [block, block, block, pltpu.VMEM((2, ROWS, COLS), F32), pltpu.SemaphoreType.DMA((4,))],
        *own, psf_index, name="pack_rows", far=4, room=60,
    )
    top = ring(down, "row", 1)
    bot = ring(up, "row", -1)
    table = psf_table.astype(F32)
    normed = (table / jnp.sum(table, axis=(1, 2), keepdims=True)).astype(BF16)
    normed = jnp.pad(normed[:, :, ::-1], ((0, 0), (1, 0), (0, 1))).reshape(64, 1024)
    to_right, to_left = call(
        pack_cols_kernel, (side, side), [], *own, psf_index, top, bot, name="pack_cols"
    )
    lf = ring(to_right, "col", 1)
    rt = ring(to_left, "col", -1)
    wide = pltpu.VMEM((192, WIDE), F32)
    return call(
        main_kernel,
        (field(ROWS, COLS), field(ROWS, COLS)),
        [
            pltpu.VMEM((272, FULL), F32), pltpu.VMEM((224, WIDE), F32),
            pltpu.VMEM((160, WIDE), F32), pltpu.VMEM((224, WIDE), F32),
            wide, wide, pltpu.VMEM((24, 1024), F32),
            pltpu.VMEM((18, 256, 256), BF16), pltpu.VMEM((20, 256, 128), BF16),
            pltpu.VMEM((20, 144, 128), F32), pltpu.VMEM((20, 144, 256), BF16),
            pltpu.VMEM((20, 160, 128), F32), pltpu.VMEM((272, FULL), F32),
            pltpu.VMEM((208, FULL), F32), pltpu.VMEM((ROWS, WIDE), F32),
        ],
        *own, psf_index, normed, top, bot, lf, rt, name="main", room=28,
    )


def solution(mesh):
    placed = (
        P("row", "col"),
        P(),
        P("row", "col"),
        P("row", "col"),
        P("row", "col"),
        P(None, "row", "col"),
    )
    return jax.shard_map(
        per_device,
        mesh=mesh,
        in_specs=placed,
        out_specs=(P("row", "col"), P("row", "col")),
        check_vma=False,
    )
```

time: 55.9 us -> 67.7 us (1.21)
  Pallas kernels: 19.9 us -> 47.3 us
  waiting for transfers between devices: 16.3 us -> 10.4 us
  starting transfers between devices: 12.5 us -> 7.53 us
  local copies, waits for them, and re-layouts: 4.37 us -> 0.41 us
    pallas_call x5 -> x3, Pallas kernels: 19.9 us -> 47.3 us  [call(): pl.pallas_call(kernel, out_shape=outs, in_specs=[pl.BlockSpec(memory_spac...]
    ppermute x8 -> x4, waiting for transfers between devices: 16.3 us -> 10.4 us  [ring(): lax.ppermute(block, axis, [(i, (i + distance) % count) for i in range(cou...]
    ppermute x8 -> x4, starting transfers between devices: 12.5 us -> 7.53 us  [ring(): lax.ppermute(block, axis, [(i, (i + distance) % count) for i in range(cou...]
    unnamed x18 -> x12, local copies, waits for them, and re-layouts: 3.91 us -> 0.02 us
  transfers between devices with their start and end apart: 8 -> 4, of which waited for: 6 -> 4; matrix products, arithmetic and copies ran while one was open for 3% -> 2% of each run, Pallas kernels for 0% -> 0%
where the time goes in v3:
time: 67.7 us; the launch traced here: 67.5 us
  Pallas kernels  47.3 us (70%)
  waiting for transfers between devices  10.4 us (15%)
  starting transfers between devices  7.53 us (11%)
  other arithmetic  1.16 us (2%)
  between operations  0.73 us (1%)
    pallas_call x3, Pallas kernels, call(): pl.pallas_call(kernel, out_shape=outs, in_specs=[pl.BlockSpec(memory_spac...  47.3 us
    ppermute x4, waiting for transfers between devices, ring(): lax.ppermute(block, axis, [(i, (i + distance) % count) for i in range(cou...  10.4 us
    ppermute x4, starting transfers between devices, ring(): lax.ppermute(block, axis, [(i, (i + distance) % count) for i in range(cou...  7.53 us
  transfers between devices with their start and end apart: 4, of which 4 were waited for; matrix products, arithmetic and copies ran while one was open for 2% of the time, Pallas kernels for 0%

profile of v3, /device:TPU:25, one launch (start us, length us, event | category | flops | bytes accessed | tf_op | source)
XLA Modules:
  0.0 67.5 jit_solution(11872028280357964207)
XLA Ops:
  0.6 0.0 copy-start
  0.6 0.0 copy-start.1
  0.7 0.0 copy-start.2
  0.7 0.0 copy-start.3
  0.7 2.9 %pack_rows.1 = (bf16[240,512]{1,0:T(8,128)(2,1)}, bf16[240,512]{1,0:T(8,128)(2,1)}) custom-call(f32[128,512]{1,0:T(8,128)} %x_ref.3, f32[128,512]{1,0:T(8,128)} %y_ref.3, f32[128,512]{1,0:T(8,128)} %o_ref.3, f32[2,128,512]{2,1,0:T(8,128)} %q_ref.3, s32[1,4]{1,0:T(1,128)} %idx_ref.5), custom_call_target="tpu_custom_call" | custom-call | tf_op jit(solution)/shard_map/pack_rows/pallas_call | solution.py:513
  3.5 3.9 %collective-permute-start = (bf16[240,512]{1,0:T(8,128)(2,1)}, bf16[240,512]{1,0:T(8,128)(2,1)S(1)}, u32[]{:S(2)}, u32[]{:S(2)}) collective-permute-start(bf16[240,512]{1,0:T(8,128)(2,1)} %get-tuple-element.6), channel_id=1, source_target_pairs={{0,8},{8,16},{16,24},{24,32},{32,40},{40,48},{48,56},{56,64},{64,7... | collective-permute-start | bytes 737288 | tf_op jit(solution)/shard_map/ppermute | solution.py:525
  7.4 0.0 copy-start.4
  7.4 0.0 collective-permute-start.1
  7.4 1.1 %convert_reduce_fusion = f32[64]{0:T(128)S(1)} fusion(bf16[64,31,31]{0,2,1:T(8,128)(2,1)} %param.7), kind=kLoop, calls=%fused_computation.1 | loop fusion | flops 122944 | bytes 123264 | tf_op jit(solution)/shard_map/reduce_sum | solution.py:541
  8.5 0.0 copy-start.5
  8.5 2.3 %collective-permute-done.top_ref = bf16[240,512]{1,0:T(8,128)(2,1)S(1)} collective-permute-done((bf16[240,512]{1,0:T(8,128)(2,1)}, bf16[240,512]{1,0:T(8,128)(2,1)S(1)}, u32[]{:S(2)}, u32[]{:S(2)}) %collective-permute-start) | collective-permute-done | bytes 245792 | tf_op jit(solution)/shard_map/ppermute | solution.py:525
  10.9 6.0 %collective-permute-done.1.bot_ref = bf16[240,512]{1,0:T(8,128)(2,1)S(1)} collective-permute-done((bf16[240,512]{1,0:T(8,128)(2,1)}, bf16[240,512]{1,0:T(8,128)(2,1)S(1)}, u32[]{:S(2)}, u32[]{:S(2)}) %collective-permute-start.1) | collective-permute-done | bytes 245792 | tf_op jit(solution)/shard_map/ppermute | solution.py:525
  16.9 0.0 copy-done
  16.9 0.0 copy-done.1
  16.9 0.0 copy-done.2
  16.9 0.0 copy-done.3
  16.9 0.0 copy-done.4
  16.9 0.5 pack_cols.1
  17.4 0.8 %collective-permute-start.2 = (bf16[2,256,128]{2,1,0:T(8,128)(2,1)S(1)}, bf16[2,256,128]{2,1,0:T(8,128)(2,1)S(1)}, u32[]{:S(2)}, u32[]{:S(2)}) collective-permute-start(bf16[2,256,128]{2,1,0:T(8,128)(2,1)S(1)} %get-tuple-element.8), channel_id=1, source_target_pairs={{0,1},{1,2},{2,3},{3,4},{4,5},{5,6},{6,7},{7,0},{8,9},{9,10},{10,1... | collective-permute-start | bytes 393224 | tf_op jit(solution)/shard_map/ppermute | solution.py:525
  18.2 2.8 %collective-permute-start.3 = (bf16[2,256,128]{2,1,0:T(8,128)(2,1)S(1)}, bf16[2,256,128]{2,1,0:T(8,128)(2,1)S(1)}, u32[]{:S(2)}, u32[]{:S(2)}) collective-permute-start(bf16[2,256,128]{2,1,0:T(8,128)(2,1)S(1)} %get-tuple-element.9), channel_id=1, source_target_pairs={{0,7},{1,0},{2,1},{3,2},{4,3},{5,4},{6,5},{7,6},{8,15},{9,8},{10,9... | collective-permute-start | bytes 393224 | tf_op jit(solution)/shard_map/ppermute | solution.py:525
  21.0 0.0 copy-done.5
  21.0 0.1 fusion
  21.1 0.2 rev.3
  21.3 0.1 pad.4
  21.3 0.1 copy.9.table_ref
  21.5 2.0 %collective-permute-done.2.lf_ref = bf16[2,256,128]{2,1,0:T(8,128)(2,1)S(1)} collective-permute-done((bf16[2,256,128]{2,1,0:T(8,128)(2,1)S(1)}, bf16[2,256,128]{2,1,0:T(8,128)(2,1)S(1)}, u32[]{:S(2)}, u32[]{:S(2)}) %collective-permute-start.2) | collective-permute-done | bytes 131104 | tf_op jit(solution)/shard_map/ppermute | solution.py:525
  23.5 0.1 collective-permute-done.3.rt_ref
  23.6 44.0 %main.1 = (f32[128,512]{1,0:T(8,128)}, f32[128,512]{1,0:T(8,128)}) custom-call(f32[128,512]{1,0:T(8,128)S(1)} %copy-done.1, f32[128,512]{1,0:T(8,128)S(1)} %copy-done.2, f32[128,512]{1,0:T(8,128)S(1)} %copy-done.3, f32[2,128,512]{2,1,0:T(8,128)S(1)} %copy-done, s32[1,4]{1,0:T(1,128)S(1)} %copy-done.4, bf16[64,1024]{1,0:T(8,128)(2,1)S(1)} %copy.9.table_ref, ...), custom_call_target="tpu_custom_call" | custom-call | tf_op jit(solution)/shard_map/main/pallas_call | solution.py:513
Async XLA Ops:
  0.6 16.2 %copy-start = (f32[2,128,512]{2,1,0:T(8,128)S(1)}, f32[2,128,512]{2,1,0:T(8,128)}, u32[]{:S(2)}) copy-start(f32[2,128,512]{2,1,0:T(8,128)} %q_ref.3) | copy-start | bytes 1572868
  0.6 16.2 %copy-start.1 = (f32[128,512]{1,0:T(8,128)S(1)}, f32[128,512]{1,0:T(8,128)}, u32[]{:S(2)}) copy-start(f32[128,512]{1,0:T(8,128)} %x_ref.3) | copy-start | bytes 786436
  0.7 16.2 %copy-start.2 = (f32[128,512]{1,0:T(8,128)S(1)}, f32[128,512]{1,0:T(8,128)}, u32[]{:S(2)}) copy-start(f32[128,512]{1,0:T(8,128)} %y_ref.3) | copy-start | bytes 786436
  0.7 16.2 %copy-start.3 = (f32[128,512]{1,0:T(8,128)S(1)}, f32[128,512]{1,0:T(8,128)}, u32[]{:S(2)}) copy-start(f32[128,512]{1,0:T(8,128)} %o_ref.3) | copy-start | bytes 786436
  3.5 7.3 %collective-permute-start = (bf16[240,512]{1,0:T(8,128)(2,1)}, bf16[240,512]{1,0:T(8,128)(2,1)S(1)}, u32[]{:S(2)}, u32[]{:S(2)}) collective-permute-start(bf16[240,512]{1,0:T(8,128)(2,1)} %get-tuple-element.6), channel_id=1, source_target_pairs={{0,8},{8,16},{16,24},{24,32},{32,40},{40,48},{48,56},{56,64},{64,7... | collective-permute-start | bytes 737288 | tf_op jit(solution)/shard_map/ppermute | solution.py:525
  7.4 9.5 %copy-start.4 = (s32[1,4]{1,0:T(1,128)S(1)}, s32[1,4]{1,0:T(1,128)}, u32[]{:S(2)}) copy-start(s32[1,4]{1,0:T(1,128)} %idx_ref.5) | copy-start | bytes 52
  7.4 9.4 %collective-permute-start.1 = (bf16[240,512]{1,0:T(8,128)(2,1)}, bf16[240,512]{1,0:T(8,128)(2,1)S(1)}, u32[]{:S(2)}, u32[]{:S(2)}) collective-permute-start(bf16[240,512]{1,0:T(8,128)(2,1)} %get-tuple-element.7), channel_id=1, source_target_pairs={{0,120},{8,0},{16,8},{24,16},{32,24},{40,32},{48,40},{56,48},{64,5... | collective-permute-start | bytes 737288 | tf_op jit(solution)/shard_map/ppermute | solution.py:525
  8.5 12.5 %copy-start.5 = (bf16[64,31,31]{0,2,1:T(8,128)(2,1)S(1)}, bf16[64,31,31]{0,2,1:T(8,128)(2,1)}, u32[]{:S(2)}) copy-start(bf16[64,31,31]{0,2,1:T(8,128)(2,1)} %param.7) | copy-start | bytes 369028
  17.4 6.1 %collective-permute-start.2 = (bf16[2,256,128]{2,1,0:T(8,128)(2,1)S(1)}, bf16[2,256,128]{2,1,0:T(8,128)(2,1)S(1)}, u32[]{:S(2)}, u32[]{:S(2)}) collective-permute-start(bf16[2,256,128]{2,1,0:T(8,128)(2,1)S(1)} %get-tuple-element.8), channel_id=1, source_target_pairs={{0,1},{1,2},{2,3},{3,4},{4,5},{5,6},{6,7},{7,0},{8,9},{9,10},{10,1... | collective-permute-start | bytes 393224 | tf_op jit(solution)/shard_map/ppermute | solution.py:525
  18.2 5.4 %collective-permute-start.3 = (bf16[2,256,128]{2,1,0:T(8,128)(2,1)S(1)}, bf16[2,256,128]{2,1,0:T(8,128)(2,1)S(1)}, u32[]{:S(2)}, u32[]{:S(2)}) collective-permute-start(bf16[2,256,128]{2,1,0:T(8,128)(2,1)S(1)} %get-tuple-element.9), channel_id=1, source_target_pairs={{0,7},{1,0},{2,1},{3,2},{4,3},{5,4},{6,5},{7,6},{8,15},{9,8},{10,9... | collective-permute-start | bytes 393224 | tf_op jit(solution)/shard_map/ppermute | solution.py:525

commit v4 on v3

--- a/solution.py
+++ b/solution.py
@@ -173,24 +173,30 @@
 
 
 def build_taps(tab_ref, t_ref):
-    k = iota((32, 128), 0)
-    j = iota((32, 128), 1) % 32
-    lower = j <= k
-    sub = iota((8, 128), 0)
+    sub = iota((144, 128), 0)
     bits = [(sub // (1 << n)) % 2 == 1 for n in range(3)]
-    for patch in range(18):
-        at = 8 * (patch // 6) + patch % 6
-        for e in range(8):
-            skew = jnp.broadcast_to(tab_ref[at : at + 1, 128 * e : 128 * e + 128], (8, 128))
-            for n in range(3):
-                skew = jnp.where(bits[n], lanes(skew, 1 << n), skew)
-            low = jnp.concatenate([lanes(skew, 8 * v - 31) for v in range(4)], axis=0)
-            high = jnp.concatenate([lanes(skew, 8 * v + 1) for v in range(4)], axis=0)
-            block = jnp.concatenate(
-                [jnp.where(lower, low, 0.0), jnp.where(lower, 0.0, high)], axis=0
-            )
-            a1, half = e // 2, e % 2
-            t_ref[patch, 64 * a1 : 64 * a1 + 64, 128 * half : 128 * half + 128] = block.astype(BF16)
+    for e in range(8):
+        a1, half = e // 2, e % 2
+        here = slice(128 * half, 128 * half + 128)
+        skew = jnp.concatenate(
+            [
+                jnp.broadcast_to(
+                    tab_ref[8 * r + p : 8 * r + p + 1, 128 * e : 128 * e + 128], (8, 128)
+                )
+                for r in range(3)
+                for p in range(6)
+            ],
+            axis=0,
+        )
+        for n in range(3):
+            skew = jnp.where(bits[n], lanes(skew, 1 << n), skew)
+        lower_all = [iota((144, 128), 1) % 32 <= sub % 8 + 8 * v for v in range(4)]
+        low = [jnp.where(lower_all[v], lanes(skew, 8 * v - 31), 0.0) for v in range(4)]
+        high = [jnp.where(lower_all[v], 0.0, lanes(skew, 8 * v + 1)) for v in range(4)]
+        for patch in range(18):
+            own = slice(8 * patch, 8 * patch + 8)
+            block = jnp.concatenate([part[own] for part in low + high], axis=0)
+            t_ref[patch, 64 * a1 : 64 * a1 + 64, here] = block.astype(BF16)
 
 
 def windows(xe_ref, p_ref, count):

time: 67.7 us -> 39.1 us (0.58)
  Pallas kernels: 47.3 us -> 18.7 us
    pallas_call x3, Pallas kernels: 47.3 us -> 18.7 us  [call(): pl.pallas_call(kernel, out_shape=outs, in_specs=[pl.BlockSpec(memory_spac...]
  transfers between devices with their start and end apart: 4 -> 4, of which waited for: 4 -> 4; matrix products, arithmetic and copies ran while one was open for 2% -> 4% of each run, Pallas kernels for 0% -> 0%
where the time goes in v4:
time: 39.1 us; the launch traced here: 38.9 us
  Pallas kernels  18.7 us (48%)
  waiting for transfers between devices  10.4 us (27%)
  starting transfers between devices  7.53 us (19%)
  other arithmetic  1.16 us (3%)
  between operations  0.73 us (2%)
  local copies, waits for them, and re-layouts  0.41 us (1%)
    pallas_call x3, Pallas kernels, call(): pl.pallas_call(kernel, out_shape=outs, in_specs=[pl.BlockSpec(memory_spac...  18.7 us
    ppermute x4, waiting for transfers between devices, ring(): lax.ppermute(block, axis, [(i, (i + distance) % count) for i in range(cou...  10.4 us
    ppermute x4, starting transfers between devices, ring(): lax.ppermute(block, axis, [(i, (i + distance) % count) for i in range(cou...  7.53 us
    reduce_sum x1, other arithmetic, per_device(): normed = (table / jnp.sum(table, axis=(1, 2), keepdims=True)).astype(BF16)  1.1 us
  transfers between devices with their start and end apart: 4, of which 4 were waited for; matrix products, arithmetic and copies ran while one was open for 4% of the time, Pallas kernels for 0%

profile of v4, /device:TPU:25, one launch (start us, length us, event | category | flops | bytes accessed | tf_op | source)
XLA Modules:
  0.0 38.9 jit_solution(13935091872372469337)
XLA Ops:
  0.6 0.0 copy-start
  0.6 0.0 copy-start.1
  0.7 0.0 copy-start.2
  0.7 0.0 copy-start.3
  0.7 2.9 %pack_rows.1 = (bf16[240,512]{1,0:T(8,128)(2,1)}, bf16[240,512]{1,0:T(8,128)(2,1)}) custom-call(f32[128,512]{1,0:T(8,128)} %x_ref.3, f32[128,512]{1,0:T(8,128)} %y_ref.3, f32[128,512]{1,0:T(8,128)} %o_ref.3, f32[2,128,512]{2,1,0:T(8,128)} %q_ref.3, s32[1,4]{1,0:T(1,128)} %idx_ref.5), custom_call_target="tpu_custom_call" | custom-call | tf_op jit(solution)/shard_map/pack_rows/pallas_call | solution.py:519
  3.5 3.9 %collective-permute-start = (bf16[240,512]{1,0:T(8,128)(2,1)}, bf16[240,512]{1,0:T(8,128)(2,1)S(1)}, u32[]{:S(2)}, u32[]{:S(2)}) collective-permute-start(bf16[240,512]{1,0:T(8,128)(2,1)} %get-tuple-element.6), channel_id=1, source_target_pairs={{0,8},{8,16},{16,24},{24,32},{32,40},{40,48},{48,56},{56,64},{64,7... | collective-permute-start | bytes 737288 | tf_op jit(solution)/shard_map/ppermute | solution.py:531
  7.4 0.0 copy-start.4
  7.4 0.0 collective-permute-start.1
  7.4 1.1 %convert_reduce_fusion = f32[64]{0:T(128)S(1)} fusion(bf16[64,31,31]{0,2,1:T(8,128)(2,1)} %param.7), kind=kLoop, calls=%fused_computation.1 | loop fusion | flops 122944 | bytes 123264 | tf_op jit(solution)/shard_map/reduce_sum | solution.py:547
  8.5 0.0 copy-start.5
  8.5 2.3 %collective-permute-done.top_ref = bf16[240,512]{1,0:T(8,128)(2,1)S(1)} collective-permute-done((bf16[240,512]{1,0:T(8,128)(2,1)}, bf16[240,512]{1,0:T(8,128)(2,1)S(1)}, u32[]{:S(2)}, u32[]{:S(2)}) %collective-permute-start) | collective-permute-done | bytes 245792 | tf_op jit(solution)/shard_map/ppermute | solution.py:531
  10.9 6.0 %collective-permute-done.1.bot_ref = bf16[240,512]{1,0:T(8,128)(2,1)S(1)} collective-permute-done((bf16[240,512]{1,0:T(8,128)(2,1)}, bf16[240,512]{1,0:T(8,128)(2,1)S(1)}, u32[]{:S(2)}, u32[]{:S(2)}) %collective-permute-start.1) | collective-permute-done | bytes 245792 | tf_op jit(solution)/shard_map/ppermute | solution.py:531
  16.9 0.0 copy-done
  16.9 0.0 copy-done.1
  16.9 0.0 copy-done.2
  16.9 0.0 copy-done.3
  16.9 0.0 copy-done.4
  16.9 0.5 %pack_cols.1 = (bf16[2,256,128]{2,1,0:T(8,128)(2,1)S(1)}, bf16[2,256,128]{2,1,0:T(8,128)(2,1)S(1)}) custom-call(f32[128,512]{1,0:T(8,128)S(1)} %copy-done.1, f32[128,512]{1,0:T(8,128)S(1)} %copy-done.2, f32[128,512]{1,0:T(8,128)S(1)} %copy-done.3, f32[2,128,512]{2,1,0:T(8,128)S(1)} %copy-done, s32[1,4]{1,0:T(1,128)S(1)} %copy-done.4, ...), custom_call_target="tpu_custom_call" | custom-call | tf_op jit(solution)/shard_map/pack_cols/pallas_call | solution.py:519
  17.4 0.8 %collective-permute-start.2 = (bf16[2,256,128]{2,1,0:T(8,128)(2,1)S(1)}, bf16[2,256,128]{2,1,0:T(8,128)(2,1)S(1)}, u32[]{:S(2)}, u32[]{:S(2)}) collective-permute-start(bf16[2,256,128]{2,1,0:T(8,128)(2,1)S(1)} %get-tuple-element.8), channel_id=1, source_target_pairs={{0,1},{1,2},{2,3},{3,4},{4,5},{5,6},{6,7},{7,0},{8,9},{9,10},{10,1... | collective-permute-start | bytes 393224 | tf_op jit(solution)/shard_map/ppermute | solution.py:531
  18.2 2.8 %collective-permute-start.3 = (bf16[2,256,128]{2,1,0:T(8,128)(2,1)S(1)}, bf16[2,256,128]{2,1,0:T(8,128)(2,1)S(1)}, u32[]{:S(2)}, u32[]{:S(2)}) collective-permute-start(bf16[2,256,128]{2,1,0:T(8,128)(2,1)S(1)} %get-tuple-element.9), channel_id=1, source_target_pairs={{0,7},{1,0},{2,1},{3,2},{4,3},{5,4},{6,5},{7,6},{8,15},{9,8},{10,9... | collective-permute-start | bytes 393224 | tf_op jit(solution)/shard_map/ppermute | solution.py:531
  21.0 0.0 copy-done.5
  21.0 0.1 fusion
  21.1 0.2 rev.3
  21.3 0.1 pad.4
  21.3 0.1 copy.9.table_ref
  21.5 2.0 %collective-permute-done.2.lf_ref = bf16[2,256,128]{2,1,0:T(8,128)(2,1)S(1)} collective-permute-done((bf16[2,256,128]{2,1,0:T(8,128)(2,1)S(1)}, bf16[2,256,128]{2,1,0:T(8,128)(2,1)S(1)}, u32[]{:S(2)}, u32[]{:S(2)}) %collective-permute-start.2) | collective-permute-done | bytes 131104 | tf_op jit(solution)/shard_map/ppermute | solution.py:531
  23.5 0.1 collective-permute-done.3.rt_ref
  23.6 15.4 %main.1 = (f32[128,512]{1,0:T(8,128)}, f32[128,512]{1,0:T(8,128)}) custom-call(f32[128,512]{1,0:T(8,128)S(1)} %copy-done.1, f32[128,512]{1,0:T(8,128)S(1)} %copy-done.2, f32[128,512]{1,0:T(8,128)S(1)} %copy-done.3, f32[2,128,512]{2,1,0:T(8,128)S(1)} %copy-done, s32[1,4]{1,0:T(1,128)S(1)} %copy-done.4, bf16[64,1024]{1,0:T(8,128)(2,1)S(1)} %copy.9.table_ref, ...), custom_call_target="tpu_custom_call" | custom-call | tf_op jit(solution)/shard_map/main/pallas_call | solution.py:519
Async XLA Ops:
  0.6 16.2 %copy-start = (f32[2,128,512]{2,1,0:T(8,128)S(1)}, f32[2,128,512]{2,1,0:T(8,128)}, u32[]{:S(2)}) copy-start(f32[2,128,512]{2,1,0:T(8,128)} %q_ref.3) | copy-start | bytes 1572868
  0.6 16.2 %copy-start.1 = (f32[128,512]{1,0:T(8,128)S(1)}, f32[128,512]{1,0:T(8,128)}, u32[]{:S(2)}) copy-start(f32[128,512]{1,0:T(8,128)} %x_ref.3) | copy-start | bytes 786436
  0.7 16.2 %copy-start.2 = (f32[128,512]{1,0:T(8,128)S(1)}, f32[128,512]{1,0:T(8,128)}, u32[]{:S(2)}) copy-start(f32[128,512]{1,0:T(8,128)} %y_ref.3) | copy-start | bytes 786436
  0.7 16.2 %copy-start.3 = (f32[128,512]{1,0:T(8,128)S(1)}, f32[128,512]{1,0:T(8,128)}, u32[]{:S(2)}) copy-start(f32[128,512]{1,0:T(8,128)} %o_ref.3) | copy-start | bytes 786436
  3.5 7.3 %collective-permute-start = (bf16[240,512]{1,0:T(8,128)(2,1)}, bf16[240,512]{1,0:T(8,128)(2,1)S(1)}, u32[]{:S(2)}, u32[]{:S(2)}) collective-permute-start(bf16[240,512]{1,0:T(8,128)(2,1)} %get-tuple-element.6), channel_id=1, source_target_pairs={{0,8},{8,16},{16,24},{24,32},{32,40},{40,48},{48,56},{56,64},{64,7... | collective-permute-start | bytes 737288 | tf_op jit(solution)/shard_map/ppermute | solution.py:531
  7.4 9.5 %copy-start.4 = (s32[1,4]{1,0:T(1,128)S(1)}, s32[1,4]{1,0:T(1,128)}, u32[]{:S(2)}) copy-start(s32[1,4]{1,0:T(1,128)} %idx_ref.5) | copy-start | bytes 52
  7.4 9.4 %collective-permute-start.1 = (bf16[240,512]{1,0:T(8,128)(2,1)}, bf16[240,512]{1,0:T(8,128)(2,1)S(1)}, u32[]{:S(2)}, u32[]{:S(2)}) collective-permute-start(bf16[240,512]{1,0:T(8,128)(2,1)} %get-tuple-element.7), channel_id=1, source_target_pairs={{0,120},{8,0},{16,8},{24,16},{32,24},{40,32},{48,40},{56,48},{64,5... | collective-permute-start | bytes 737288 | tf_op jit(solution)/shard_map/ppermute | solution.py:531
  8.5 12.5 %copy-start.5 = (bf16[64,31,31]{0,2,1:T(8,128)(2,1)S(1)}, bf16[64,31,31]{0,2,1:T(8,128)(2,1)}, u32[]{:S(2)}) copy-start(bf16[64,31,31]{0,2,1:T(8,128)(2,1)} %param.7) | copy-start | bytes 369028
  17.4 6.1 %collective-permute-start.2 = (bf16[2,256,128]{2,1,0:T(8,128)(2,1)S(1)}, bf16[2,256,128]{2,1,0:T(8,128)(2,1)S(1)}, u32[]{:S(2)}, u32[]{:S(2)}) collective-permute-start(bf16[2,256,128]{2,1,0:T(8,128)(2,1)S(1)} %get-tuple-element.8), channel_id=1, source_target_pairs={{0,1},{1,2},{2,3},{3,4},{4,5},{5,6},{6,7},{7,0},{8,9},{9,10},{10,1... | collective-permute-start | bytes 393224 | tf_op jit(solution)/shard_map/ppermute | solution.py:531
  18.2 5.4 %collective-permute-start.3 = (bf16[2,256,128]{2,1,0:T(8,128)(2,1)S(1)}, bf16[2,256,128]{2,1,0:T(8,128)(2,1)S(1)}, u32[]{:S(2)}, u32[]{:S(2)}) collective-permute-start(bf16[2,256,128]{2,1,0:T(8,128)(2,1)S(1)} %get-tuple-element.9), channel_id=1, source_target_pairs={{0,7},{1,0},{2,1},{3,2},{4,3},{5,4},{6,5},{7,6},{8,15},{9,8},{10,9... | collective-permute-start | bytes 393224 | tf_op jit(solution)/shard_map/ppermute | solution.py:531

commit v5 on v4

v5 whole, which is shorter than its diff:
```python
import jax
import jax.numpy as jnp
from jax import lax
from jax.experimental import pallas as pl
from jax.experimental.pallas import tpu as pltpu
from jax.sharding import PartitionSpec as P

SIGMA = 0.15
TAU = 0.6
TV = 0.5
F32 = jnp.float32
BF16 = jnp.bfloat16

ROWS = 128
COLS = 512
XO = 80
YO = 64
WIDE = 640
FULL = 768
SEGS1 = ((0, 48, 64), (48, 128, 144), (176, 48, 64))
SEGS2 = ((0, 16, 32), (16, 128, 144), (144, 16, 32))
PATCHES2 = ((1,), (2, 3, 4, 5), (6, 7, 8, 9), (10, 11, 12, 13), (14, 15, 16, 17), (18,))
INNER = ((0, (3, 4, 5)), (1, (6, 7, 8, 9)), (2, (10, 11, 12, 13)), (3, (14, 15, 16)))
OUTER = ((-1, (0, 1)), (0, (2,)), (3, (17,)), (4, (18, 19)))
ALL = tuple((patch - 1, blocks) for patch, blocks in enumerate(PATCHES2))
SX, SXL, SC, SCL, SO, S1, S2, SM, STRIP = 0, 64, 80, 128, 144, 160, 192, 224, 240


def iota(shape, dim):
    return lax.broadcasted_iota(jnp.int32, shape, dim)


def split(value):
    hi = value.astype(BF16).astype(F32)
    return hi, value - hi


def lanes(value, shift):
    shift = shift % value.shape[1]
    return pltpu.roll(value, shift, 1) if shift else value


def rows(value, shift):
    shift = shift % value.shape[0]
    return pltpu.roll(value, shift, 0) if shift else value


def between(shape, lo, hi):
    lane = iota(shape, 1)
    return (lane >= lo) & (lane < hi)


def flags():
    row = lax.axis_index("row")
    col = lax.axis_index("col")
    return (
        row > 0,
        row < lax.axis_size("row") - 1,
        col > 0,
        col < lax.axis_size("col") - 1,
    )


def index_line(idx_ref, width):
    lane = iota((1, width), 1)
    line = jnp.zeros((1, width), F32)
    for j in range(4):
        line = jnp.where(lane == 1 + j, idx_ref[0:1, j : j + 1].astype(F32), line)
    return line


def parities():
    return lax.axis_index("row") % 2 == 1, lax.axis_index("col") % 2 == 1


def chosen(flag, one_ref, two_ref):
    def read(at):
        return jnp.where(flag, one_ref[at].astype(F32), two_ref[at].astype(F32))

    return read


def sides(a_ref, b_ref, odd):
    return chosen(odd, a_ref, b_ref), chosen(odd, b_ref, a_ref)


def pack_rows_kernel(x_hbm, y_hbm, o_hbm, q_hbm, idx_ref, a_ref, b_ref, x_ref, y_ref, o_ref, q_ref, sems):
    copies = [
        pltpu.make_async_copy(src, dst, sems.at[i])
        for i, (src, dst) in enumerate(((x_hbm, x_ref), (y_hbm, y_ref), (o_hbm, o_ref), (q_hbm, q_ref)))
    ]
    for copy in copies:
        copy.start()
    line = index_line(idx_ref, COLS)
    odd, _ = parities()

    def put(at, count, down, up):
        a_ref[at : at + count] = jnp.where(odd, up, down).astype(BF16)
        b_ref[at : at + count] = jnp.where(odd, down, up).astype(BF16)

    copies[0].wait()
    put(SX, 64, x_ref[64:128], x_ref[0:64])
    put(SXL, 16, split(x_ref[112:128])[1], split(x_ref[0:16])[1])
    copies[1].wait()
    copies[2].wait()
    up = y_ref[0:48] - SIGMA * o_ref[0:48]
    down = y_ref[80:128] - SIGMA * o_ref[80:128]
    put(SC, 48, down, up)
    put(SCL, 16, split(down[32:48])[1], split(up[0:16])[1])
    put(SO, 16, o_ref[112:128], o_ref[0:16])
    copies[3].wait()
    put(S1, 32, q_ref[0, 96:128], q_ref[0, 0:32])
    put(S2, 32, q_ref[1, 96:128], q_ref[1, 0:32])
    row = iota((16, COLS), 0)
    rest = []
    for edge in (127, 0):
        misc = jnp.zeros((16, COLS), F32)
        for comp in range(2):
            misc = jnp.where(row == comp, split(q_ref[comp, edge : edge + 1])[1], misc)
        rest.append(jnp.where(row == 2, line, misc))
    put(SM, 16, *rest)


def pack_cols_kernel(x_ref, y_ref, o_ref, q_ref, idx_ref, ra_ref, rb_ref, a_ref, b_ref):
    odd_row, odd_col = parities()
    top, bot = sides(ra_ref, rb_ref, odd_row)
    made = []
    for base in (384, 0):
        right = base > 0
        own = slice(base, base + 128)

        def strip(read, at, count, own=own):
            return read((slice(at, at + count), own))

        def column(middle, at, count, shift):
            parts = [strip(top, at, count), middle, strip(bot, at, count)]
            return lanes(jnp.concatenate(parts, axis=0), shift)

        seen = o_ref[:, own]
        x_hi, x_lo = split(x_ref[:, own])
        c_hi, c_lo = split(y_ref[:, own] - SIGMA * seen)
        zeros = jnp.zeros((128, 128), F32)
        buf = column(x_hi, SX, 64, 80)
        part = jnp.concatenate([column(c_hi, SC, 48, 0 if right else 16), zeros[:32]], axis=0)
        at = 80 if right else 16
        buf = jnp.where(between((256, 128), at, at + 48), part, buf)
        part = jnp.concatenate([column(seen, SO, 16, 16 if right else 64), zeros[:96]], axis=0)
        at = 0 if right else 64
        buf = jnp.where(between((256, 128), at, at + 16), part, buf)
        made.append(buf)
        buf = jnp.concatenate([column(q_ref[0, :, own], S1, 32, 80), zeros[:64]], axis=0)
        part = jnp.concatenate(
            [column(q_ref[1, :, own], S2, 32, 112 if right else 0), zeros[:64]], axis=0
        )
        at = 80 if right else 0
        buf = jnp.where(between((256, 128), at, at + 32), part, buf)
        shift = 0 if right else 32
        part = jnp.concatenate(
            [
                zeros[:48],
                lanes(strip(top, SXL, 16), shift),
                lanes(x_lo, shift),
                lanes(strip(bot, SXL, 16), shift),
                zeros[:48],
            ],
            axis=0,
        )
        at = 112 if right else 32
        buf = jnp.where(between((256, 128), at, at + 16), part, buf)
        shift = 16 if right else 64
        part = jnp.concatenate(
            [
                zeros[:32],
                lanes(strip(top, SCL, 16), shift),
                lanes(c_lo, shift),
                lanes(strip(bot, SCL, 16), shift),
                zeros[:64],
            ],
            axis=0,
        )
        at = 0 if right else 64
        buf = jnp.where(between((256, 128), at, at + 16), part, buf)
        if right:
            for comp in range(2):
                low = lanes(split(q_ref[comp, :, own])[1], 17 + comp)
                part = jnp.concatenate([zeros[:32], low, zeros[:96]], axis=0)
                buf = jnp.where(between((256, 128), 16 + comp, 17 + comp), part, buf)
        row = iota((256, 1), 0)
        spot = 4 if right else 1
        first = top((slice(SM, SM + 16), slice(0, 128)))[2:3, spot : spot + 1]
        last = bot((slice(SM, SM + 16), slice(0, 128)))[2:3, spot : spot + 1]
        mine = idx_ref[0:1, spot - 1 : spot].astype(F32)
        entry = jnp.where(row == 0, first, jnp.where(row == 1, mine, last))
        at = 18 if right else 112
        buf = jnp.where(between((256, 128), at, at + 1), entry, buf)
        made.append(buf)
    for tile in range(2):
        a_ref[tile] = jnp.where(odd_col, made[2 + tile], made[tile]).astype(BF16)
        b_ref[tile] = jnp.where(odd_col, made[tile], made[2 + tile]).astype(BF16)


def build_taps(tab_ref, t_ref, places):
    size = 8 * len(places)
    sub = iota((size, 128), 0)
    bits = [(sub // (1 << n)) % 2 == 1 for n in range(3)]
    for e in range(8):
        a1, half = e // 2, e % 2
        here = slice(128 * half, 128 * half + 128)
        skew = jnp.concatenate(
            [
                jnp.broadcast_to(
                    tab_ref[at : at + 1, 128 * e : 128 * e + 128], (8, 128)
                )
                for at in places
            ],
            axis=0,
        )
        for n in range(3):
            skew = jnp.where(bits[n], lanes(skew, 1 << n), skew)
        lower_all = [iota((size, 128), 1) % 32 <= sub % 8 + 8 * v for v in range(4)]
        low = [jnp.where(lower_all[v], lanes(skew, 8 * v - 31), 0.0) for v in range(4)]
        high = [jnp.where(lower_all[v], 0.0, lanes(skew, 8 * v + 1)) for v in range(4)]
        for patch in range(len(places)):
            own = slice(8 * patch, 8 * patch + 8)
            block = jnp.concatenate([part[own] for part in low + high], axis=0)
            t_ref[patch, 64 * a1 : 64 * a1 + 64, here] = block.astype(BF16)


def windows(get, p_ref, blocks, count):
    low = between((count, 128), 0, 64)
    tail = between((count, 128), 96, 128)
    for b in blocks:
        tile, place = b // 4, b % 4
        x0, x8 = get(tile, 0), get(tile, 8)
        if place == 0:
            part = jnp.where(low, x0, lanes(x8, 64))
        elif place == 1:
            part = jnp.where(low, lanes(x0, 96), lanes(x8, 32))
        elif place == 2:
            part = jnp.where(low, lanes(x0, 64), x8)
        else:
            w0 = jnp.where(tail, x0, get(tile + 1, 0))
            w8 = jnp.where(tail, x8, get(tile + 1, 8))
            part = jnp.where(low, lanes(w0, 32), lanes(w8, 96))
        p_ref[b, 0:count] = part.astype(BF16)


def blur(segs, groups, taps, p_ref, a_ref, put):
    present = [b for _, blocks in groups for b in blocks]
    for seg, (first, size, padded) in enumerate(segs):
        for patch, blocks in groups:
            lhs = jnp.concatenate(
                [
                    jnp.concatenate(
                        [
                            p_ref[b, first : first + padded],
                            p_ref[b, first + 16 : first + 16 + padded],
                        ],
                        axis=1,
                    )
                    for b in blocks
                ],
                axis=0,
            )
            v = jnp.dot(lhs, taps(seg, patch), preferred_element_type=F32)
            for place, b in enumerate(blocks):
                part = v[place * padded : place * padded + padded]
                a_ref[b, 0:padded] = part[:, :128] + rows(part[:, 128:], -4)
        low = between((padded, 128), 0, 64)
        even = iota((padded, 128), 1) % 64 < 32
        for tile in sorted({b // 4 for b in present}):
            a = [
                a_ref[4 * tile + p, 0:padded]
                if 4 * tile + p in present
                else jnp.zeros((padded, 128), F32)
                for p in range(4)
            ]
            e = []
            for p in range(2):
                z = lanes(jnp.where(low, a[p + 2], a[p]), 64)
                e.append(jnp.where(low, a[p], z) + rows(jnp.where(low, z, a[p + 2]), -2))
            m1 = jnp.where(even, e[0], lanes(e[1], 32))
            m2 = jnp.where(even, lanes(e[0], 96), e[1])
            blurred = (m1 + rows(m2, -1))[0:size]
            put(seg, first, size, tile, blurred)


def adjoint(segs, groups, taps, get, l_ref, f_ref, z_ref):
    present = [b for _, blocks in groups for b in blocks]
    tiles = sorted({b // 4 for b in present})
    for seg, (first, size, padded) in enumerate(segs):
        low = between((padded, 128), 0, 64)
        even = iota((padded, 128), 1) % 64 < 32
        for tile in tiles:
            o = jnp.concatenate(
                [get(first, size, tile), jnp.zeros((padded - size, 128), F32)], axis=0
            )
            o1 = rows(o, 1)
            e = [jnp.where(even, o, lanes(o1, 32)), jnp.where(even, lanes(o, 96), o1)]
            for p in range(2):
                s = rows(e[p], 2)
                for place in (p, p + 2):
                    b = 4 * tile + place
                    if b not in present:
                        continue
                    if place < 2:
                        part = jnp.where(low, e[p], lanes(s, 64))
                    else:
                        part = jnp.where(low, lanes(e[p], 64), s)
                    l_ref[b, 0:padded, 0:128] = part.astype(BF16)
                    l_ref[b, 0:padded, 128:256] = rows(part, 4).astype(BF16)
        for patch, blocks in groups:
            lhs = jnp.concatenate([l_ref[b, 0:padded] for b in blocks], axis=0)
            g = lax.dot_general(
                lhs, taps(seg, patch), (((1,), (1,)), ((), ())), preferred_element_type=F32
            )
            zero = jnp.zeros((16, 128), F32)
            for place, b in enumerate(blocks):
                part = g[place * padded : place * padded + padded]
                f_ref[b, 0 : padded + 16] = jnp.concatenate(
                    [part[:, :128], zero], axis=0
                ) + jnp.concatenate([zero, part[:, 128:]], axis=0)
        tall = padded + 24
        low = between((tall, 128), 0, 64)
        head = between((tall, 128), 0, 32)
        pad8 = jnp.zeros((8, 128), F32)

        def both_ways(b):
            if b not in present:
                zero = jnp.zeros((tall, 128), F32)
                return zero, zero
            f = f_ref[b, 0 : padded + 16]
            return jnp.concatenate([f, pad8], axis=0), jnp.concatenate([pad8, f], axis=0)

        for tile in tiles:
            both = []
            for p in range(2):
                a0, a8 = both_ways(4 * tile + p)
                b0, b8 = both_ways(4 * tile + p + 2)
                both.append(jnp.where(low, a0, b8) + lanes(jnp.where(low, b0, a8), 64))
            turned = lanes(both[1], 32)
            here = slice(128 * tile, 128 * tile + 128)
            after = slice(128 * tile + 128, 128 * tile + 256)
            span = slice(first, first + tall)
            z_ref[span, here] += both[0] + jnp.where(head, 0.0, turned)
            z_ref[span, after] += jnp.where(head, turned, 0.0)


def total_variation(get_x, get_q, q1_ref, q2_ref, chunks, place):
    row0, col0, limit_row, limit_col = place
    for chunk in chunks:
        start = 16 * chunk
        tall = get_x(start, 24)
        x = tall[0:16]
        below = rows(tall, -1)[0:16]
        right = lanes(x, -1)
        r = row0 - 32 + start + iota((16, WIDE), 0)
        c = col0 - XO + iota((16, WIDE), 1)
        g1 = jnp.where(r < limit_row, below - x, 0.0)
        g2 = jnp.where(c < limit_col, right - x, 0.0)
        span = slice(start, start + 16)
        u1 = get_q(0, start) + SIGMA * g1
        u2 = get_q(1, start) + SIGMA * g2
        shrink = jnp.maximum(1.0, jnp.sqrt(u1 * u1 + u2 * u2) / TV)
        inv = 1.0 / shrink
        q1_ref[span] = u1 * inv
        q2_ref[span] = u2 * inv


def divergence(q1_ref, q2_ref, start, place):
    row0, col0, limit_row, limit_col = place
    above = max(start - 8, 0)
    m1 = q1_ref[above : start + 16]
    m2 = q2_ref[start : start + 16]
    r = row0 - 32 + above + iota(m1.shape, 0)
    c = col0 - XO + iota((16, WIDE), 1)
    m1 = jnp.where((r >= 0) & (r < limit_row), m1, 0.0)
    m2 = jnp.where((c >= 0) & (c < limit_col), m2, 0.0)
    return (m1 - rows(m1, 1))[start - above :] + (m2 - lanes(m2, 1))


def places():
    row = lax.axis_index("row")
    col = lax.axis_index("col")
    return (
        row * ROWS,
        col * COLS,
        lax.axis_size("row") * ROWS - 1,
        lax.axis_size("col") * COLS - 1,
    )


def masks():
    top, bot, left, right = flags()

    def row_ok(seg):
        if seg == 1:
            return jnp.bool_(True)
        return top if seg == 0 else bot

    def col_ok(tile, size):
        lane = iota((size, 128), 1)
        if tile == 0:
            return (lane >= YO) | left
        if tile == 4:
            return (lane < YO) | right
        return jnp.ones((size, 128), jnp.bool_)

    return row_ok, col_ok


def widen(value, shift, width=WIDE):
    pad = jnp.zeros((value.shape[0], width - COLS), F32)
    return lanes(jnp.concatenate([value, pad], axis=1), shift)


def select_tables(table_ref, total, tab_ref):
    onehot = jnp.where(total == iota((64, 128), 0).astype(F32), 1.0, 0.0).astype(BF16)
    picked = lax.dot_general(
        onehot, table_ref[...], (((0,), (0,)), ((), ())), preferred_element_type=F32
    )
    tab_ref[...] = picked[0:24]


def tile_of(value, tile):
    return value[:, 128 * tile : 128 * tile + 128]


def middle_kernel(
    x_ref, y_ref, o_ref, q_ref, idx_ref, table_ref, ra_ref, rb_ref,
    xe_ref, c_ref, ob_ref, ys_ref, q1_ref, q2_ref, z_ref, t_ref,
    tab_ref, p_ref, a_ref, l_ref, f_ref,
):
    top_ok, bot_ok, _, _ = flags()
    odd, _ = parities()
    top, bot = sides(ra_ref, rb_ref, odd)
    misc = slice(SM, SM + 16)
    lane = iota((1, 128), 1)
    lines = (
        top((misc, slice(0, 128)))[2:3], index_line(idx_ref, 128), bot((misc, slice(0, 128)))[2:3],
    )
    total = jnp.full((1, 128), -1.0, F32)
    for r in range(3):
        total = jnp.where((lane >= 8 * r) & (lane < 8 * r + 6), lanes(lines[r], 8 * r), total)
    select_tables(table_ref, total, tab_ref)
    build_taps(tab_ref, t_ref, [8 * r + 1 + p for r in range(3) for p in range(4)])

    def part(read, at, count):
        return read(slice(at, at + count))

    zero = jnp.zeros((48, COLS), F32)
    above = part(top, SX, 64) + jnp.concatenate([zero, part(top, SXL, 16)], axis=0)
    below = part(bot, SX, 64) + jnp.concatenate([part(bot, SXL, 16), zero], axis=0)
    xe_ref[0:64] = widen(jnp.where(top_ok, above, 0.0), XO, FULL)
    xe_ref[64:192] = widen(x_ref[...], XO, FULL)
    xe_ref[192:256] = widen(jnp.where(bot_ok, below, 0.0), XO, FULL)
    xe_ref[256:272] = jnp.zeros((16, FULL), F32)
    seen = o_ref[...]
    c_ref[48:176] = widen(y_ref[...] - SIGMA * seen, YO)
    ob_ref[16:144] = widen(seen, YO)
    zero = jnp.zeros((32, COLS), F32)
    above = part(top, SC, 48) + jnp.concatenate([zero, part(top, SCL, 16)], axis=0)
    below = part(bot, SC, 48) + jnp.concatenate([part(bot, SCL, 16), zero], axis=0)
    c_ref[0:48] = widen(above, YO)
    c_ref[176:224] = widen(below, YO)
    ob_ref[0:16] = widen(part(top, SO, 16), YO)
    ob_ref[144:160] = widen(part(bot, SO, 16), YO)
    rix = iota((32, COLS), 0)
    rest = top(misc)
    for comp, (ref, section) in enumerate(((q1_ref, S1), (q2_ref, S2))):
        above = part(top, section, 32) + jnp.where(rix == 31, rest[comp : comp + 1], 0.0)
        ref[0:32] = widen(above, XO)
        ref[32:160] = widen(q_ref[comp], XO)
        ref[160:192] = widen(part(bot, section, 32), XO)
    row_ok, _ = masks()

    def taps(seg, patch):
        return t_ref[4 * seg + patch]

    def get_x(tile, first):
        return xe_ref[first : first + 256, 128 * tile : 128 * tile + 128]

    def put(seg, first, size, tile, blurred):
        here = slice(128 * tile, 128 * tile + 128)
        new = (c_ref[first : first + size, here] + SIGMA * blurred) / (1.0 + SIGMA)
        ys_ref[first : first + size, here] = jnp.where(row_ok(seg), new, 0.0)

    def get_y(first, size, tile):
        return ys_ref[first : first + size, 128 * tile : 128 * tile + 128]

    windows(get_x, p_ref, range(3, 17), 256)
    blur(SEGS1, INNER, taps, p_ref, a_ref, put)
    z_ref[...] = jnp.zeros_like(z_ref)
    adjoint(SEGS1, INNER, taps, get_y, l_ref, f_ref, z_ref)


def main_kernel(
    idx_ref, table_ref, ra_ref, rb_ref, ca_ref, cb_ref,
    xi_ref, ci_ref, oi_ref, yi_ref, q1i_ref, q2i_ref, zi_ref, ti_ref,
    x2_ref, y2_ref,
    side_ref, qs_ref, ys_ref, c_ref, q1_ref, q2_ref, tab_ref, t_ref, p_ref, a_ref, l_ref, f_ref,
    z_ref, xb_ref, x1_ref,
):
    top_ok, bot_ok, left_ok, right_ok = flags()
    place = places()
    odd_row, odd_col = parities()
    top, bot = sides(ra_ref, rb_ref, odd_row)
    before, after = sides(ca_ref, cb_ref, odd_col)
    lf0, lf1, rt0, rt1 = before(0), before(1), after(0), after(1)
    lane = iota((1, 128), 1)
    total = jnp.full((1, 128), -1.0, F32)
    for r in range(3):
        total = jnp.where(lane == 8 * r, lf1[r : r + 1, 18:19], total)
        total = jnp.where(lane == 8 * r + 5, rt1[r : r + 1, 112:113], total)
    select_tables(table_ref, total, tab_ref)
    build_taps(tab_ref, t_ref, [8 * r + p for r in range(3) for p in (0, 5)])

    def taps(seg, patch):
        if 0 <= patch < 4:
            return ti_ref[4 * seg + patch]
        return t_ref[2 * seg + (patch == 4)]

    rr = iota((256, 128), 0)
    rows_ok = ((rr >= 64) | top_ok) & ((rr < 192) | bot_ok)
    shape = (256, 128)
    part = jnp.where(between(shape, 16, 80), lf0, 0.0)
    part += jnp.where(between(shape, 64, 80), lanes(lf1, 80), 0.0)
    side_ref[0, 0:256] = xi_ref[0:256, 0:128] + jnp.where(rows_ok & left_ok, part, 0.0)
    part = jnp.where(between(shape, 80, 128), rt0, 0.0)
    part += jnp.where(between(shape, 80, 96), lanes(rt1, 48), 0.0)
    side_ref[1, 0:256] = xi_ref[0:256, 512:640] + jnp.where(rows_ok & right_ok, part, 0.0)
    part = jnp.where(between(shape, 0, 16), rt0, 0.0)
    side_ref[2, 0:256] = xi_ref[0:256, 640:768] + jnp.where(rows_ok & right_ok, part, 0.0)
    side_ref[:, 256:272] = jnp.zeros((3, 16, 128), F32)
    shape = (192, 128)
    for comp, ref in enumerate((q1i_ref, q2i_ref)):
        part = lanes(lf1[0:192], 96 * comp)
        part += jnp.where(between(shape, 79, 80), lanes(lf1[0:192], 63 - comp), 0.0)
        qs_ref[comp, 0] = jnp.where(between(shape, 48, 80), part, ref[:, 0:128])
        part = lanes(rt1[0:192], 80 * comp)
        qs_ref[comp, 1] = jnp.where(between(shape, 80, 112), part, ref[:, 512:640])
    shape = (224, 128)
    part = lanes(lf0[0:224], 64) + jnp.where(between(shape, 48, 64), lanes(lf1[0:224], 48), 0.0)
    c_first = jnp.where(between(shape, 16, 64), part, ci_ref[:, 0:128])
    part = lanes(rt0[0:224], 48) + jnp.where(between(shape, 64, 80), rt1[0:224], 0.0)
    c_last = jnp.where(between(shape, 64, 112), part, ci_ref[:, 512:640])
    shape = (160, 128)
    o_first = jnp.where(between(shape, 48, 64), lanes(lf0[0:160], 48), oi_ref[:, 0:128])
    o_last = jnp.where(between(shape, 64, 80), rt0[0:160], oi_ref[:, 512:640])
    row_ok, col_ok = masks()

    def get_side(tile, first):
        which = {0: 0, 4: 1, 5: 2}[tile]
        return side_ref[which, first : first + 256]

    def put_side(seg, first, size, tile, blurred):
        c = (c_first if tile == 0 else c_last)[first : first + size]
        new = (c + SIGMA * blurred) / (1.0 + SIGMA)
        new = jnp.where(col_ok(tile, size) & row_ok(seg), new, 0.0)
        old = yi_ref[first : first + size, 128 * tile : 128 * tile + 128]
        inner = between((size, 128), 96, 128) if tile == 0 else between((size, 128), 0, 32)
        ys_ref[tile // 4, first : first + size] = jnp.where(inner, old, new)

    def get_side_y(first, size, tile):
        return ys_ref[tile // 4, first : first + size]

    windows(get_side, p_ref, (0, 1, 2, 17, 18, 19), 256)
    blur(SEGS1, OUTER, taps, p_ref, a_ref, put_side)

    def get_x(start, count):
        at = slice(32 + start, 32 + start + count)
        return jnp.concatenate([side_ref[0, at], xi_ref[at, 128:512], side_ref[1, at]], axis=1)

    def get_q(comp, start):
        at = slice(start, start + 16)
        ref = q2i_ref if comp else q1i_ref
        return jnp.concatenate([qs_ref[comp, 0, at], ref[at, 128:512], qs_ref[comp, 1, at]], axis=1)

    total_variation(get_x, get_q, q1_ref, q2_ref, range(12), place)
    z_ref[...] = zi_ref[...]
    adjoint(SEGS1, OUTER, taps, get_side_y, l_ref, f_ref, z_ref)
    lane = iota((16, WIDE), 1)
    inside = ((lane >= XO) | left_ok) & ((lane < XO + COLS) | right_ok)
    for chunk in range(12):
        start = 16 * chunk
        ext = slice(32 + start, 48 + start)
        x = get_x(start, 16)
        new = x - TAU * (z_ref[ext, 0:WIDE] - divergence(q1_ref, q2_ref, start, place))
        keep = inside & (top_ok if chunk < 2 else bot_ok) if chunk < 2 or chunk >= 10 else inside
        xb_ref[start : start + 16, 0:WIDE] = jnp.where(keep, 2.0 * new - x, 0.0)
        if 2 <= chunk < 10:
            x1_ref[start - 32 : start - 16] = new
    xb_ref[192:208, 0:WIDE] = jnp.zeros((16, WIDE), F32)
    xb_ref[:, WIDE:FULL] = jnp.zeros((208, FULL - WIDE), F32)
    c_ref[:, 0:128] = ys_ref[0, 32:192] - SIGMA * o_first
    c_ref[:, 128:512] = yi_ref[32:192, 128:512] - SIGMA * oi_ref[:, 128:512]
    c_ref[:, 512:640] = ys_ref[1, 32:192] - SIGMA * o_last

    def get_xb(tile, first):
        return xb_ref[first : first + 192, 128 * tile : 128 * tile + 128]

    def put(seg, first, size, tile, blurred):
        here = slice(128 * tile, 128 * tile + 128)
        new = (c_ref[first : first + size, here] + SIGMA * blurred) / (1.0 + SIGMA)
        c_ref[first : first + size, here] = jnp.where(col_ok(tile, size) & row_ok(seg), new, 0.0)

    def get_y(first, size, tile):
        return c_ref[first : first + size, 128 * tile : 128 * tile + 128]

    windows(get_xb, p_ref, range(1, 19), 192)
    blur(SEGS2, ALL, taps, p_ref, a_ref, put)
    total_variation(
        lambda start, count: xb_ref[start : start + count, 0:WIDE],
        lambda comp, start: (q2_ref if comp else q1_ref)[start : start + 16],
        q1_ref, q2_ref, range(1, 10), place,
    )
    z_ref[...] = jnp.zeros_like(z_ref)
    adjoint(SEGS2, ALL, taps, get_y, l_ref, f_ref, z_ref)
    for chunk in range(8):
        span = slice(16 * chunk, 16 * chunk + 16)
        ext = slice(32 + 16 * chunk, 48 + 16 * chunk)
        div = divergence(q1_ref, q2_ref, 32 + 16 * chunk, place)
        new = x1_ref[span] - TAU * (z_ref[ext, 0:WIDE] - div)
        x2_ref[span] = lanes(new, -XO)[:, :COLS]
        y2_ref[span] = lanes(c_ref[16 + 16 * chunk : 32 + 16 * chunk], -YO)[:, :COLS]


def field(*shape, dtype=F32):
    return jax.ShapeDtypeStruct(shape, dtype)


def call(kernel, outs, scratch, *args, name, room=4, far=0, flops=0):
    spaces = [pltpu.HBM] * far + [pltpu.VMEM] * (len(args) - far)
    return pl.pallas_call(
        kernel,
        out_shape=outs,
        in_specs=[pl.BlockSpec(memory_space=space) for space in spaces],
        scratch_shapes=scratch,
        compiler_params=pltpu.CompilerParams(vmem_limit_bytes=room * 1024 * 1024),
        cost_estimate=pl.CostEstimate(flops=flops, bytes_accessed=0, transcendentals=0)
        if flops
        else None,
        name=name,
    )(*args)


def swap(block, axis, first):
    count = lax.axis_size(axis)
    pairs = [(i % count, (i + 1) % count) for i in range(first, count + first, 2)]
    return lax.ppermute(block, axis, pairs + [(b, a) for a, b in pairs])


def per_device(observed, psf_table, psf_index, start_image, blur_dual, tv_dual):
    own = (start_image, blur_dual, observed, tv_dual)
    block = pltpu.VMEM((ROWS, COLS), F32)
    strip = field(STRIP, COLS, dtype=BF16)
    side = field(2, 256, 128, dtype=BF16)
    a, b = call(
        pack_rows_kernel, (strip, strip),
        [block, block, block, pltpu.VMEM((2, ROWS, COLS), F32), pltpu.SemaphoreType.DMA((4,))],
        *own, psf_index, name="pack_rows", far=4, room=62,
    )
    ra = swap(a, "row", 0)
    rb = swap(b, "row", 1)
    table = psf_table.astype(F32)
    normed = (table / jnp.sum(table, axis=(1, 2), keepdims=True)).astype(BF16)
    normed = jnp.pad(normed[:, :, ::-1], ((0, 0), (1, 0), (0, 1))).reshape(64, 1024)
    a, b = call(
        pack_cols_kernel, (side, side), [], *own, psf_index, ra, rb, name="pack_cols"
    )
    ca = swap(a, "col", 0)
    cb = swap(b, "col", 1)
    work = [
        pltpu.VMEM((20, 256, 128), BF16), pltpu.VMEM((20, 144, 128), F32),
        pltpu.VMEM((20, 144, 256), BF16), pltpu.VMEM((20, 160, 128), F32),
    ]
    wide = field(192, WIDE)
    ready = call(
        middle_kernel,
        (
            field(272, FULL), field(224, WIDE), field(160, WIDE), field(224, WIDE), wide, wide,
            field(272, FULL), field(12, 256, 256, dtype=BF16),
        ),
        [pltpu.VMEM((24, 1024), F32)] + work,
        *own, psf_index, normed, ra, rb, name="middle", room=16, flops=1 << 33,
    )
    return call(
        main_kernel,
        (field(ROWS, COLS), field(ROWS, COLS)),
        [
            pltpu.VMEM((3, 272, 128), F32), pltpu.VMEM((2, 2, 192, 128), F32),
            pltpu.VMEM((2, 224, 128), F32), pltpu.VMEM((160, WIDE), F32),
            pltpu.VMEM((192, WIDE), F32), pltpu.VMEM((192, WIDE), F32),
            pltpu.VMEM((24, 1024), F32), pltpu.VMEM((6, 256, 256), BF16),
        ] + work + [
            pltpu.VMEM((272, FULL), F32), pltpu.VMEM((208, FULL), F32), pltpu.VMEM((ROWS, WIDE), F32),
        ],
        psf_index, normed, ra, rb, ca, cb, *ready, name="main", room=20,
    )


def solution(mesh):
    placed = (
        P("row", "col"),
        P(),
        P("row", "col"),
        P("row", "col"),
        P("row", "col"),
        P(None, "row", "col"),
    )
    return jax.shard_map(
        per_device,
        mesh=mesh,
        in_specs=placed,
        out_specs=(P("row", "col"), P("row", "col")),
        check_vma=False,
    )
```

time: 39.1 us -> 34.9 us (0.89)
  the two profiles are of different devices: /device:TPU:25 before, /device:TPU:0 now
where the time goes in v5:
time: 34.9 us; the launch traced here: 34.7 us
  Pallas kernels  18.9 us (54%)
  starting transfers between devices  10.9 us (31%)
  waiting for transfers between devices  2.53 us (7%)
  other arithmetic  1.15 us (3%)
  between operations  0.78 us (2%)
  local copies, waits for them, and re-layouts  0.41 us (1%)
    pallas_call x4, Pallas kernels, call(): pl.pallas_call(kernel, out_shape=outs, in_specs=[pl.BlockSpec(memory_spac...  18.9 us
    ppermute x4, starting transfers between devices, swap(): return lax.ppermute(block, axis, pairs + [(b, a) for a, b in pairs])  10.9 us
    ppermute x4, waiting for transfers between devices, swap(): return lax.ppermute(block, axis, pairs + [(b, a) for a, b in pairs])  2.53 us
    reduce_sum x1, other arithmetic, per_device(): normed = (table / jnp.sum(table, axis=(1, 2), keepdims=True)).astype(BF16)  1.09 us
  transfers between devices with their start and end apart: 4, of which 1 were waited for; matrix products, arithmetic and copies ran while one was open for 4% of the time, Pallas kernels for 18%

profile of v5, /device:TPU:0, one launch (start us, length us, event | category | flops | bytes accessed | tf_op | source)
XLA Modules:
  0.0 34.7 jit_solution(9486502747618779967)
XLA Ops:
  0.6 0.0 copy-start.4
  0.6 0.0 copy-start
  0.7 0.0 copy-start.2
  0.7 0.0 copy-start.1
  0.7 0.0 copy-start.3
  0.7 0.0 copy-start.5
  0.7 2.9 %pack_rows.1 = (bf16[240,512]{1,0:T(8,128)(2,1)}, bf16[240,512]{1,0:T(8,128)(2,1)}) custom-call(f32[128,512]{1,0:T(8,128)} %x_ref.3, f32[128,512]{1,0:T(8,128)} %y_ref.3, f32[128,512]{1,0:T(8,128)} %o_ref.3, f32[2,128,512]{2,1,0:T(8,128)} %q_ref.3, s32[1,4]{1,0:T(1,128)} %idx_ref.7), custom_call_target="tpu_custom_call" | custom-call | tf_op jit(solution)/shard_map/pack_rows/pallas_call | solution.py:634
  3.6 0.1 collective-permute-start
  3.7 6.5 %collective-permute-start.1 = (bf16[240,512]{1,0:T(8,128)(2,1)}, bf16[240,512]{1,0:T(8,128)(2,1)S(1)}, u32[]{:S(2)}, u32[]{:S(2)}) collective-permute-start(bf16[240,512]{1,0:T(8,128)(2,1)} %get-tuple-element.15), channel_id=1, source_target_pairs={{8,16},{24,32},{40,48},{56,64},{72,80},{88,96},{104,112},{120,0},{... | collective-permute-start | bytes 737288 | tf_op jit(solution)/shard_map/ppermute | solution.py:650
  10.2 1.1 %convert_reduce_fusion = f32[64]{0:T(128)S(1)} fusion(bf16[64,31,31]{0,2,1:T(8,128)(2,1)} %param.7), kind=kLoop, calls=%fused_computation.1 | loop fusion | flops 122944 | bytes 123264 | tf_op jit(solution)/shard_map/reduce_sum | solution.py:666
  11.3 0.0 copy-done.5
  11.3 0.1 fusion
  11.4 0.2 rev.3
  11.6 0.1 pad.4
  11.7 0.1 copy.10.table_ref
  11.8 0.0 collective-permute-done.ra_ref
  11.8 2.5 %collective-permute-done.1.rb_ref = bf16[240,512]{1,0:T(8,128)(2,1)S(1)} collective-permute-done((bf16[240,512]{1,0:T(8,128)(2,1)}, bf16[240,512]{1,0:T(8,128)(2,1)S(1)}, u32[]{:S(2)}, u32[]{:S(2)}) %collective-permute-start.1) | collective-permute-done | bytes 245792 | tf_op jit(solution)/shard_map/ppermute | solution.py:650
  14.3 0.0 copy-done.4
  14.3 0.0 copy-done
  14.3 0.0 copy-done.2
  14.3 0.0 copy-done.1
  14.3 0.0 copy-done.3
  14.3 0.4 %pack_cols.1 = (bf16[2,256,128]{2,1,0:T(8,128)(2,1)S(1)}, bf16[2,256,128]{2,1,0:T(8,128)(2,1)S(1)}) custom-call(f32[128,512]{1,0:T(8,128)S(1)} %copy-done.1, f32[128,512]{1,0:T(8,128)S(1)} %copy-done.2, f32[128,512]{1,0:T(8,128)S(1)} %copy-done.3, f32[2,128,512]{2,1,0:T(8,128)S(1)} %copy-done, s32[1,4]{1,0:T(1,128)S(1)} %copy-done.4, ...), custom_call_target="tpu_custom_call" | custom-call | tf_op jit(solution)/shard_map/pack_cols/pallas_call | solution.py:634
  14.7 1.1 %collective-permute-start.2 = (bf16[2,256,128]{2,1,0:T(8,128)(2,1)S(1)}, bf16[2,256,128]{2,1,0:T(8,128)(2,1)S(1)}, u32[]{:S(2)}, u32[]{:S(2)}) collective-permute-start(bf16[2,256,128]{2,1,0:T(8,128)(2,1)S(1)} %get-tuple-element.16), channel_id=1, source_target_pairs={{0,1},{2,3},{4,5},{6,7},{1,0},{3,2},{5,4},{7,6},{8,9},{10,11},{12,... | collective-permute-start | bytes 393224 | tf_op jit(solution)/shard_map/ppermute | solution.py:650
  15.8 3.2 %collective-permute-start.3 = (bf16[2,256,128]{2,1,0:T(8,128)(2,1)S(1)}, bf16[2,256,128]{2,1,0:T(8,128)(2,1)S(1)}, u32[]{:S(2)}, u32[]{:S(2)}) collective-permute-start(bf16[2,256,128]{2,1,0:T(8,128)(2,1)S(1)} %get-tuple-element.17), channel_id=1, source_target_pairs={{1,2},{3,4},{5,6},{7,0},{2,1},{4,3},{6,5},{0,7},{9,10},{11,12},{13... | collective-permute-start | bytes 393224 | tf_op jit(solution)/shard_map/ppermute | solution.py:650
  19.0 6.2 %middle.1 = (f32[272,768]{1,0:T(8,128)S(1)}, f32[224,640]{1,0:T(8,128)S(1)}, f32[160,640]{1,0:T(8,128)S(1)}, f32[224,640]{1,0:T(8,128)S(1)}, f32[192,640]{1,0:T(...) custom-call(f32[128,512]{1,0:T(8,128)S(1)} %copy-done.1, ...), custom_call_target="tpu_custom_call" | custom-call | flops 8589934592 | tf_op jit(solution)/shard_map/middle/pallas_call | solution.py:634
  25.2 0.0 collective-permute-done.2.ca_ref
  25.2 0.0 collective-permute-done.3.cb_ref
  25.2 9.4 %main.1 = (f32[128,512]{1,0:T(8,128)}, f32[128,512]{1,0:T(8,128)}) custom-call(s32[1,4]{1,0:T(1,128)S(1)} %copy-done.4, bf16[64,1024]{1,0:T(8,128)(2,1)S(1)} %copy.10.table_ref, bf16[240,512]{1,0:T(8,128)(2,1)S(1)} %collective-permute-done.ra_ref, bf16[240,512]{1,0:T(8,128)(2,1)S(1)} %collective-permute-done.1.rb_ref, ...), custom_call_target="tpu_custom_call" | custom-call | tf_op jit(solution)/shard_map/main/pallas_call | solution.py:634
Async XLA Ops:
  0.6 13.7 %copy-start.4 = (s32[1,4]{1,0:T(1,128)S(1)}, s32[1,4]{1,0:T(1,128)}, u32[]{:S(2)}) copy-start(s32[1,4]{1,0:T(1,128)} %idx_ref.7) | copy-start | bytes 52
  0.6 13.7 %copy-start = (f32[2,128,512]{2,1,0:T(8,128)S(1)}, f32[2,128,512]{2,1,0:T(8,128)}, u32[]{:S(2)}) copy-start(f32[2,128,512]{2,1,0:T(8,128)} %q_ref.3) | copy-start | bytes 1572868
  0.7 13.7 %copy-start.2 = (f32[128,512]{1,0:T(8,128)S(1)}, f32[128,512]{1,0:T(8,128)}, u32[]{:S(2)}) copy-start(f32[128,512]{1,0:T(8,128)} %y_ref.3) | copy-start | bytes 786436
  0.7 13.7 %copy-start.1 = (f32[128,512]{1,0:T(8,128)S(1)}, f32[128,512]{1,0:T(8,128)}, u32[]{:S(2)}) copy-start(f32[128,512]{1,0:T(8,128)} %x_ref.3) | copy-start | bytes 786436
  0.7 13.7 %copy-start.3 = (f32[128,512]{1,0:T(8,128)S(1)}, f32[128,512]{1,0:T(8,128)}, u32[]{:S(2)}) copy-start(f32[128,512]{1,0:T(8,128)} %o_ref.3) | copy-start | bytes 786436
  0.7 10.6 %copy-start.5 = (bf16[64,31,31]{0,2,1:T(8,128)(2,1)S(1)}, bf16[64,31,31]{0,2,1:T(8,128)(2,1)}, u32[]{:S(2)}) copy-start(bf16[64,31,31]{0,2,1:T(8,128)(2,1)} %param.7) | copy-start | bytes 369028
  3.6 8.2 %collective-permute-start = (bf16[240,512]{1,0:T(8,128)(2,1)}, bf16[240,512]{1,0:T(8,128)(2,1)S(1)}, u32[]{:S(2)}, u32[]{:S(2)}) collective-permute-start(bf16[240,512]{1,0:T(8,128)(2,1)} %get-tuple-element.14), channel_id=1, source_target_pairs={{0,8},{16,24},{32,40},{48,56},{64,72},{80,88},{96,104},{112,120},{... | collective-permute-start | bytes 737288 | tf_op jit(solution)/shard_map/ppermute | solution.py:650
  3.7 10.6 %collective-permute-start.1 = (bf16[240,512]{1,0:T(8,128)(2,1)}, bf16[240,512]{1,0:T(8,128)(2,1)S(1)}, u32[]{:S(2)}, u32[]{:S(2)}) collective-permute-start(bf16[240,512]{1,0:T(8,128)(2,1)} %get-tuple-element.15), channel_id=1, source_target_pairs={{8,16},{24,32},{40,48},{56,64},{72,80},{88,96},{104,112},{120,0},{... | collective-permute-start | bytes 737288 | tf_op jit(solution)/shard_map/ppermute | solution.py:650
  14.7 10.5 %collective-permute-start.2 = (bf16[2,256,128]{2,1,0:T(8,128)(2,1)S(1)}, bf16[2,256,128]{2,1,0:T(8,128)(2,1)S(1)}, u32[]{:S(2)}, u32[]{:S(2)}) collective-permute-start(bf16[2,256,128]{2,1,0:T(8,128)(2,1)S(1)} %get-tuple-element.16), channel_id=1, source_target_pairs={{0,1},{2,3},{4,5},{6,7},{1,0},{3,2},{5,4},{7,6},{8,9},{10,11},{12,... | collective-permute-start | bytes 393224 | tf_op jit(solution)/shard_map/ppermute | solution.py:650
  15.8 9.4 %collective-permute-start.3 = (bf16[2,256,128]{2,1,0:T(8,128)(2,1)S(1)}, bf16[2,256,128]{2,1,0:T(8,128)(2,1)S(1)}, u32[]{:S(2)}, u32[]{:S(2)}) collective-permute-start(bf16[2,256,128]{2,1,0:T(8,128)(2,1)S(1)} %get-tuple-element.17), channel_id=1, source_target_pairs={{1,2},{3,4},{5,6},{7,0},{2,1},{4,3},{6,5},{0,7},{9,10},{11,12},{13... | collective-permute-start | bytes 393224 | tf_op jit(solution)/shard_map/ppermute | solution.py:650

commit v6 on v5

--- a/solution.py
+++ b/solution.py
@@ -426,8 +426,23 @@
     return value[:, 128 * tile : 128 * tile + 128]
 
 
+def local_kernel(
+    x_ref, y_ref, o_ref, q_ref, idx_ref, table_ref,
+    xw_ref, cw_ref, ow_ref, q1w_ref, q2w_ref, t_ref,
+    tab_ref,
+):
+    select_tables(table_ref, index_line(idx_ref, 128), tab_ref)
+    build_taps(tab_ref, t_ref, range(1, 5))
+    xw_ref[...] = widen(x_ref[...], XO, FULL)
+    seen = o_ref[...]
+    cw_ref[...] = widen(y_ref[...] - SIGMA * seen, YO)
+    ow_ref[...] = widen(seen, YO)
+    q1w_ref[...] = widen(q_ref[0], XO)
+    q2w_ref[...] = widen(q_ref[1], XO)
+
+
 def middle_kernel(
-    x_ref, y_ref, o_ref, q_ref, idx_ref, table_ref, ra_ref, rb_ref,
+    xw_ref, cw_ref, ow_ref, q1w_ref, q2w_ref, own_ref, table_ref, ra_ref, rb_ref,
     xe_ref, c_ref, ob_ref, ys_ref, q1_ref, q2_ref, z_ref, t_ref,
     tab_ref, p_ref, a_ref, l_ref, f_ref,
 ):
@@ -436,14 +451,10 @@
     top, bot = sides(ra_ref, rb_ref, odd)
     misc = slice(SM, SM + 16)
     lane = iota((1, 128), 1)
-    lines = (
-        top((misc, slice(0, 128)))[2:3], index_line(idx_ref, 128), bot((misc, slice(0, 128)))[2:3],
-    )
-    total = jnp.full((1, 128), -1.0, F32)
-    for r in range(3):
-        total = jnp.where((lane >= 8 * r) & (lane < 8 * r + 6), lanes(lines[r], 8 * r), total)
-    select_tables(table_ref, total, tab_ref)
-    build_taps(tab_ref, t_ref, [8 * r + 1 + p for r in range(3) for p in range(4)])
+    upper = top((misc, slice(0, 128)))[2:3]
+    lower = bot((misc, slice(0, 128)))[2:3]
+    select_tables(table_ref, jnp.where(lane < 8, upper, lanes(lower, 8)), tab_ref)
+    build_taps(tab_ref, t_ref, [1, 2, 3, 4, 9, 10, 11, 12])
 
     def part(read, at, count):
         return read(slice(at, at + count))
@@ -452,12 +463,11 @@
     above = part(top, SX, 64) + jnp.concatenate([zero, part(top, SXL, 16)], axis=0)
     below = part(bot, SX, 64) + jnp.concatenate([part(bot, SXL, 16), zero], axis=0)
     xe_ref[0:64] = widen(jnp.where(top_ok, above, 0.0), XO, FULL)
-    xe_ref[64:192] = widen(x_ref[...], XO, FULL)
+    xe_ref[64:192] = xw_ref[...]
     xe_ref[192:256] = widen(jnp.where(bot_ok, below, 0.0), XO, FULL)
     xe_ref[256:272] = jnp.zeros((16, FULL), F32)
-    seen = o_ref[...]
-    c_ref[48:176] = widen(y_ref[...] - SIGMA * seen, YO)
-    ob_ref[16:144] = widen(seen, YO)
+    c_ref[48:176] = cw_ref[...]
+    ob_ref[16:144] = ow_ref[...]
     zero = jnp.zeros((32, COLS), F32)
     above = part(top, SC, 48) + jnp.concatenate([zero, part(top, SCL, 16)], axis=0)
     below = part(bot, SC, 48) + jnp.concatenate([part(bot, SCL, 16), zero], axis=0)
@@ -467,15 +477,15 @@
     ob_ref[144:160] = widen(part(bot, SO, 16), YO)
     rix = iota((32, COLS), 0)
     rest = top(misc)
-    for comp, (ref, section) in enumerate(((q1_ref, S1), (q2_ref, S2))):
+    for comp, (ref, section, own) in enumerate(((q1_ref, S1, q1w_ref), (q2_ref, S2, q2w_ref))):
         above = part(top, section, 32) + jnp.where(rix == 31, rest[comp : comp + 1], 0.0)
         ref[0:32] = widen(above, XO)
-        ref[32:160] = widen(q_ref[comp], XO)
+        ref[32:160] = own[...]
         ref[160:192] = widen(part(bot, section, 32), XO)
     row_ok, _ = masks()
 
     def taps(seg, patch):
-        return t_ref[4 * seg + patch]
+        return own_ref[patch] if seg == 1 else t_ref[2 * seg + patch]
 
     def get_x(tile, first):
         return xe_ref[first : first + 256, 128 * tile : 128 * tile + 128]
@@ -495,16 +505,15 @@
 
 
 def main_kernel(
-    idx_ref, table_ref, ra_ref, rb_ref, ca_ref, cb_ref,
-    xi_ref, ci_ref, oi_ref, yi_ref, q1i_ref, q2i_ref, zi_ref, ti_ref,
+    table_ref, ca_ref, cb_ref,
+    xi_ref, ci_ref, oi_ref, yi_ref, q1i_ref, q2i_ref, zi_ref, ti_ref, own_ref,
     x2_ref, y2_ref,
     side_ref, qs_ref, ys_ref, c_ref, q1_ref, q2_ref, tab_ref, t_ref, p_ref, a_ref, l_ref, f_ref,
     z_ref, xb_ref, x1_ref,
 ):
     top_ok, bot_ok, left_ok, right_ok = flags()
     place = places()
-    odd_row, odd_col = parities()
-    top, bot = sides(ra_ref, rb_ref, odd_row)
+    _, odd_col = parities()
     before, after = sides(ca_ref, cb_ref, odd_col)
     lf0, lf1, rt0, rt1 = before(0), before(1), after(0), after(1)
     lane = iota((1, 128), 1)
@@ -517,7 +526,7 @@
 
     def taps(seg, patch):
         if 0 <= patch < 4:
-            return ti_ref[4 * seg + patch]
+            return own_ref[patch] if seg == 1 else ti_ref[2 * seg + patch]
         return t_ref[2 * seg + (patch == 4)]
 
     rr = iota((256, 128), 0)
@@ -645,9 +654,21 @@
 
 
 def swap(block, axis, first):
-    count = lax.axis_size(axis)
-    pairs = [(i % count, (i + 1) % count) for i in range(first, count + first, 2)]
-    return lax.ppermute(block, axis, pairs + [(b, a) for a, b in pairs])
+    high, wide = lax.axis_size("row"), lax.axis_size("col")
+
+    def partner(row, col):
+        if axis == "row":
+            to = ((row - first) ^ 1) + first
+            return (to, col) if 0 <= to < high else (row, col ^ 2 if wide > 2 else col ^ 1)
+        to = ((col - first) ^ 1) + first
+        return (row, to) if 0 <= to < wide else (row ^ 1, col)
+
+    pairs = []
+    for row in range(high):
+        for col in range(wide):
+            to_row, to_col = partner(row, col)
+            pairs.append((row * wide + col, to_row * wide + to_col))
+    return lax.ppermute(block, ("row", "col"), pairs)
 
 
 def per_device(observed, psf_table, psf_index, start_image, blur_dual, tv_dual):
@@ -675,14 +696,21 @@
         pltpu.VMEM((20, 144, 256), BF16), pltpu.VMEM((20, 160, 128), F32),
     ]
     wide = field(192, WIDE)
+    local = field(ROWS, WIDE)
+    *fields, taps = call(
+        local_kernel,
+        (field(ROWS, FULL), local, local, local, local, field(4, 256, 256, dtype=BF16)),
+        [pltpu.VMEM((24, 1024), F32)],
+        *own, psf_index, normed, name="local", room=4, flops=1 << 32,
+    )
     ready = call(
         middle_kernel,
         (
             field(272, FULL), field(224, WIDE), field(160, WIDE), field(224, WIDE), wide, wide,
-            field(272, FULL), field(12, 256, 256, dtype=BF16),
+            field(272, FULL), field(8, 256, 256, dtype=BF16),
         ),
         [pltpu.VMEM((24, 1024), F32)] + work,
-        *own, psf_index, normed, ra, rb, name="middle", room=16, flops=1 << 33,
+        *fields, taps, normed, ra, rb, name="middle", room=16, flops=1 << 33,
     )
     return call(
         main_kernel,
@@ -695,7 +723,7 @@
         ] + work + [
             pltpu.VMEM((272, FULL), F32), pltpu.VMEM((208, FULL), F32), pltpu.VMEM((ROWS, WIDE), F32),
         ],
-        psf_index, normed, ra, rb, ca, cb, *ready, name="main", room=20,
+        normed, ca, cb, *ready, taps, name="main", room=20,
     )
 
 

time: 34.9 us -> 31.6 us (0.905)
  the two profiles are of different devices: /device:TPU:0 before, /device:TPU:96 now
where the time goes in v6:
time: 31.6 us; the launch traced here: 31.4 us
  Pallas kernels  18.8 us (59%)
  starting transfers between devices  6.22 us (20%)
  waiting for transfers between devices  4.14 us (13%)
  local copies, waits for them, and re-layouts  1.33 us (4%)
  between operations  0.77 us (2%)
    pallas_call x5, Pallas kernels, call(): pl.pallas_call(kernel, out_shape=outs, in_specs=[pl.BlockSpec(memory_spac...  18.8 us
    ppermute x4, starting transfers between devices, swap(): return lax.ppermute(block, ('row', 'col'), pairs)  6.22 us
    ppermute x4, waiting for transfers between devices, swap(): return lax.ppermute(block, ('row', 'col'), pairs)  4.14 us
    unnamed x12, local copies, waits for them, and re-layouts  0.94 us
  transfers between devices with their start and end apart: 4, of which 1 were waited for; matrix products, arithmetic and copies ran while one was open for 2% of the time, Pallas kernels for 20%

profile of v6, /device:TPU:96, one launch (start us, length us, event | category | flops | bytes accessed | tf_op | source)
XLA Modules:
  0.0 31.4 jit_solution(15412525243403928032)
XLA Ops:
  0.6 0.0 copy-start.5
  0.6 2.8 %pack_rows.1 = (bf16[240,512]{1,0:T(8,128)(2,1)}, bf16[240,512]{1,0:T(8,128)(2,1)}) custom-call(f32[128,512]{1,0:T(8,128)} %x_ref.3, f32[128,512]{1,0:T(8,128)} %y_ref.3, f32[128,512]{1,0:T(8,128)} %o_ref.3, f32[2,128,512]{2,1,0:T(8,128)} %q_ref.3, s32[1,4]{1,0:T(1,128)} %idx_ref.5), custom_call_target="tpu_custom_call" | custom-call | tf_op jit(solution)/shard_map/pack_rows/pallas_call | solution.py:643
  3.5 0.1 collective-permute-start
  3.6 3.1 %collective-permute-start.1 = (bf16[240,512]{1,0:T(8,128)(2,1)}, bf16[240,512]{1,0:T(8,128)(2,1)S(1)}, u32[]{:S(2)}, u32[]{:S(2)}) collective-permute-start(bf16[240,512]{1,0:T(8,128)(2,1)} %get-tuple-element.21), channel_id=1, source_target_pairs={{0,2},{1,3},{2,0},{3,1},{4,6},{5,7},{6,4},{7,5},{8,16},{9,17},{10,... | collective-permute-start | bytes 737288 | tf_op jit(solution)/shard_map/ppermute | solution.py:671
  6.7 0.0 copy-done.5
  6.7 0.1 convert_reduce_fusion
  6.8 0.1 fusion
  6.9 0.0 copy-start.2
  6.9 0.0 copy-start.3
  6.9 0.2 rev.3
  7.1 0.0 copy-start
  7.1 0.1 pad.4
  7.2 0.0 copy-start.1
  7.2 0.0 copy-start.4
  7.2 0.1 copy.11.table_ref
  7.3 0.5 %copy-done.2 = f32[128,512]{1,0:T(8,128)S(1)} copy-done((f32[128,512]{1,0:T(8,128)S(1)}, f32[128,512]{1,0:T(8,128)}, u32[]{:S(2)}) %copy-start.2) | copy-done | bytes 262168
  7.8 0.1 copy-done.3
  7.9 0.3 copy-done
  8.2 0.1 copy-done.1
  8.3 0.0 copy-done.4
  8.3 0.8 %local.1 = (f32[128,768]{1,0:T(8,128)S(1)}, f32[128,640]{1,0:T(8,128)S(1)}, f32[128,640]{1,0:T(8,128)S(1)}, f32[128,640]{1,0:T(8,128)S(1)}, f32[128,640]{1,0:T(8,128)S(1)}, /*index=5*/bf16[4,256,256]{2,1,0:T(8,128)(2,1)S(1)}) custom-call(f32[128,512]{1,0:T(8,128)S(1)} %copy-done.1, f32[128,512]{1,0:T(8,128)S(1)} %copy-done.2, f32[128,512]{1,0:T(8,128)S(1)} %copy-done.3, ...), custom_call_target="tpu_custom_call" | custom-call | flops 4294967296 | tf_op jit(solution)/shard_map/local/pallas_call | solution.py:643
  9.0 0.0 collective-permute-done.ra_ref
  9.1 4.1 %collective-permute-done.1.rb_ref = bf16[240,512]{1,0:T(8,128)(2,1)S(1)} collective-permute-done((bf16[240,512]{1,0:T(8,128)(2,1)}, bf16[240,512]{1,0:T(8,128)(2,1)S(1)}, u32[]{:S(2)}, u32[]{:S(2)}) %collective-permute-start.1) | collective-permute-done | bytes 245792 | tf_op jit(solution)/shard_map/ppermute | solution.py:671
  13.2 0.4 %pack_cols.1 = (bf16[2,256,128]{2,1,0:T(8,128)(2,1)S(1)}, bf16[2,256,128]{2,1,0:T(8,128)(2,1)S(1)}) custom-call(f32[128,512]{1,0:T(8,128)S(1)} %copy-done.1, f32[128,512]{1,0:T(8,128)S(1)} %copy-done.2, f32[128,512]{1,0:T(8,128)S(1)} %copy-done.3, f32[2,128,512]{2,1,0:T(8,128)S(1)} %copy-done, s32[1,4]{1,0:T(1,128)S(1)} %copy-done.4, ...), custom_call_target="tpu_custom_call" | custom-call | tf_op jit(solution)/shard_map/pack_cols/pallas_call | solution.py:643
  13.6 0.4 %collective-permute-start.2 = (bf16[2,256,128]{2,1,0:T(8,128)(2,1)S(1)}, bf16[2,256,128]{2,1,0:T(8,128)(2,1)S(1)}, u32[]{:S(2)}, u32[]{:S(2)}) collective-permute-start(bf16[2,256,128]{2,1,0:T(8,128)(2,1)S(1)} %get-tuple-element.22), channel_id=1, source_target_pairs={{0,1},{1,0},{2,3},{3,2},{4,5},{5,4},{6,7},{7,6},{8,9},{9,8},{10,11... | collective-permute-start | bytes 393224 | tf_op jit(solution)/shard_map/ppermute | solution.py:671
  14.0 2.6 %collective-permute-start.3 = (bf16[2,256,128]{2,1,0:T(8,128)(2,1)S(1)}, bf16[2,256,128]{2,1,0:T(8,128)(2,1)S(1)}, u32[]{:S(2)}, u32[]{:S(2)}) collective-permute-start(bf16[2,256,128]{2,1,0:T(8,128)(2,1)S(1)} %get-tuple-element.23), channel_id=1, source_target_pairs={{0,8},{1,2},{2,1},{3,4},{4,3},{5,6},{6,5},{7,15},{8,0},{9,10},{10,... | collective-permute-start | bytes 393224 | tf_op jit(solution)/shard_map/ppermute | solution.py:671
  16.6 5.5 %middle.1 = (f32[272,768]{1,0:T(8,128)S(1)}, f32[224,640]{1,0:T(8,128)S(1)}, f32[160,640]{1,0:T(8,128)S(1)}, f32[224,640]{1,0:T(8,128)S(1)}, f32[192,640]{1,0:T(...) custom-call(f32[128,768]{1,0:T(8,128)S(1)} %get-tuple-element.24.xw_ref, ...), custom_call_target="tpu_custom_call" | custom-call | flops 8589934592 | tf_op jit(solution)/shard_map/middle/pallas_call | solution.py:643
  22.1 0.0 collective-permute-done.2.ca_ref
  22.1 0.0 collective-permute-done.3.cb_ref
  22.1 9.3 %main.1 = (f32[128,512]{1,0:T(8,128)}, f32[128,512]{1,0:T(8,128)}) custom-call(bf16[64,1024]{1,0:T(8,128)(2,1)S(1)} %copy.11.table_ref, bf16[2,256,128]{2,1,0:T(8,128)(2,1)S(1)} %collective-permute-done.2.ca_ref, bf16[2,256,128]{2,1,0:T(8,128)(2,1)S(1)} %collective-permute-done.3.cb_ref, f32[272,768]{1,0:T(8,128)S(1)} %get-tuple-element.30.xi_ref, ...), custom_call_target="tpu_custom_call" | custom-call | tf_op jit(solution)/shard_map/main/pallas_call | solution.py:643
Async XLA Ops:
  0.6 6.0 %copy-start.5 = (bf16[64,31,31]{0,2,1:T(8,128)(2,1)S(1)}, bf16[64,31,31]{0,2,1:T(8,128)(2,1)}, u32[]{:S(2)}) copy-start(bf16[64,31,31]{0,2,1:T(8,128)(2,1)} %param.7) | copy-start | bytes 369028
  3.5 5.6 %collective-permute-start = (bf16[240,512]{1,0:T(8,128)(2,1)}, bf16[240,512]{1,0:T(8,128)(2,1)S(1)}, u32[]{:S(2)}, u32[]{:S(2)}) collective-permute-start(bf16[240,512]{1,0:T(8,128)(2,1)} %get-tuple-element.20), channel_id=1, source_target_pairs={{0,8},{1,9},{2,10},{3,11},{4,12},{5,13},{6,14},{7,15},{8,0},{9,1},... | collective-permute-start | bytes 737288 | tf_op jit(solution)/shard_map/ppermute | solution.py:671
  3.6 9.6 %collective-permute-start.1 = (bf16[240,512]{1,0:T(8,128)(2,1)}, bf16[240,512]{1,0:T(8,128)(2,1)S(1)}, u32[]{:S(2)}, u32[]{:S(2)}) collective-permute-start(bf16[240,512]{1,0:T(8,128)(2,1)} %get-tuple-element.21), channel_id=1, source_target_pairs={{0,2},{1,3},{2,0},{3,1},{4,6},{5,7},{6,4},{7,5},{8,16},{9,17},{10,... | collective-permute-start | bytes 737288 | tf_op jit(solution)/shard_map/ppermute | solution.py:671
  6.9 1.0 %copy-start.2 = (f32[128,512]{1,0:T(8,128)S(1)}, f32[128,512]{1,0:T(8,128)}, u32[]{:S(2)}) copy-start(f32[128,512]{1,0:T(8,128)} %y_ref.3) | copy-start | bytes 786436
  6.9 1.0 %copy-start.3 = (f32[128,512]{1,0:T(8,128)S(1)}, f32[128,512]{1,0:T(8,128)}, u32[]{:S(2)}) copy-start(f32[128,512]{1,0:T(8,128)} %o_ref.3) | copy-start | bytes 786436
  7.1 1.1 %copy-start = (f32[2,128,512]{2,1,0:T(8,128)S(1)}, f32[2,128,512]{2,1,0:T(8,128)}, u32[]{:S(2)}) copy-start(f32[2,128,512]{2,1,0:T(8,128)} %q_ref.3) | copy-start | bytes 1572868
  7.2 1.1 %copy-start.1 = (f32[128,512]{1,0:T(8,128)S(1)}, f32[128,512]{1,0:T(8,128)}, u32[]{:S(2)}) copy-start(f32[128,512]{1,0:T(8,128)} %x_ref.3) | copy-start | bytes 786436
  7.2 1.1 %copy-start.4 = (s32[1,4]{1,0:T(1,128)S(1)}, s32[1,4]{1,0:T(1,128)}, u32[]{:S(2)}) copy-start(s32[1,4]{1,0:T(1,128)} %idx_ref.5) | copy-start | bytes 52
  13.6 8.5 %collective-permute-start.2 = (bf16[2,256,128]{2,1,0:T(8,128)(2,1)S(1)}, bf16[2,256,128]{2,1,0:T(8,128)(2,1)S(1)}, u32[]{:S(2)}, u32[]{:S(2)}) collective-permute-start(bf16[2,256,128]{2,1,0:T(8,128)(2,1)S(1)} %get-tuple-element.22), channel_id=1, source_target_pairs={{0,1},{1,0},{2,3},{3,2},{4,5},{5,4},{6,7},{7,6},{8,9},{9,8},{10,11... | collective-permute-start | bytes 393224 | tf_op jit(solution)/shard_map/ppermute | solution.py:671
  14.0 8.1 %collective-permute-start.3 = (bf16[2,256,128]{2,1,0:T(8,128)(2,1)S(1)}, bf16[2,256,128]{2,1,0:T(8,128)(2,1)S(1)}, u32[]{:S(2)}, u32[]{:S(2)}) collective-permute-start(bf16[2,256,128]{2,1,0:T(8,128)(2,1)S(1)} %get-tuple-element.23), channel_id=1, source_target_pairs={{0,8},{1,2},{2,1},{3,4},{4,3},{5,6},{6,5},{7,15},{8,0},{9,10},{10,... | collective-permute-start | bytes 393224 | tf_op jit(solution)/shard_map/ppermute | solution.py:671

commit v7 on v6

--- a/solution.py
+++ b/solution.py
@@ -204,7 +204,7 @@
     sub = iota((size, 128), 0)
     bits = [(sub // (1 << n)) % 2 == 1 for n in range(3)]
     for e in range(8):
-        a1, half = e // 2, e % 2
+        a1, half = 2 * (e // 4) + e % 2, e // 2 % 2
         here = slice(128 * half, 128 * half + 128)
         skew = jnp.concatenate(
             [
@@ -231,17 +231,17 @@
     tail = between((count, 128), 96, 128)
     for b in blocks:
         tile, place = b // 4, b % 4
-        x0, x8 = get(tile, 0), get(tile, 8)
+        x0, x4 = get(tile, 0), get(tile, 4)
         if place == 0:
-            part = jnp.where(low, x0, lanes(x8, 64))
+            part = jnp.where(low, x0, lanes(x4, 64))
         elif place == 1:
-            part = jnp.where(low, lanes(x0, 96), lanes(x8, 32))
+            part = jnp.where(low, lanes(x0, 96), lanes(x4, 32))
         elif place == 2:
-            part = jnp.where(low, lanes(x0, 64), x8)
+            part = jnp.where(low, lanes(x0, 64), x4)
         else:
             w0 = jnp.where(tail, x0, get(tile + 1, 0))
-            w8 = jnp.where(tail, x8, get(tile + 1, 8))
-            part = jnp.where(low, lanes(w0, 32), lanes(w8, 96))
+            w4 = jnp.where(tail, x4, get(tile + 1, 4))
+            part = jnp.where(low, lanes(w0, 32), lanes(w4, 96))
         p_ref[b, 0:count] = part.astype(BF16)
 
 
@@ -265,7 +265,7 @@
             v = jnp.dot(lhs, taps(seg, patch), preferred_element_type=F32)
             for place, b in enumerate(blocks):
                 part = v[place * padded : place * padded + padded]
-                a_ref[b, 0:padded] = part[:, :128] + rows(part[:, 128:], -4)
+                a_ref[b, 0:padded] = part[:, :128] + rows(part[:, 128:], -8)
         low = between((padded, 128), 0, 64)
         even = iota((padded, 128), 1) % 64 < 32
         for tile in sorted({b // 4 for b in present}):
@@ -308,7 +308,7 @@
                     else:
                         part = jnp.where(low, lanes(e[p], 64), s)
                     l_ref[b, 0:padded, 0:128] = part.astype(BF16)
-                    l_ref[b, 0:padded, 128:256] = rows(part, 4).astype(BF16)
+                    l_ref[b, 0:padded, 128:256] = rows(part, 8).astype(BF16)
         for patch, blocks in groups:
             lhs = jnp.concatenate([l_ref[b, 0:padded] for b in blocks], axis=0)
             g = lax.dot_general(
@@ -317,20 +317,20 @@
             zero = jnp.zeros((16, 128), F32)
             for place, b in enumerate(blocks):
                 part = g[place * padded : place * padded + padded]
-                f_ref[b, 0 : padded + 16] = jnp.concatenate(
+                f_ref[b, 0:8] = zero[0:8]
+                f_ref[b, 8 : padded + 24] = jnp.concatenate(
                     [part[:, :128], zero], axis=0
                 ) + jnp.concatenate([zero, part[:, 128:]], axis=0)
+                f_ref[b, padded + 24 : padded + 32] = zero[0:8]
         tall = padded + 24
         low = between((tall, 128), 0, 64)
         head = between((tall, 128), 0, 32)
-        pad8 = jnp.zeros((8, 128), F32)
 
         def both_ways(b):
             if b not in present:
                 zero = jnp.zeros((tall, 128), F32)
                 return zero, zero
-            f = f_ref[b, 0 : padded + 16]
-            return jnp.concatenate([f, pad8], axis=0), jnp.concatenate([pad8, f], axis=0)
+            return f_ref[b, 8 : 8 + tall], f_ref[b, 4 : 4 + tall]
 
         for tile in tiles:
             both = []
@@ -346,48 +346,52 @@
             z_ref[span, after] += jnp.where(head, turned, 0.0)
 
 
-def total_variation(get_x, get_q, q1_ref, q2_ref, chunks, place):
-    row0, col0, limit_row, limit_col = place
+def on_tile(value, tile, change):
+    parts = [value[:, 128 * k : 128 * k + 128] for k in range(5)]
+    parts[tile] = change(parts[tile])
+    return jnp.concatenate(parts, axis=1)
+
+
+def unless(bad, value):
+    return jnp.where(bad, 0.0, value)
+
+
+def total_variation(get_x, get_q, q1_ref, q2_ref, chunks):
+    _, bot_ok, _, right_ok = flags()
+    lane = iota((16, 128), 1)
+    past = (lane + 512 - XO >= COLS - 1) & jnp.logical_not(right_ok)
     for chunk in chunks:
         start = 16 * chunk
         tall = get_x(start, 24)
         x = tall[0:16]
-        below = rows(tall, -1)[0:16]
-        right = lanes(x, -1)
-        r = row0 - 32 + start + iota((16, WIDE), 0)
-        c = col0 - XO + iota((16, WIDE), 1)
-        g1 = jnp.where(r < limit_row, below - x, 0.0)
-        g2 = jnp.where(c < limit_col, right - x, 0.0)
+        g1 = rows(tall, -1)[0:16] - x
+        g2 = on_tile(lanes(x, -1) - x, 4, lambda part: unless(past, part))
+        if start + 16 > 31 + ROWS:
+            row = start - 32 + iota((16, WIDE), 0)
+            g1 = unless((row >= ROWS - 1) & jnp.logical_not(bot_ok), g1)
         span = slice(start, start + 16)
         u1 = get_q(0, start) + SIGMA * g1
         u2 = get_q(1, start) + SIGMA * g2
-        shrink = jnp.maximum(1.0, jnp.sqrt(u1 * u1 + u2 * u2) / TV)
-        inv = 1.0 / shrink
-        q1_ref[span] = u1 * inv
-        q2_ref[span] = u2 * inv
-
-
-def divergence(q1_ref, q2_ref, start, place):
-    row0, col0, limit_row, limit_col = place
+        scale = jnp.minimum(1.0, TV * lax.rsqrt(u1 * u1 + u2 * u2))
+        q1_ref[span] = u1 * scale
+        q2_ref[span] = u2 * scale
+
+
+def divergence(q1_ref, q2_ref, start):
+    top_ok, bot_ok, left_ok, right_ok = flags()
     above = max(start - 8, 0)
     m1 = q1_ref[above : start + 16]
     m2 = q2_ref[start : start + 16]
-    r = row0 - 32 + above + iota(m1.shape, 0)
-    c = col0 - XO + iota((16, WIDE), 1)
-    m1 = jnp.where((r >= 0) & (r < limit_row), m1, 0.0)
-    m2 = jnp.where((c >= 0) & (c < limit_col), m2, 0.0)
+    row = above - 32 + iota(m1.shape, 0)
+    if above < 32:
+        m1 = unless((row < 0) & jnp.logical_not(top_ok), m1)
+    if start + 16 > 31 + ROWS:
+        m1 = unless((row >= ROWS - 1) & jnp.logical_not(bot_ok), m1)
+    lane = iota((16, 128), 1)
+    m2 = on_tile(m2, 0, lambda part: unless((lane < XO) & jnp.logical_not(left_ok), part))
+    past = (lane + 512 - XO >= COLS - 1) & jnp.logical_not(right_ok)
+    m2 = on_tile(m2, 4, lambda part: unless(past, part))
     return (m1 - rows(m1, 1))[start - above :] + (m2 - lanes(m2, 1))
-
-
-def places():
-    row = lax.axis_index("row")
-    col = lax.axis_index("col")
-    return (
-        row * ROWS,
-        col * COLS,
-        lax.axis_size("row") * ROWS - 1,
-        lax.axis_size("col") * COLS - 1,
-    )
 
 
 def masks():
@@ -492,8 +496,8 @@
 
     def put(seg, first, size, tile, blurred):
         here = slice(128 * tile, 128 * tile + 128)
-        new = (c_ref[first : first + size, here] + SIGMA * blurred) / (1.0 + SIGMA)
-        ys_ref[first : first + size, here] = jnp.where(row_ok(seg), new, 0.0)
+        new = (c_ref[first : first + size, here] + SIGMA * blurred) * (1.0 / (1.0 + SIGMA))
+        ys_ref[first : first + size, here] = new if seg == 1 else jnp.where(row_ok(seg), new, 0.0)
 
     def get_y(first, size, tile):
         return ys_ref[first : first + size, 128 * tile : 128 * tile + 128]
@@ -507,12 +511,11 @@
 def main_kernel(
     table_ref, ca_ref, cb_ref,
     xi_ref, ci_ref, oi_ref, yi_ref, q1i_ref, q2i_ref, zi_ref, ti_ref, own_ref,
-    x2_ref, y2_ref,
+    x2_ref, y2_hbm,
     side_ref, qs_ref, ys_ref, c_ref, q1_ref, q2_ref, tab_ref, t_ref, p_ref, a_ref, l_ref, f_ref,
-    z_ref, xb_ref, x1_ref,
+    z_ref, xb_ref, x1_ref, y2_ref, sem,
 ):
     top_ok, bot_ok, left_ok, right_ok = flags()
-    place = places()
     _, odd_col = parities()
     before, after = sides(ca_ref, cb_ref, odd_col)
     lf0, lf1, rt0, rt1 = before(0), before(1), after(0), after(1)
@@ -564,7 +567,7 @@
 
     def put_side(seg, first, size, tile, blurred):
         c = (c_first if tile == 0 else c_last)[first : first + size]
-        new = (c + SIGMA * blurred) / (1.0 + SIGMA)
+        new = (c + SIGMA * blurred) * (1.0 / (1.0 + SIGMA))
         new = jnp.where(col_ok(tile, size) & row_ok(seg), new, 0.0)
         old = yi_ref[first : first + size, 128 * tile : 128 * tile + 128]
         inner = between((size, 128), 96, 128) if tile == 0 else between((size, 128), 0, 32)
@@ -585,18 +588,22 @@
         ref = q2i_ref if comp else q1i_ref
         return jnp.concatenate([qs_ref[comp, 0, at], ref[at, 128:512], qs_ref[comp, 1, at]], axis=1)
 
-    total_variation(get_x, get_q, q1_ref, q2_ref, range(12), place)
+    total_variation(get_x, get_q, q1_ref, q2_ref, range(12))
     z_ref[...] = zi_ref[...]
     adjoint(SEGS1, OUTER, taps, get_side_y, l_ref, f_ref, z_ref)
-    lane = iota((16, WIDE), 1)
-    inside = ((lane >= XO) | left_ok) & ((lane < XO + COLS) | right_ok)
+    lane = iota((16, 128), 1)
     for chunk in range(12):
         start = 16 * chunk
         ext = slice(32 + start, 48 + start)
         x = get_x(start, 16)
-        new = x - TAU * (z_ref[ext, 0:WIDE] - divergence(q1_ref, q2_ref, start, place))
-        keep = inside & (top_ok if chunk < 2 else bot_ok) if chunk < 2 or chunk >= 10 else inside
-        xb_ref[start : start + 16, 0:WIDE] = jnp.where(keep, 2.0 * new - x, 0.0)
+        new = x - TAU * (z_ref[ext, 0:WIDE] - divergence(q1_ref, q2_ref, start))
+        ahead = 2.0 * new - x
+        ahead = on_tile(ahead, 0, lambda part: unless((lane < XO) & jnp.logical_not(left_ok), part))
+        past = (lane + 512 - XO >= COLS) & jnp.logical_not(right_ok)
+        ahead = on_tile(ahead, 4, lambda part: unless(past, part))
+        if chunk < 2 or chunk >= 10:
+            ahead = jnp.where(top_ok if chunk < 2 else bot_ok, ahead, 0.0)
+        xb_ref[start : start + 16, 0:WIDE] = ahead
         if 2 <= chunk < 10:
             x1_ref[start - 32 : start - 16] = new
     xb_ref[192:208, 0:WIDE] = jnp.zeros((16, WIDE), F32)
@@ -610,42 +617,53 @@
 
     def put(seg, first, size, tile, blurred):
         here = slice(128 * tile, 128 * tile + 128)
-        new = (c_ref[first : first + size, here] + SIGMA * blurred) / (1.0 + SIGMA)
-        c_ref[first : first + size, here] = jnp.where(col_ok(tile, size) & row_ok(seg), new, 0.0)
+        new = (c_ref[first : first + size, here] + SIGMA * blurred) * (1.0 / (1.0 + SIGMA))
+        if seg != 1 or tile in (0, 4):
+            new = jnp.where(col_ok(tile, size) & row_ok(seg), new, 0.0)
+        c_ref[first : first + size, here] = new
 
     def get_y(first, size, tile):
         return c_ref[first : first + size, 128 * tile : 128 * tile + 128]
 
     windows(get_xb, p_ref, range(1, 19), 192)
     blur(SEGS2, ALL, taps, p_ref, a_ref, put)
+    for chunk in range(8):
+        span = slice(16 * chunk, 16 * chunk + 16)
+        y2_ref[span] = lanes(c_ref[16 + 16 * chunk : 32 + 16 * chunk], -YO)[:, :COLS]
     total_variation(
         lambda start, count: xb_ref[start : start + count, 0:WIDE],
         lambda comp, start: (q2_ref if comp else q1_ref)[start : start + 16],
-        q1_ref, q2_ref, range(1, 10), place,
-    )
+        q1_ref, q2_ref, range(1, 10),
+    )
+    done = pltpu.make_async_copy(y2_ref, y2_hbm, sem.at[0])
+    done.start()
     z_ref[...] = jnp.zeros_like(z_ref)
     adjoint(SEGS2, ALL, taps, get_y, l_ref, f_ref, z_ref)
     for chunk in range(8):
         span = slice(16 * chunk, 16 * chunk + 16)
         ext = slice(32 + 16 * chunk, 48 + 16 * chunk)
-        div = divergence(q1_ref, q2_ref, 32 + 16 * chunk, place)
+        div = divergence(q1_ref, q2_ref, 32 + 16 * chunk)
         new = x1_ref[span] - TAU * (z_ref[ext, 0:WIDE] - div)
         x2_ref[span] = lanes(new, -XO)[:, :COLS]
-        y2_ref[span] = lanes(c_ref[16 + 16 * chunk : 32 + 16 * chunk], -YO)[:, :COLS]
+    done.wait()
 
 
 def field(*shape, dtype=F32):
     return jax.ShapeDtypeStruct(shape, dtype)
 
 
-def call(kernel, outs, scratch, *args, name, room=4, far=0, flops=0):
+def call(kernel, outs, scratch, *args, name, room=4, far=0, flops=0, out_far=0):
     spaces = [pltpu.HBM] * far + [pltpu.VMEM] * (len(args) - far)
     return pl.pallas_call(
         kernel,
         out_shape=outs,
+        out_specs=tuple(
+            pl.BlockSpec(memory_space=pltpu.HBM if i >= len(outs) - out_far else pltpu.VMEM)
+            for i in range(len(outs))
+        ),
         in_specs=[pl.BlockSpec(memory_space=space) for space in spaces],
         scratch_shapes=scratch,
-        compiler_params=pltpu.CompilerParams(vmem_limit_bytes=room * 1024 * 1024),
+        compiler_params=pltpu.CompilerParams(vmem_limit_bytes=int(room * 1024 * 1024)),
         cost_estimate=pl.CostEstimate(flops=flops, bytes_accessed=0, transcendentals=0)
         if flops
         else None,
@@ -679,7 +697,7 @@
     a, b = call(
         pack_rows_kernel, (strip, strip),
         [block, block, block, pltpu.VMEM((2, ROWS, COLS), F32), pltpu.SemaphoreType.DMA((4,))],
-        *own, psf_index, name="pack_rows", far=4, room=62,
+        *own, psf_index, name="pack_rows", far=4, room=53.3,
     )
     ra = swap(a, "row", 0)
     rb = swap(b, "row", 1)
@@ -693,7 +711,7 @@
     cb = swap(b, "col", 1)
     work = [
         pltpu.VMEM((20, 256, 128), BF16), pltpu.VMEM((20, 144, 128), F32),
-        pltpu.VMEM((20, 144, 256), BF16), pltpu.VMEM((20, 160, 128), F32),
+        pltpu.VMEM((20, 144, 256), BF16), pltpu.VMEM((20, 176, 128), F32),
     ]
     wide = field(192, WIDE)
     local = field(ROWS, WIDE)
@@ -722,8 +740,9 @@
             pltpu.VMEM((24, 1024), F32), pltpu.VMEM((6, 256, 256), BF16),
         ] + work + [
             pltpu.VMEM((272, FULL), F32), pltpu.VMEM((208, FULL), F32), pltpu.VMEM((ROWS, WIDE), F32),
+            pltpu.VMEM((ROWS, COLS), F32), pltpu.SemaphoreType.DMA((1,)),
         ],
-        normed, ca, cb, *ready, taps, name="main", room=20,
+        normed, ca, cb, *ready, taps, name="main", room=20, out_far=1,
     )
 
 

time: 31.6 us -> 30 us (0.949)
  Pallas kernels: 18.8 us -> 16.5 us
  local copies, waits for them, and re-layouts: 1.33 us -> 1.98 us
    pallas_call x5, Pallas kernels: 18.8 us -> 16.5 us  [call(): pl.pallas_call(kernel, out_shape=outs, out_specs=tuple((pl.BlockSpec(memo...]
    unnamed x12 -> x14, local copies, waits for them, and re-layouts: 0.94 us -> 1.59 us
  transfers between devices with their start and end apart: 4 -> 4, of which waited for: 1 -> 1; matrix products, arithmetic and copies ran while one was open for 2% -> 2% of each run, Pallas kernels for 20% -> 21%
where the time goes in v7:
time: 30 us; the launch traced here: 29.8 us
  Pallas kernels  16.5 us (55%)
  starting transfers between devices  6.22 us (21%)
  waiting for transfers between devices  3.93 us (13%)
  local copies, waits for them, and re-layouts  1.98 us (7%)
  between operations  0.92 us (3%)
    pallas_call x5, Pallas kernels, call(): pl.pallas_call(kernel, out_shape=outs, out_specs=tuple((pl.BlockSpec(memo...  16.5 us
    ppermute x4, starting transfers between devices, swap(): return lax.ppermute(block, ('row', 'col'), pairs)  6.22 us
    ppermute x4, waiting for transfers between devices, swap(): return lax.ppermute(block, ('row', 'col'), pairs)  3.93 us
    unnamed x14, local copies, waits for them, and re-layouts  1.59 us
  transfers between devices with their start and end apart: 4, of which 1 were waited for; matrix products, arithmetic and copies ran while one was open for 2% of the time, Pallas kernels for 21%

profile of v7, /device:TPU:96, one launch (start us, length us, event | category | flops | bytes accessed | tf_op | source)
XLA Modules:
  0.0 29.8 jit_solution(10065374206833035333)
XLA Ops:
  0.6 0.0 copy-start.4
  0.6 0.6 %copy-done.4 = s32[1,4]{1,0:T(1,128)S(1)} copy-done((s32[1,4]{1,0:T(1,128)S(1)}, s32[1,4]{1,0:T(1,128)}, u32[]{:S(2)}) %copy-start.4) | copy-done | bytes 40
  1.3 0.0 copy-start.6
  1.3 1.4 %pack_rows.1 = (bf16[240,512]{1,0:T(8,128)(2,1)S(1)}, bf16[240,512]{1,0:T(8,128)(2,1)S(1)}) custom-call(f32[128,512]{1,0:T(8,128)} %x_ref.3, f32[128,512]{1,0:T(8,128)} %y_ref.3, f32[128,512]{1,0:T(8,128)} %o_ref.3, f32[2,128,512]{2,1,0:T(8,128)} %q_ref.3, s32[1,4]{1,0:T(1,128)S(1)} %copy-done.4), custom_call_target="tpu_custom_call" | custom-call | tf_op jit(solution)/shard_map/pack_rows/pallas_call | solution.py:657
  2.7 0.1 collective-permute-start
  2.8 3.1 %collective-permute-start.1 = (bf16[240,512]{1,0:T(8,128)(2,1)S(1)}, bf16[240,512]{1,0:T(8,128)(2,1)S(1)}, u32[]{:S(2)}, u32[]{:S(2)}) collective-permute-start(bf16[240,512]{1,0:T(8,128)(2,1)S(1)} %get-tuple-element.21), channel_id=1, source_target_pairs={{0,2},{1,3},{2,0},{3,1},{4,6},{5,7},{6,4},{7,5},{8,16},{9,17},{10,... | collective-permute-start | bytes 737288 | tf_op jit(solution)/shard_map/ppermute | solution.py:689
  5.9 0.0 copy-done.6
  5.9 0.1 convert_reduce_fusion
  6.0 0.1 fusion
  6.1 0.0 copy-start.2
  6.1 0.0 copy-start.3
  6.1 0.2 rev.3
  6.3 0.0 copy-start
  6.3 0.1 pad.4
  6.4 0.0 copy-start.1
  6.4 0.0 copy-start.5
  6.4 0.1 copy.11.table_ref
  6.6 0.5 %copy-done.2 = f32[128,512]{1,0:T(8,128)S(1)} copy-done((f32[128,512]{1,0:T(8,128)S(1)}, f32[128,512]{1,0:T(8,128)}, u32[]{:S(2)}) %copy-start.2) | copy-done | bytes 262168
  7.0 0.1 copy-done.3
  7.1 0.3 copy-done
  7.4 0.1 copy-done.1
  7.5 0.0 copy-done.5
  7.5 0.8 %local.1 = (f32[128,768]{1,0:T(8,128)S(1)}, f32[128,640]{1,0:T(8,128)S(1)}, f32[128,640]{1,0:T(8,128)S(1)}, f32[128,640]{1,0:T(8,128)S(1)}, f32[128,640]{1,0:T(8,128)S(1)}, /*index=5*/bf16[4,256,256]{2,1,0:T(8,128)(2,1)S(1)}) custom-call(f32[128,512]{1,0:T(8,128)S(1)} %copy-done.1, f32[128,512]{1,0:T(8,128)S(1)} %copy-done.2, f32[128,512]{1,0:T(8,128)S(1)} %copy-done.3, ...), custom_call_target="tpu_custom_call" | custom-call | flops 4294967296 | tf_op jit(solution)/shard_map/local/pallas_call | solution.py:657
  8.3 0.0 collective-permute-done.ra_ref
  8.3 3.9 %collective-permute-done.1.rb_ref = bf16[240,512]{1,0:T(8,128)(2,1)S(1)} collective-permute-done((bf16[240,512]{1,0:T(8,128)(2,1)S(1)}, bf16[240,512]{1,0:T(8,128)(2,1)S(1)}, u32[]{:S(2)}, u32[]{:S(2)}) %collective-permute-start.1) | collective-permute-done | bytes 245792 | tf_op jit(solution)/shard_map/ppermute | solution.py:689
  12.2 0.4 %pack_cols.1 = (bf16[2,256,128]{2,1,0:T(8,128)(2,1)S(1)}, bf16[2,256,128]{2,1,0:T(8,128)(2,1)S(1)}) custom-call(f32[128,512]{1,0:T(8,128)S(1)} %copy-done.1, f32[128,512]{1,0:T(8,128)S(1)} %copy-done.2, f32[128,512]{1,0:T(8,128)S(1)} %copy-done.3, f32[2,128,512]{2,1,0:T(8,128)S(1)} %copy-done, s32[1,4]{1,0:T(1,128)S(1)} %copy-done.5, ...), custom_call_target="tpu_custom_call" | custom-call | tf_op jit(solution)/shard_map/pack_cols/pallas_call | solution.py:657
  12.6 0.4 %collective-permute-start.2 = (bf16[2,256,128]{2,1,0:T(8,128)(2,1)S(1)}, bf16[2,256,128]{2,1,0:T(8,128)(2,1)S(1)}, u32[]{:S(2)}, u32[]{:S(2)}) collective-permute-start(bf16[2,256,128]{2,1,0:T(8,128)(2,1)S(1)} %get-tuple-element.22), channel_id=1, source_target_pairs={{0,1},{1,0},{2,3},{3,2},{4,5},{5,4},{6,7},{7,6},{8,9},{9,8},{10,11... | collective-permute-start | bytes 393224 | tf_op jit(solution)/shard_map/ppermute | solution.py:689
  13.0 2.6 %collective-permute-start.3 = (bf16[2,256,128]{2,1,0:T(8,128)(2,1)S(1)}, bf16[2,256,128]{2,1,0:T(8,128)(2,1)S(1)}, u32[]{:S(2)}, u32[]{:S(2)}) collective-permute-start(bf16[2,256,128]{2,1,0:T(8,128)(2,1)S(1)} %get-tuple-element.23), channel_id=1, source_target_pairs={{0,8},{1,2},{2,1},{3,4},{4,3},{5,6},{6,5},{7,15},{8,0},{9,10},{10,... | collective-permute-start | bytes 393224 | tf_op jit(solution)/shard_map/ppermute | solution.py:689
  15.6 5.4 %middle.1 = (f32[272,768]{1,0:T(8,128)S(1)}, f32[224,640]{1,0:T(8,128)S(1)}, f32[160,640]{1,0:T(8,128)S(1)}, f32[224,640]{1,0:T(8,128)S(1)}, f32[192,640]{1,0:T(...) custom-call(f32[128,768]{1,0:T(8,128)S(1)} %get-tuple-element.24.xw_ref, ...), custom_call_target="tpu_custom_call" | custom-call | flops 8589934592 | tf_op jit(solution)/shard_map/middle/pallas_call | solution.py:657
  21.0 0.0 collective-permute-done.2.ca_ref
  21.0 0.0 collective-permute-done.3.cb_ref
  21.0 8.6 %main.1 = (f32[128,512]{1,0:T(8,128)}, f32[128,512]{1,0:T(8,128)}) custom-call(bf16[64,1024]{1,0:T(8,128)(2,1)S(1)} %copy.11.table_ref, bf16[2,256,128]{2,1,0:T(8,128)(2,1)S(1)} %collective-permute-done.2.ca_ref, bf16[2,256,128]{2,1,0:T(8,128)(2,1)S(1)} %collective-permute-done.3.cb_ref, f32[272,768]{1,0:T(8,128)S(1)} %get-tuple-element.30.xi_ref, ...), custom_call_target="tpu_custom_call" | custom-call | tf_op jit(solution)/shard_map/main/pallas_call | solution.py:657
Async XLA Ops:
  0.6 0.7 %copy-start.4 = (s32[1,4]{1,0:T(1,128)S(1)}, s32[1,4]{1,0:T(1,128)}, u32[]{:S(2)}) copy-start(s32[1,4]{1,0:T(1,128)} %idx_ref.5) | copy-start | bytes 52
  1.3 4.6 %copy-start.6 = (bf16[64,31,31]{0,2,1:T(8,128)(2,1)S(1)}, bf16[64,31,31]{0,2,1:T(8,128)(2,1)}, u32[]{:S(2)}) copy-start(bf16[64,31,31]{0,2,1:T(8,128)(2,1)} %param.7) | copy-start | bytes 369028
  2.7 5.6 %collective-permute-start = (bf16[240,512]{1,0:T(8,128)(2,1)S(1)}, bf16[240,512]{1,0:T(8,128)(2,1)S(1)}, u32[]{:S(2)}, u32[]{:S(2)}) collective-permute-start(bf16[240,512]{1,0:T(8,128)(2,1)S(1)} %get-tuple-element.20), channel_id=1, source_target_pairs={{0,8},{1,9},{2,10},{3,11},{4,12},{5,13},{6,14},{7,15},{8,0},{9,1},... | collective-permute-start | bytes 737288 | tf_op jit(solution)/shard_map/ppermute | solution.py:689
  2.8 9.4 %collective-permute-start.1 = (bf16[240,512]{1,0:T(8,128)(2,1)S(1)}, bf16[240,512]{1,0:T(8,128)(2,1)S(1)}, u32[]{:S(2)}, u32[]{:S(2)}) collective-permute-start(bf16[240,512]{1,0:T(8,128)(2,1)S(1)} %get-tuple-element.21), channel_id=1, source_target_pairs={{0,2},{1,3},{2,0},{3,1},{4,6},{5,7},{6,4},{7,5},{8,16},{9,17},{10,... | collective-permute-start | bytes 737288 | tf_op jit(solution)/shard_map/ppermute | solution.py:689
  6.1 1.0 %copy-start.2 = (f32[128,512]{1,0:T(8,128)S(1)}, f32[128,512]{1,0:T(8,128)}, u32[]{:S(2)}) copy-start(f32[128,512]{1,0:T(8,128)} %y_ref.3) | copy-start | bytes 786436
  6.1 1.0 %copy-start.3 = (f32[128,512]{1,0:T(8,128)S(1)}, f32[128,512]{1,0:T(8,128)}, u32[]{:S(2)}) copy-start(f32[128,512]{1,0:T(8,128)} %o_ref.3) | copy-start | bytes 786436
  6.3 1.1 %copy-start = (f32[2,128,512]{2,1,0:T(8,128)S(1)}, f32[2,128,512]{2,1,0:T(8,128)}, u32[]{:S(2)}) copy-start(f32[2,128,512]{2,1,0:T(8,128)} %q_ref.3) | copy-start | bytes 1572868
  6.4 1.1 %copy-start.1 = (f32[128,512]{1,0:T(8,128)S(1)}, f32[128,512]{1,0:T(8,128)}, u32[]{:S(2)}) copy-start(f32[128,512]{1,0:T(8,128)} %x_ref.3) | copy-start | bytes 786436
  6.4 1.1 %copy-start.5 = (s32[1,4]{1,0:T(1,128)S(1)}, s32[1,4]{1,0:T(1,128)}, u32[]{:S(2)}) copy-start(s32[1,4]{1,0:T(1,128)} %idx_ref.5) | copy-start | bytes 52
  12.6 8.4 %collective-permute-start.2 = (bf16[2,256,128]{2,1,0:T(8,128)(2,1)S(1)}, bf16[2,256,128]{2,1,0:T(8,128)(2,1)S(1)}, u32[]{:S(2)}, u32[]{:S(2)}) collective-permute-start(bf16[2,256,128]{2,1,0:T(8,128)(2,1)S(1)} %get-tuple-element.22), channel_id=1, source_target_pairs={{0,1},{1,0},{2,3},{3,2},{4,5},{5,4},{6,7},{7,6},{8,9},{9,8},{10,11... | collective-permute-start | bytes 393224 | tf_op jit(solution)/shard_map/ppermute | solution.py:689
  13.0 8.0 %collective-permute-start.3 = (bf16[2,256,128]{2,1,0:T(8,128)(2,1)S(1)}, bf16[2,256,128]{2,1,0:T(8,128)(2,1)S(1)}, u32[]{:S(2)}, u32[]{:S(2)}) collective-permute-start(bf16[2,256,128]{2,1,0:T(8,128)(2,1)S(1)} %get-tuple-element.23), channel_id=1, source_target_pairs={{0,8},{1,2},{2,1},{3,4},{4,3},{5,6},{6,5},{7,15},{8,0},{9,10},{10,... | collective-permute-start | bytes 393224 | tf_op jit(solution)/shard_map/ppermute | solution.py:689

commit v8 on v7

--- a/solution.py
+++ b/solution.py
@@ -148,55 +148,53 @@
         at = 0 if right else 64
         buf = jnp.where(between((256, 128), at, at + 16), part, buf)
         made.append(buf)
-        buf = jnp.concatenate([column(q_ref[0, :, own], S1, 32, 80), zeros[:64]], axis=0)
+        buf = jnp.concatenate([column(q_ref[0, :, own], S1, 32, 80)], axis=0)
         part = jnp.concatenate(
-            [column(q_ref[1, :, own], S2, 32, 112 if right else 0), zeros[:64]], axis=0
+            [column(q_ref[1, :, own], S2, 32, 112 if right else 0)], axis=0
         )
         at = 80 if right else 0
-        buf = jnp.where(between((256, 128), at, at + 32), part, buf)
+        buf = jnp.where(between((192, 128), at, at + 32), part, buf)
         shift = 0 if right else 32
         part = jnp.concatenate(
             [
-                zeros[:48],
                 lanes(strip(top, SXL, 16), shift),
                 lanes(x_lo, shift),
                 lanes(strip(bot, SXL, 16), shift),
-                zeros[:48],
+                zeros[:32],
             ],
             axis=0,
         )
         at = 112 if right else 32
-        buf = jnp.where(between((256, 128), at, at + 16), part, buf)
+        buf = jnp.where(between((192, 128), at, at + 16), part, buf)
         shift = 16 if right else 64
         part = jnp.concatenate(
             [
-                zeros[:32],
                 lanes(strip(top, SCL, 16), shift),
                 lanes(c_lo, shift),
                 lanes(strip(bot, SCL, 16), shift),
-                zeros[:64],
+                zeros[:32],
             ],
             axis=0,
         )
         at = 0 if right else 64
-        buf = jnp.where(between((256, 128), at, at + 16), part, buf)
+        buf = jnp.where(between((192, 128), at, at + 16), part, buf)
         if right:
             for comp in range(2):
                 low = lanes(split(q_ref[comp, :, own])[1], 17 + comp)
-                part = jnp.concatenate([zeros[:32], low, zeros[:96]], axis=0)
-                buf = jnp.where(between((256, 128), 16 + comp, 17 + comp), part, buf)
-        row = iota((256, 1), 0)
+                part = jnp.concatenate([zeros[:32], low, zeros[:32]], axis=0)
+                buf = jnp.where(between((192, 128), 16 + comp, 17 + comp), part, buf)
+        row = iota((192, 1), 0)
         spot = 4 if right else 1
         first = top((slice(SM, SM + 16), slice(0, 128)))[2:3, spot : spot + 1]
         last = bot((slice(SM, SM + 16), slice(0, 128)))[2:3, spot : spot + 1]
         mine = idx_ref[0:1, spot - 1 : spot].astype(F32)
         entry = jnp.where(row == 0, first, jnp.where(row == 1, mine, last))
         at = 18 if right else 112
-        buf = jnp.where(between((256, 128), at, at + 1), entry, buf)
+        buf = jnp.where(between((192, 128), at, at + 1), entry, buf)
         made.append(buf)
-    for tile in range(2):
-        a_ref[tile] = jnp.where(odd_col, made[2 + tile], made[tile]).astype(BF16)
-        b_ref[tile] = jnp.where(odd_col, made[tile], made[2 + tile]).astype(BF16)
+    for tile, span in enumerate((slice(0, 256), slice(256, 448))):
+        a_ref[span] = jnp.where(odd_col, made[2 + tile], made[tile]).astype(BF16)
+        b_ref[span] = jnp.where(odd_col, made[tile], made[2 + tile]).astype(BF16)
 
 
 def build_taps(tab_ref, t_ref, places):
@@ -332,6 +330,7 @@
                 return zero, zero
             return f_ref[b, 8 : 8 + tall], f_ref[b, 4 : 4 + tall]
 
+        spill = None
         for tile in tiles:
             both = []
             for p in range(2):
@@ -342,8 +341,15 @@
             here = slice(128 * tile, 128 * tile + 128)
             after = slice(128 * tile + 128, 128 * tile + 256)
             span = slice(first, first + tall)
-            z_ref[span, here] += both[0] + jnp.where(head, 0.0, turned)
-            z_ref[span, after] += jnp.where(head, turned, 0.0)
+            if spill is None:
+                turned_here = jnp.where(head, 0.0, turned)
+            else:
+                turned_here = jnp.where(head, spill, turned)
+            z_ref[span, here] += both[0] + turned_here
+            spill = turned
+            if tile + 1 not in tiles:
+                z_ref[span, after] += jnp.where(head, turned, 0.0)
+                spill = None
 
 
 def on_tile(value, tile, change):
@@ -518,7 +524,13 @@
     top_ok, bot_ok, left_ok, right_ok = flags()
     _, odd_col = parities()
     before, after = sides(ca_ref, cb_ref, odd_col)
-    lf0, lf1, rt0, rt1 = before(0), before(1), after(0), after(1)
+    first, second = slice(0, 256), slice(256, 448)
+    lf0, lf1, rt0, rt1 = before(first), before(second), after(first), after(second)
+    gap = jnp.zeros((48, 128), F32)
+
+    def from_row(value, count):
+        return jnp.concatenate([gap[: count // 2 - 80], value[0:160], gap[: count // 2 - 80]], axis=0)
+
     lane = iota((1, 128), 1)
     total = jnp.full((1, 128), -1.0, F32)
     for r in range(3):
@@ -536,10 +548,10 @@
     rows_ok = ((rr >= 64) | top_ok) & ((rr < 192) | bot_ok)
     shape = (256, 128)
     part = jnp.where(between(shape, 16, 80), lf0, 0.0)
-    part += jnp.where(between(shape, 64, 80), lanes(lf1, 80), 0.0)
+    part += jnp.where(between(shape, 64, 80), lanes(from_row(lf1, 256), 80), 0.0)
     side_ref[0, 0:256] = xi_ref[0:256, 0:128] + jnp.where(rows_ok & left_ok, part, 0.0)
     part = jnp.where(between(shape, 80, 128), rt0, 0.0)
-    part += jnp.where(between(shape, 80, 96), lanes(rt1, 48), 0.0)
+    part += jnp.where(between(shape, 80, 96), lanes(from_row(rt1, 256), 48), 0.0)
     side_ref[1, 0:256] = xi_ref[0:256, 512:640] + jnp.where(rows_ok & right_ok, part, 0.0)
     part = jnp.where(between(shape, 0, 16), rt0, 0.0)
     side_ref[2, 0:256] = xi_ref[0:256, 640:768] + jnp.where(rows_ok & right_ok, part, 0.0)
@@ -552,9 +564,9 @@
         part = lanes(rt1[0:192], 80 * comp)
         qs_ref[comp, 1] = jnp.where(between(shape, 80, 112), part, ref[:, 512:640])
     shape = (224, 128)
-    part = lanes(lf0[0:224], 64) + jnp.where(between(shape, 48, 64), lanes(lf1[0:224], 48), 0.0)
+    part = lanes(lf0[0:224], 64) + jnp.where(between(shape, 48, 64), lanes(from_row(lf1, 224), 48), 0.0)
     c_first = jnp.where(between(shape, 16, 64), part, ci_ref[:, 0:128])
-    part = lanes(rt0[0:224], 48) + jnp.where(between(shape, 64, 80), rt1[0:224], 0.0)
+    part = lanes(rt0[0:224], 48) + jnp.where(between(shape, 64, 80), from_row(rt1, 224), 0.0)
     c_last = jnp.where(between(shape, 64, 112), part, ci_ref[:, 512:640])
     shape = (160, 128)
     o_first = jnp.where(between(shape, 48, 64), lanes(lf0[0:160], 48), oi_ref[:, 0:128])
@@ -693,7 +705,7 @@
     own = (start_image, blur_dual, observed, tv_dual)
     block = pltpu.VMEM((ROWS, COLS), F32)
     strip = field(STRIP, COLS, dtype=BF16)
-    side = field(2, 256, 128, dtype=BF16)
+    side = field(448, 128, dtype=BF16)
     a, b = call(
         pack_rows_kernel, (strip, strip),
         [block, block, block, pltpu.VMEM((2, ROWS, COLS), F32), pltpu.SemaphoreType.DMA((4,))],

time: 30 us -> 30 us (level)
  no operation moved by 1% of the time
where the time goes in v8:
time: 30 us; the launch traced here: 29.8 us
  Pallas kernels  16.5 us (55%)
  starting transfers between devices  6.22 us (21%)
  waiting for transfers between devices  3.93 us (13%)
  local copies, waits for them, and re-layouts  1.98 us (7%)
  between operations  0.93 us (3%)
    pallas_call x5, Pallas kernels, call(): pl.pallas_call(kernel, out_shape=outs, out_specs=tuple((pl.BlockSpec(memo...  16.5 us
    ppermute x4, starting transfers between devices, swap(): return lax.ppermute(block, ('row', 'col'), pairs)  6.22 us
    ppermute x4, waiting for transfers between devices, swap(): return lax.ppermute(block, ('row', 'col'), pairs)  3.93 us
    unnamed x14, local copies, waits for them, and re-layouts  1.59 us
  transfers between devices with their start and end apart: 4, of which 1 were waited for; matrix products, arithmetic and copies ran while one was open for 2% of the time, Pallas kernels for 21%

profile of v8, /device:TPU:96, one launch (start us, length us, event | category | flops | bytes accessed | tf_op | source)
XLA Modules:
  0.0 29.8 jit_solution(16906042106805445212)
XLA Ops:
  0.6 0.0 copy-start.4
  0.6 0.6 %copy-done.4 = s32[1,4]{1,0:T(1,128)S(1)} copy-done((s32[1,4]{1,0:T(1,128)S(1)}, s32[1,4]{1,0:T(1,128)}, u32[]{:S(2)}) %copy-start.4) | copy-done | bytes 40
  1.3 0.0 copy-start.6
  1.3 1.4 %pack_rows.1 = (bf16[240,512]{1,0:T(8,128)(2,1)S(1)}, bf16[240,512]{1,0:T(8,128)(2,1)S(1)}) custom-call(f32[128,512]{1,0:T(8,128)} %x_ref.3, f32[128,512]{1,0:T(8,128)} %y_ref.3, f32[128,512]{1,0:T(8,128)} %o_ref.3, f32[2,128,512]{2,1,0:T(8,128)} %q_ref.3, s32[1,4]{1,0:T(1,128)S(1)} %copy-done.4), custom_call_target="tpu_custom_call" | custom-call | tf_op jit(solution)/shard_map/pack_rows/pallas_call | solution.py:669
  2.7 0.1 collective-permute-start
  2.8 3.1 %collective-permute-start.1 = (bf16[240,512]{1,0:T(8,128)(2,1)S(1)}, bf16[240,512]{1,0:T(8,128)(2,1)S(1)}, u32[]{:S(2)}, u32[]{:S(2)}) collective-permute-start(bf16[240,512]{1,0:T(8,128)(2,1)S(1)} %get-tuple-element.21), channel_id=1, source_target_pairs={{0,2},{1,3},{2,0},{3,1},{4,6},{5,7},{6,4},{7,5},{8,16},{9,17},{10,... | collective-permute-start | bytes 737288 | tf_op jit(solution)/shard_map/ppermute | solution.py:701
  5.9 0.0 copy-done.6
  5.9 0.1 convert_reduce_fusion
  6.0 0.1 fusion
  6.1 0.0 copy-start.2
  6.1 0.0 copy-start.3
  6.1 0.2 rev.3
  6.3 0.0 copy-start
  6.3 0.1 pad.4
  6.4 0.0 copy-start.1
  6.4 0.0 copy-start.5
  6.4 0.1 copy.11.table_ref
  6.6 0.5 %copy-done.2 = f32[128,512]{1,0:T(8,128)S(1)} copy-done((f32[128,512]{1,0:T(8,128)S(1)}, f32[128,512]{1,0:T(8,128)}, u32[]{:S(2)}) %copy-start.2) | copy-done | bytes 262168
  7.0 0.1 copy-done.3
  7.1 0.3 copy-done
  7.4 0.1 copy-done.1
  7.5 0.0 copy-done.5
  7.5 0.8 %local.1 = (f32[128,768]{1,0:T(8,128)S(1)}, f32[128,640]{1,0:T(8,128)S(1)}, f32[128,640]{1,0:T(8,128)S(1)}, f32[128,640]{1,0:T(8,128)S(1)}, f32[128,640]{1,0:T(8,128)S(1)}, /*index=5*/bf16[4,256,256]{2,1,0:T(8,128)(2,1)S(1)}) custom-call(f32[128,512]{1,0:T(8,128)S(1)} %copy-done.1, f32[128,512]{1,0:T(8,128)S(1)} %copy-done.2, f32[128,512]{1,0:T(8,128)S(1)} %copy-done.3, ...), custom_call_target="tpu_custom_call" | custom-call | flops 4294967296 | tf_op jit(solution)/shard_map/local/pallas_call | solution.py:669
  8.3 0.0 collective-permute-done.ra_ref
  8.3 3.9 %collective-permute-done.1.rb_ref = bf16[240,512]{1,0:T(8,128)(2,1)S(1)} collective-permute-done((bf16[240,512]{1,0:T(8,128)(2,1)S(1)}, bf16[240,512]{1,0:T(8,128)(2,1)S(1)}, u32[]{:S(2)}, u32[]{:S(2)}) %collective-permute-start.1) | collective-permute-done | bytes 245792 | tf_op jit(solution)/shard_map/ppermute | solution.py:701
  12.2 0.4 %pack_cols.1 = (bf16[448,128]{1,0:T(8,128)(2,1)S(1)}, bf16[448,128]{1,0:T(8,128)(2,1)S(1)}) custom-call(f32[128,512]{1,0:T(8,128)S(1)} %copy-done.1, f32[128,512]{1,0:T(8,128)S(1)} %copy-done.2, f32[128,512]{1,0:T(8,128)S(1)} %copy-done.3, f32[2,128,512]{2,1,0:T(8,128)S(1)} %copy-done, s32[1,4]{1,0:T(1,128)S(1)} %copy-done.5, ...), custom_call_target="tpu_custom_call" | custom-call | tf_op jit(solution)/shard_map/pack_cols/pallas_call | solution.py:669
  12.6 0.4 %collective-permute-start.2 = (bf16[448,128]{1,0:T(8,128)(2,1)S(1)}, bf16[448,128]{1,0:T(8,128)(2,1)S(1)}, u32[]{:S(2)}, u32[]{:S(2)}) collective-permute-start(bf16[448,128]{1,0:T(8,128)(2,1)S(1)} %get-tuple-element.22), channel_id=1, source_target_pairs={{0,1},{1,0},{2,3},{3,2},{4,5},{5,4},{6,7},{7,6},{8,9},{9,8},{10,11... | collective-permute-start | bytes 344072 | tf_op jit(solution)/shard_map/ppermute | solution.py:701
  13.0 2.6 %collective-permute-start.3 = (bf16[448,128]{1,0:T(8,128)(2,1)S(1)}, bf16[448,128]{1,0:T(8,128)(2,1)S(1)}, u32[]{:S(2)}, u32[]{:S(2)}) collective-permute-start(bf16[448,128]{1,0:T(8,128)(2,1)S(1)} %get-tuple-element.23), channel_id=1, source_target_pairs={{0,8},{1,2},{2,1},{3,4},{4,3},{5,6},{6,5},{7,15},{8,0},{9,10},{10,... | collective-permute-start | bytes 344072 | tf_op jit(solution)/shard_map/ppermute | solution.py:701
  15.6 5.4 %middle.1 = (f32[272,768]{1,0:T(8,128)S(1)}, f32[224,640]{1,0:T(8,128)S(1)}, f32[160,640]{1,0:T(8,128)S(1)}, f32[224,640]{1,0:T(8,128)S(1)}, f32[192,640]{1,0:T(...) custom-call(f32[128,768]{1,0:T(8,128)S(1)} %get-tuple-element.24.xw_ref, ...), custom_call_target="tpu_custom_call" | custom-call | flops 8589934592 | tf_op jit(solution)/shard_map/middle/pallas_call | solution.py:669
  21.0 0.0 collective-permute-done.2.ca_ref
  21.0 0.0 collective-permute-done.3.cb_ref
  21.0 8.6 %main.1 = (f32[128,512]{1,0:T(8,128)}, f32[128,512]{1,0:T(8,128)}) custom-call(bf16[64,1024]{1,0:T(8,128)(2,1)S(1)} %copy.11.table_ref, bf16[448,128]{1,0:T(8,128)(2,1)S(1)} %collective-permute-done.2.ca_ref, bf16[448,128]{1,0:T(8,128)(2,1)S(1)} %collective-permute-done.3.cb_ref, f32[272,768]{1,0:T(8,128)S(1)} %get-tuple-element.30.xi_ref, ...), custom_call_target="tpu_custom_call" | custom-call | tf_op jit(solution)/shard_map/main/pallas_call | solution.py:669
Async XLA Ops:
  0.6 0.7 %copy-start.4 = (s32[1,4]{1,0:T(1,128)S(1)}, s32[1,4]{1,0:T(1,128)}, u32[]{:S(2)}) copy-start(s32[1,4]{1,0:T(1,128)} %idx_ref.5) | copy-start | bytes 52
  1.3 4.6 %copy-start.6 = (bf16[64,31,31]{0,2,1:T(8,128)(2,1)S(1)}, bf16[64,31,31]{0,2,1:T(8,128)(2,1)}, u32[]{:S(2)}) copy-start(bf16[64,31,31]{0,2,1:T(8,128)(2,1)} %param.7) | copy-start | bytes 369028
  2.7 5.6 %collective-permute-start = (bf16[240,512]{1,0:T(8,128)(2,1)S(1)}, bf16[240,512]{1,0:T(8,128)(2,1)S(1)}, u32[]{:S(2)}, u32[]{:S(2)}) collective-permute-start(bf16[240,512]{1,0:T(8,128)(2,1)S(1)} %get-tuple-element.20), channel_id=1, source_target_pairs={{0,8},{1,9},{2,10},{3,11},{4,12},{5,13},{6,14},{7,15},{8,0},{9,1},... | collective-permute-start | bytes 737288 | tf_op jit(solution)/shard_map/ppermute | solution.py:701
  2.8 9.4 %collective-permute-start.1 = (bf16[240,512]{1,0:T(8,128)(2,1)S(1)}, bf16[240,512]{1,0:T(8,128)(2,1)S(1)}, u32[]{:S(2)}, u32[]{:S(2)}) collective-permute-start(bf16[240,512]{1,0:T(8,128)(2,1)S(1)} %get-tuple-element.21), channel_id=1, source_target_pairs={{0,2},{1,3},{2,0},{3,1},{4,6},{5,7},{6,4},{7,5},{8,16},{9,17},{10,... | collective-permute-start | bytes 737288 | tf_op jit(solution)/shard_map/ppermute | solution.py:701
  6.1 1.0 %copy-start.2 = (f32[128,512]{1,0:T(8,128)S(1)}, f32[128,512]{1,0:T(8,128)}, u32[]{:S(2)}) copy-start(f32[128,512]{1,0:T(8,128)} %y_ref.3) | copy-start | bytes 786436
  6.1 1.0 %copy-start.3 = (f32[128,512]{1,0:T(8,128)S(1)}, f32[128,512]{1,0:T(8,128)}, u32[]{:S(2)}) copy-start(f32[128,512]{1,0:T(8,128)} %o_ref.3) | copy-start | bytes 786436
  6.3 1.1 %copy-start = (f32[2,128,512]{2,1,0:T(8,128)S(1)}, f32[2,128,512]{2,1,0:T(8,128)}, u32[]{:S(2)}) copy-start(f32[2,128,512]{2,1,0:T(8,128)} %q_ref.3) | copy-start | bytes 1572868
  6.4 1.1 %copy-start.1 = (f32[128,512]{1,0:T(8,128)S(1)}, f32[128,512]{1,0:T(8,128)}, u32[]{:S(2)}) copy-start(f32[128,512]{1,0:T(8,128)} %x_ref.3) | copy-start | bytes 786436
  6.4 1.1 %copy-start.5 = (s32[1,4]{1,0:T(1,128)S(1)}, s32[1,4]{1,0:T(1,128)}, u32[]{:S(2)}) copy-start(s32[1,4]{1,0:T(1,128)} %idx_ref.5) | copy-start | bytes 52
  12.6 8.4 %collective-permute-start.2 = (bf16[448,128]{1,0:T(8,128)(2,1)S(1)}, bf16[448,128]{1,0:T(8,128)(2,1)S(1)}, u32[]{:S(2)}, u32[]{:S(2)}) collective-permute-start(bf16[448,128]{1,0:T(8,128)(2,1)S(1)} %get-tuple-element.22), channel_id=1, source_target_pairs={{0,1},{1,0},{2,3},{3,2},{4,5},{5,4},{6,7},{7,6},{8,9},{9,8},{10,11... | collective-permute-start | bytes 344072 | tf_op jit(solution)/shard_map/ppermute | solution.py:701
  13.0 8.0 %collective-permute-start.3 = (bf16[448,128]{1,0:T(8,128)(2,1)S(1)}, bf16[448,128]{1,0:T(8,128)(2,1)S(1)}, u32[]{:S(2)}, u32[]{:S(2)}) collective-permute-start(bf16[448,128]{1,0:T(8,128)(2,1)S(1)} %get-tuple-element.23), channel_id=1, source_target_pairs={{0,8},{1,2},{2,1},{3,4},{4,3},{5,6},{6,5},{7,15},{8,0},{9,10},{10,... | collective-permute-start | bytes 344072 | tf_op jit(solution)/shard_map/ppermute | solution.py:701

commit v9 on v8

--- a/solution.py
+++ b/solution.py
@@ -283,7 +283,7 @@
             put(seg, first, size, tile, blurred)
 
 
-def adjoint(segs, groups, taps, get, l_ref, f_ref, z_ref):
+def adjoint(segs, groups, taps, get, l_ref, f_ref, z_ref, keep):
     present = [b for _, blocks in groups for b in blocks]
     tiles = sorted({b // 4 for b in present})
     for seg, (first, size, padded) in enumerate(segs):
@@ -320,7 +320,8 @@
                     [part[:, :128], zero], axis=0
                 ) + jnp.concatenate([zero, part[:, 128:]], axis=0)
                 f_ref[b, padded + 24 : padded + 32] = zero[0:8]
-        tall = padded + 24
+        begin, end = max(first, keep[0]), min(first + padded + 24, keep[1])
+        tall, skip = end - begin, begin - first
         low = between((tall, 128), 0, 64)
         head = between((tall, 128), 0, 32)
 
@@ -328,7 +329,7 @@
             if b not in present:
                 zero = jnp.zeros((tall, 128), F32)
                 return zero, zero
-            return f_ref[b, 8 : 8 + tall], f_ref[b, 4 : 4 + tall]
+            return f_ref[b, 8 + skip : 8 + skip + tall], f_ref[b, 4 + skip : 4 + skip + tall]
 
         spill = None
         for tile in tiles:
@@ -340,14 +341,14 @@
             turned = lanes(both[1], 32)
             here = slice(128 * tile, 128 * tile + 128)
             after = slice(128 * tile + 128, 128 * tile + 256)
-            span = slice(first, first + tall)
+            span = slice(begin, end)
             if spill is None:
                 turned_here = jnp.where(head, 0.0, turned)
             else:
                 turned_here = jnp.where(head, spill, turned)
             z_ref[span, here] += both[0] + turned_here
             spill = turned
-            if tile + 1 not in tiles:
+            if tile < 4 and tile + 1 not in tiles:
                 z_ref[span, after] += jnp.where(head, turned, 0.0)
                 spill = None
 
@@ -511,7 +512,7 @@
     windows(get_x, p_ref, range(3, 17), 256)
     blur(SEGS1, INNER, taps, p_ref, a_ref, put)
     z_ref[...] = jnp.zeros_like(z_ref)
-    adjoint(SEGS1, INNER, taps, get_y, l_ref, f_ref, z_ref)
+    adjoint(SEGS1, INNER, taps, get_y, l_ref, f_ref, z_ref, (32, 224))
 
 
 def main_kernel(
@@ -601,8 +602,8 @@
         return jnp.concatenate([qs_ref[comp, 0, at], ref[at, 128:512], qs_ref[comp, 1, at]], axis=1)
 
     total_variation(get_x, get_q, q1_ref, q2_ref, range(12))
-    z_ref[...] = zi_ref[...]
-    adjoint(SEGS1, OUTER, taps, get_side_y, l_ref, f_ref, z_ref)
+    z_ref[32:224] = zi_ref[32:224]
+    adjoint(SEGS1, OUTER, taps, get_side_y, l_ref, f_ref, z_ref, (32, 224))
     lane = iota((16, 128), 1)
     for chunk in range(12):
         start = 16 * chunk
@@ -649,8 +650,8 @@
     )
     done = pltpu.make_async_copy(y2_ref, y2_hbm, sem.at[0])
     done.start()
-    z_ref[...] = jnp.zeros_like(z_ref)
-    adjoint(SEGS2, ALL, taps, get_y, l_ref, f_ref, z_ref)
+    z_ref[32:160] = jnp.zeros((128, WIDE), F32)
+    adjoint(SEGS2, ALL, taps, get_y, l_ref, f_ref, z_ref, (32, 160))
     for chunk in range(8):
         span = slice(16 * chunk, 16 * chunk + 16)
         ext = slice(32 + 16 * chunk, 48 + 16 * chunk)
@@ -737,7 +738,7 @@
         middle_kernel,
         (
             field(272, FULL), field(224, WIDE), field(160, WIDE), field(224, WIDE), wide, wide,
-            field(272, FULL), field(8, 256, 256, dtype=BF16),
+            field(224, WIDE), field(8, 256, 256, dtype=BF16),
         ),
         [pltpu.VMEM((24, 1024), F32)] + work,
         *fields, taps, normed, ra, rb, name="middle", room=16, flops=1 << 33,
@@ -751,7 +752,7 @@
             pltpu.VMEM((192, WIDE), F32), pltpu.VMEM((192, WIDE), F32),
             pltpu.VMEM((24, 1024), F32), pltpu.VMEM((6, 256, 256), BF16),
         ] + work + [
-            pltpu.VMEM((272, FULL), F32), pltpu.VMEM((208, FULL), F32), pltpu.VMEM((ROWS, WIDE), F32),
+            pltpu.VMEM((224, WIDE), F32), pltpu.VMEM((208, FULL), F32), pltpu.VMEM((ROWS, WIDE), F32),
             pltpu.VMEM((ROWS, COLS), F32), pltpu.SemaphoreType.DMA((1,)),
         ],
         normed, ca, cb, *ready, taps, name="main", room=20, out_far=1,

time: 30 us -> 29.7 us (0.990)
  transfers between devices with their start and end apart: 4 -> 4, of which waited for: 1 -> 1; matrix products, arithmetic and copies ran while one was open for 2% -> 2% of each run, Pallas kernels for 21% -> 20%
where the time goes in v9:
time: 29.7 us; the launch traced here: 29.6 us
  Pallas kernels  16.3 us (55%)
  starting transfers between devices  6.22 us (21%)
  waiting for transfers between devices  3.93 us (13%)
  local copies, waits for them, and re-layouts  1.98 us (7%)
  between operations  0.93 us (3%)
    pallas_call x5, Pallas kernels, call(): pl.pallas_call(kernel, out_shape=outs, out_specs=tuple((pl.BlockSpec(memo...  16.3 us
    ppermute x4, starting transfers between devices, swap(): return lax.ppermute(block, ('row', 'col'), pairs)  6.22 us
    ppermute x4, waiting for transfers between devices, swap(): return lax.ppermute(block, ('row', 'col'), pairs)  3.93 us
    unnamed x14, local copies, waits for them, and re-layouts  1.59 us
  transfers between devices with their start and end apart: 4, of which 1 were waited for; matrix products, arithmetic and copies ran while one was open for 2% of the time, Pallas kernels for 20%

profile of v9, /device:TPU:96, one launch (start us, length us, event | category | flops | bytes accessed | tf_op | source)
XLA Modules:
  0.0 29.6 jit_solution(14272573856943651428)
XLA Ops:
  0.6 0.0 copy-start.4
  0.6 0.6 %copy-done.4 = s32[1,4]{1,0:T(1,128)S(1)} copy-done((s32[1,4]{1,0:T(1,128)S(1)}, s32[1,4]{1,0:T(1,128)}, u32[]{:S(2)}) %copy-start.4) | copy-done | bytes 40
  1.3 0.0 copy-start.6
  1.3 1.4 %pack_rows.1 = (bf16[240,512]{1,0:T(8,128)(2,1)S(1)}, bf16[240,512]{1,0:T(8,128)(2,1)S(1)}) custom-call(f32[128,512]{1,0:T(8,128)} %x_ref.3, f32[128,512]{1,0:T(8,128)} %y_ref.3, f32[128,512]{1,0:T(8,128)} %o_ref.3, f32[2,128,512]{2,1,0:T(8,128)} %q_ref.3, s32[1,4]{1,0:T(1,128)S(1)} %copy-done.4), custom_call_target="tpu_custom_call" | custom-call | tf_op jit(solution)/shard_map/pack_rows/pallas_call | solution.py:670
  2.7 0.1 collective-permute-start
  2.8 3.1 %collective-permute-start.1 = (bf16[240,512]{1,0:T(8,128)(2,1)S(1)}, bf16[240,512]{1,0:T(8,128)(2,1)S(1)}, u32[]{:S(2)}, u32[]{:S(2)}) collective-permute-start(bf16[240,512]{1,0:T(8,128)(2,1)S(1)} %get-tuple-element.21), channel_id=1, source_target_pairs={{0,2},{1,3},{2,0},{3,1},{4,6},{5,7},{6,4},{7,5},{8,16},{9,17},{10,... | collective-permute-start | bytes 737288 | tf_op jit(solution)/shard_map/ppermute | solution.py:702
  5.9 0.0 copy-done.6
  5.9 0.1 convert_reduce_fusion
  6.0 0.1 fusion
  6.1 0.0 copy-start.2
  6.1 0.0 copy-start.3
  6.1 0.2 rev.3
  6.3 0.0 copy-start
  6.3 0.1 pad.4
  6.4 0.0 copy-start.1
  6.4 0.0 copy-start.5
  6.4 0.1 copy.11.table_ref
  6.6 0.5 %copy-done.2 = f32[128,512]{1,0:T(8,128)S(1)} copy-done((f32[128,512]{1,0:T(8,128)S(1)}, f32[128,512]{1,0:T(8,128)}, u32[]{:S(2)}) %copy-start.2) | copy-done | bytes 262168
  7.0 0.1 copy-done.3
  7.1 0.3 copy-done
  7.4 0.1 copy-done.1
  7.5 0.0 copy-done.5
  7.5 0.8 %local.1 = (f32[128,768]{1,0:T(8,128)S(1)}, f32[128,640]{1,0:T(8,128)S(1)}, f32[128,640]{1,0:T(8,128)S(1)}, f32[128,640]{1,0:T(8,128)S(1)}, f32[128,640]{1,0:T(8,128)S(1)}, /*index=5*/bf16[4,256,256]{2,1,0:T(8,128)(2,1)S(1)}) custom-call(f32[128,512]{1,0:T(8,128)S(1)} %copy-done.1, f32[128,512]{1,0:T(8,128)S(1)} %copy-done.2, f32[128,512]{1,0:T(8,128)S(1)} %copy-done.3, ...), custom_call_target="tpu_custom_call" | custom-call | flops 4294967296 | tf_op jit(solution)/shard_map/local/pallas_call | solution.py:670
  8.3 0.0 collective-permute-done.ra_ref
  8.3 3.9 %collective-permute-done.1.rb_ref = bf16[240,512]{1,0:T(8,128)(2,1)S(1)} collective-permute-done((bf16[240,512]{1,0:T(8,128)(2,1)S(1)}, bf16[240,512]{1,0:T(8,128)(2,1)S(1)}, u32[]{:S(2)}, u32[]{:S(2)}) %collective-permute-start.1) | collective-permute-done | bytes 245792 | tf_op jit(solution)/shard_map/ppermute | solution.py:702
  12.2 0.4 %pack_cols.1 = (bf16[448,128]{1,0:T(8,128)(2,1)S(1)}, bf16[448,128]{1,0:T(8,128)(2,1)S(1)}) custom-call(f32[128,512]{1,0:T(8,128)S(1)} %copy-done.1, f32[128,512]{1,0:T(8,128)S(1)} %copy-done.2, f32[128,512]{1,0:T(8,128)S(1)} %copy-done.3, f32[2,128,512]{2,1,0:T(8,128)S(1)} %copy-done, s32[1,4]{1,0:T(1,128)S(1)} %copy-done.5, ...), custom_call_target="tpu_custom_call" | custom-call | tf_op jit(solution)/shard_map/pack_cols/pallas_call | solution.py:670
  12.6 0.4 %collective-permute-start.2 = (bf16[448,128]{1,0:T(8,128)(2,1)S(1)}, bf16[448,128]{1,0:T(8,128)(2,1)S(1)}, u32[]{:S(2)}, u32[]{:S(2)}) collective-permute-start(bf16[448,128]{1,0:T(8,128)(2,1)S(1)} %get-tuple-element.22), channel_id=1, source_target_pairs={{0,1},{1,0},{2,3},{3,2},{4,5},{5,4},{6,7},{7,6},{8,9},{9,8},{10,11... | collective-permute-start | bytes 344072 | tf_op jit(solution)/shard_map/ppermute | solution.py:702
  13.0 2.6 %collective-permute-start.3 = (bf16[448,128]{1,0:T(8,128)(2,1)S(1)}, bf16[448,128]{1,0:T(8,128)(2,1)S(1)}, u32[]{:S(2)}, u32[]{:S(2)}) collective-permute-start(bf16[448,128]{1,0:T(8,128)(2,1)S(1)} %get-tuple-element.23), channel_id=1, source_target_pairs={{0,8},{1,2},{2,1},{3,4},{4,3},{5,6},{6,5},{7,15},{8,0},{9,10},{10,... | collective-permute-start | bytes 344072 | tf_op jit(solution)/shard_map/ppermute | solution.py:702
  15.6 5.2 %middle.1 = (f32[272,768]{1,0:T(8,128)S(1)}, f32[224,640]{1,0:T(8,128)S(1)}, f32[160,640]{1,0:T(8,128)S(1)}, f32[224,640]{1,0:T(8,128)S(1)}, f32[192,640]{1,0:T(...) custom-call(f32[128,768]{1,0:T(8,128)S(1)} %get-tuple-element.24.xw_ref, ...), custom_call_target="tpu_custom_call" | custom-call | flops 8589934592 | tf_op jit(solution)/shard_map/middle/pallas_call | solution.py:670
  20.8 0.0 collective-permute-done.2.ca_ref
  20.8 0.0 collective-permute-done.3.cb_ref
  20.8 8.6 %main.1 = (f32[128,512]{1,0:T(8,128)}, f32[128,512]{1,0:T(8,128)}) custom-call(bf16[64,1024]{1,0:T(8,128)(2,1)S(1)} %copy.11.table_ref, bf16[448,128]{1,0:T(8,128)(2,1)S(1)} %collective-permute-done.2.ca_ref, bf16[448,128]{1,0:T(8,128)(2,1)S(1)} %collective-permute-done.3.cb_ref, f32[272,768]{1,0:T(8,128)S(1)} %get-tuple-element.30.xi_ref, ...), custom_call_target="tpu_custom_call" | custom-call | tf_op jit(solution)/shard_map/main/pallas_call | solution.py:670
Async XLA Ops:
  0.6 0.7 %copy-start.4 = (s32[1,4]{1,0:T(1,128)S(1)}, s32[1,4]{1,0:T(1,128)}, u32[]{:S(2)}) copy-start(s32[1,4]{1,0:T(1,128)} %idx_ref.5) | copy-start | bytes 52
  1.3 4.6 %copy-start.6 = (bf16[64,31,31]{0,2,1:T(8,128)(2,1)S(1)}, bf16[64,31,31]{0,2,1:T(8,128)(2,1)}, u32[]{:S(2)}) copy-start(bf16[64,31,31]{0,2,1:T(8,128)(2,1)} %param.7) | copy-start | bytes 369028
  2.7 5.6 %collective-permute-start = (bf16[240,512]{1,0:T(8,128)(2,1)S(1)}, bf16[240,512]{1,0:T(8,128)(2,1)S(1)}, u32[]{:S(2)}, u32[]{:S(2)}) collective-permute-start(bf16[240,512]{1,0:T(8,128)(2,1)S(1)} %get-tuple-element.20), channel_id=1, source_target_pairs={{0,8},{1,9},{2,10},{3,11},{4,12},{5,13},{6,14},{7,15},{8,0},{9,1},... | collective-permute-start | bytes 737288 | tf_op jit(solution)/shard_map/ppermute | solution.py:702
  2.8 9.4 %collective-permute-start.1 = (bf16[240,512]{1,0:T(8,128)(2,1)S(1)}, bf16[240,512]{1,0:T(8,128)(2,1)S(1)}, u32[]{:S(2)}, u32[]{:S(2)}) collective-permute-start(bf16[240,512]{1,0:T(8,128)(2,1)S(1)} %get-tuple-element.21), channel_id=1, source_target_pairs={{0,2},{1,3},{2,0},{3,1},{4,6},{5,7},{6,4},{7,5},{8,16},{9,17},{10,... | collective-permute-start | bytes 737288 | tf_op jit(solution)/shard_map/ppermute | solution.py:702
  6.1 1.0 %copy-start.2 = (f32[128,512]{1,0:T(8,128)S(1)}, f32[128,512]{1,0:T(8,128)}, u32[]{:S(2)}) copy-start(f32[128,512]{1,0:T(8,128)} %y_ref.3) | copy-start | bytes 786436
  6.1 1.0 %copy-start.3 = (f32[128,512]{1,0:T(8,128)S(1)}, f32[128,512]{1,0:T(8,128)}, u32[]{:S(2)}) copy-start(f32[128,512]{1,0:T(8,128)} %o_ref.3) | copy-start | bytes 786436
  6.3 1.1 %copy-start = (f32[2,128,512]{2,1,0:T(8,128)S(1)}, f32[2,128,512]{2,1,0:T(8,128)}, u32[]{:S(2)}) copy-start(f32[2,128,512]{2,1,0:T(8,128)} %q_ref.3) | copy-start | bytes 1572868
  6.4 1.1 %copy-start.1 = (f32[128,512]{1,0:T(8,128)S(1)}, f32[128,512]{1,0:T(8,128)}, u32[]{:S(2)}) copy-start(f32[128,512]{1,0:T(8,128)} %x_ref.3) | copy-start | bytes 786436
  6.4 1.1 %copy-start.5 = (s32[1,4]{1,0:T(1,128)S(1)}, s32[1,4]{1,0:T(1,128)}, u32[]{:S(2)}) copy-start(s32[1,4]{1,0:T(1,128)} %idx_ref.5) | copy-start | bytes 52
  12.6 8.2 %collective-permute-start.2 = (bf16[448,128]{1,0:T(8,128)(2,1)S(1)}, bf16[448,128]{1,0:T(8,128)(2,1)S(1)}, u32[]{:S(2)}, u32[]{:S(2)}) collective-permute-start(bf16[448,128]{1,0:T(8,128)(2,1)S(1)} %get-tuple-element.22), channel_id=1, source_target_pairs={{0,1},{1,0},{2,3},{3,2},{4,5},{5,4},{6,7},{7,6},{8,9},{9,8},{10,11... | collective-permute-start | bytes 344072 | tf_op jit(solution)/shard_map/ppermute | solution.py:702
  13.0 7.8 %collective-permute-start.3 = (bf16[448,128]{1,0:T(8,128)(2,1)S(1)}, bf16[448,128]{1,0:T(8,128)(2,1)S(1)}, u32[]{:S(2)}, u32[]{:S(2)}) collective-permute-start(bf16[448,128]{1,0:T(8,128)(2,1)S(1)} %get-tuple-element.23), channel_id=1, source_target_pairs={{0,8},{1,2},{2,1},{3,4},{4,3},{5,6},{6,5},{7,15},{8,0},{9,10},{10,... | collective-permute-start | bytes 344072 | tf_op jit(solution)/shard_map/ppermute | solution.py:702

commit v10 on v9

--- a/solution.py
+++ b/solution.py
@@ -363,42 +363,49 @@
     return jnp.where(bad, 0.0, value)
 
 
-def total_variation(get_x, get_q, q1_ref, q2_ref, chunks):
+CHUNK = 32
+
+
+def chunks(first, count, body):
+    def step(i, carry):
+        body(pl.multiple_of(first + CHUNK * i, CHUNK))
+        return carry
+
+    lax.fori_loop(0, count // CHUNK, step, 0)
+
+
+def total_variation(get_x, get_q, q1_ref, q2_ref, count):
     _, bot_ok, _, right_ok = flags()
-    lane = iota((16, 128), 1)
-    past = (lane + 512 - XO >= COLS - 1) & jnp.logical_not(right_ok)
-    for chunk in chunks:
-        start = 16 * chunk
-        tall = get_x(start, 24)
-        x = tall[0:16]
-        g1 = rows(tall, -1)[0:16] - x
+
+    def body(start):
+        lane = iota((CHUNK, 128), 1)
+        past = (lane + 512 - XO >= COLS - 1) & jnp.logical_not(right_ok)
+        tall = get_x(start, CHUNK + 8)
+        x = tall[0:CHUNK]
+        row = start - 32 + iota((CHUNK, WIDE), 0)
+        g1 = unless((row >= ROWS - 1) & jnp.logical_not(bot_ok), rows(tall, -1)[0:CHUNK] - x)
         g2 = on_tile(lanes(x, -1) - x, 4, lambda part: unless(past, part))
-        if start + 16 > 31 + ROWS:
-            row = start - 32 + iota((16, WIDE), 0)
-            g1 = unless((row >= ROWS - 1) & jnp.logical_not(bot_ok), g1)
-        span = slice(start, start + 16)
         u1 = get_q(0, start) + SIGMA * g1
         u2 = get_q(1, start) + SIGMA * g2
         scale = jnp.minimum(1.0, TV * lax.rsqrt(u1 * u1 + u2 * u2))
-        q1_ref[span] = u1 * scale
-        q2_ref[span] = u2 * scale
+        q1_ref[pl.ds(start + 8, CHUNK)] = u1 * scale
+        q2_ref[pl.ds(start + 8, CHUNK)] = u2 * scale
+
+    chunks(0, count, body)
 
 
 def divergence(q1_ref, q2_ref, start):
     top_ok, bot_ok, left_ok, right_ok = flags()
-    above = max(start - 8, 0)
-    m1 = q1_ref[above : start + 16]
-    m2 = q2_ref[start : start + 16]
-    row = above - 32 + iota(m1.shape, 0)
-    if above < 32:
-        m1 = unless((row < 0) & jnp.logical_not(top_ok), m1)
-    if start + 16 > 31 + ROWS:
-        m1 = unless((row >= ROWS - 1) & jnp.logical_not(bot_ok), m1)
-    lane = iota((16, 128), 1)
+    m1 = q1_ref[pl.ds(start, CHUNK + 8)]
+    m2 = q2_ref[pl.ds(start + 8, CHUNK)]
+    row = start - 40 + iota(m1.shape, 0)
+    out = ((row < 0) & jnp.logical_not(top_ok)) | ((row >= ROWS - 1) & jnp.logical_not(bot_ok))
+    m1 = unless(out, m1)
+    lane = iota((CHUNK, 128), 1)
     m2 = on_tile(m2, 0, lambda part: unless((lane < XO) & jnp.logical_not(left_ok), part))
     past = (lane + 512 - XO >= COLS - 1) & jnp.logical_not(right_ok)
     m2 = on_tile(m2, 4, lambda part: unless(past, part))
-    return (m1 - rows(m1, 1))[start - above :] + (m2 - lanes(m2, 1))
+    return (m1 - rows(m1, 1))[8:] + (m2 - lanes(m2, 1))
 
 
 def masks():
@@ -593,32 +600,33 @@
     blur(SEGS1, OUTER, taps, p_ref, a_ref, put_side)
 
     def get_x(start, count):
-        at = slice(32 + start, 32 + start + count)
+        at = pl.ds(start + 32, count)
         return jnp.concatenate([side_ref[0, at], xi_ref[at, 128:512], side_ref[1, at]], axis=1)
 
     def get_q(comp, start):
-        at = slice(start, start + 16)
+        at = pl.ds(start, CHUNK)
         ref = q2i_ref if comp else q1i_ref
         return jnp.concatenate([qs_ref[comp, 0, at], ref[at, 128:512], qs_ref[comp, 1, at]], axis=1)
 
-    total_variation(get_x, get_q, q1_ref, q2_ref, range(12))
+    q1_ref[0:8] = jnp.zeros((8, WIDE), F32)
+    total_variation(get_x, get_q, q1_ref, q2_ref, 192)
     z_ref[32:224] = zi_ref[32:224]
     adjoint(SEGS1, OUTER, taps, get_side_y, l_ref, f_ref, z_ref, (32, 224))
-    lane = iota((16, 128), 1)
-    for chunk in range(12):
-        start = 16 * chunk
-        ext = slice(32 + start, 48 + start)
-        x = get_x(start, 16)
-        new = x - TAU * (z_ref[ext, 0:WIDE] - divergence(q1_ref, q2_ref, start))
+
+    def first_update(start):
+        lane = iota((CHUNK, 128), 1)
+        x = get_x(start, CHUNK)
+        new = x - TAU * (z_ref[pl.ds(start + 32, CHUNK)] - divergence(q1_ref, q2_ref, start))
         ahead = 2.0 * new - x
         ahead = on_tile(ahead, 0, lambda part: unless((lane < XO) & jnp.logical_not(left_ok), part))
         past = (lane + 512 - XO >= COLS) & jnp.logical_not(right_ok)
         ahead = on_tile(ahead, 4, lambda part: unless(past, part))
-        if chunk < 2 or chunk >= 10:
-            ahead = jnp.where(top_ok if chunk < 2 else bot_ok, ahead, 0.0)
-        xb_ref[start : start + 16, 0:WIDE] = ahead
-        if 2 <= chunk < 10:
-            x1_ref[start - 32 : start - 16] = new
+        row = start - 32 + iota((CHUNK, WIDE), 0)
+        keep = ((row >= 0) | top_ok) & ((row < ROWS) | bot_ok)
+        xb_ref[pl.ds(start, CHUNK), 0:WIDE] = jnp.where(keep, ahead, 0.0)
+        x1_ref[pl.ds(start, CHUNK)] = new
+
+    chunks(0, 192, first_update)
     xb_ref[192:208, 0:WIDE] = jnp.zeros((16, WIDE), F32)
     xb_ref[:, WIDE:FULL] = jnp.zeros((208, FULL - WIDE), F32)
     c_ref[:, 0:128] = ys_ref[0, 32:192] - SIGMA * o_first
@@ -640,24 +648,27 @@
 
     windows(get_xb, p_ref, range(1, 19), 192)
     blur(SEGS2, ALL, taps, p_ref, a_ref, put)
-    for chunk in range(8):
-        span = slice(16 * chunk, 16 * chunk + 16)
-        y2_ref[span] = lanes(c_ref[16 + 16 * chunk : 32 + 16 * chunk], -YO)[:, :COLS]
+
+    def put_y(start):
+        y2_ref[pl.ds(start, CHUNK)] = lanes(c_ref[pl.ds(start + 16, CHUNK)], -YO)[:, :COLS]
+
+    chunks(0, ROWS, put_y)
     total_variation(
-        lambda start, count: xb_ref[start : start + count, 0:WIDE],
-        lambda comp, start: (q2_ref if comp else q1_ref)[start : start + 16],
-        q1_ref, q2_ref, range(1, 10),
+        lambda start, count: xb_ref[pl.ds(start, count), 0:WIDE],
+        lambda comp, start: (q2_ref if comp else q1_ref)[pl.ds(start + 8, CHUNK)],
+        q1_ref, q2_ref, 160,
     )
     done = pltpu.make_async_copy(y2_ref, y2_hbm, sem.at[0])
     done.start()
     z_ref[32:160] = jnp.zeros((128, WIDE), F32)
     adjoint(SEGS2, ALL, taps, get_y, l_ref, f_ref, z_ref, (32, 160))
-    for chunk in range(8):
-        span = slice(16 * chunk, 16 * chunk + 16)
-        ext = slice(32 + 16 * chunk, 48 + 16 * chunk)
-        div = divergence(q1_ref, q2_ref, 32 + 16 * chunk)
-        new = x1_ref[span] - TAU * (z_ref[ext, 0:WIDE] - div)
-        x2_ref[span] = lanes(new, -XO)[:, :COLS]
+
+    def second_update(start):
+        div = divergence(q1_ref, q2_ref, start)
+        new = x1_ref[pl.ds(start, CHUNK)] - TAU * (z_ref[pl.ds(start, CHUNK)] - div)
+        x2_ref[pl.ds(start - 32, CHUNK)] = lanes(new, -XO)[:, :COLS]
+
+    chunks(32, ROWS, second_update)
     done.wait()
 
 
@@ -749,10 +760,10 @@
         [
             pltpu.VMEM((3, 272, 128), F32), pltpu.VMEM((2, 2, 192, 128), F32),
             pltpu.VMEM((2, 224, 128), F32), pltpu.VMEM((160, WIDE), F32),
-            pltpu.VMEM((192, WIDE), F32), pltpu.VMEM((192, WIDE), F32),
+            pltpu.VMEM((200, WIDE), F32), pltpu.VMEM((200, WIDE), F32),
             pltpu.VMEM((24, 1024), F32), pltpu.VMEM((6, 256, 256), BF16),
         ] + work + [
-            pltpu.VMEM((224, WIDE), F32), pltpu.VMEM((208, FULL), F32), pltpu.VMEM((ROWS, WIDE), F32),
+            pltpu.VMEM((224, WIDE), F32), pltpu.VMEM((208, FULL), F32), pltpu.VMEM((192, WIDE), F32),
             pltpu.VMEM((ROWS, COLS), F32), pltpu.SemaphoreType.DMA((1,)),
         ],
         normed, ca, cb, *ready, taps, name="main", room=20, out_far=1,

time: 29.7 us -> 31.4 us (1.057)
  Pallas kernels: 16.3 us -> 18 us
    pallas_call x5, Pallas kernels: 16.3 us -> 18 us  [call(): pl.pallas_call(kernel, out_shape=outs, out_specs=tuple((pl.BlockSpec(memo...]
  transfers between devices with their start and end apart: 4 -> 4, of which waited for: 1 -> 1; matrix products, arithmetic and copies ran while one was open for 2% -> 2% of each run, Pallas kernels for 20% -> 19%
where the time goes in v10:
time: 31.4 us; the launch traced here: 31.3 us
  Pallas kernels  18 us (57%)
  starting transfers between devices  6.22 us (20%)
  waiting for transfers between devices  3.93 us (13%)
  local copies, waits for them, and re-layouts  1.98 us (6%)
  between operations  0.93 us (3%)
    pallas_call x5, Pallas kernels, call(): pl.pallas_call(kernel, out_shape=outs, out_specs=tuple((pl.BlockSpec(memo...  18 us
    ppermute x4, starting transfers between devices, swap(): return lax.ppermute(block, ('row', 'col'), pairs)  6.22 us
    ppermute x4, waiting for transfers between devices, swap(): return lax.ppermute(block, ('row', 'col'), pairs)  3.93 us
    unnamed x14, local copies, waits for them, and re-layouts  1.59 us
  transfers between devices with their start and end apart: 4, of which 1 were waited for; matrix products, arithmetic and copies ran while one was open for 2% of the time, Pallas kernels for 19%

profile of v10, /device:TPU:96, one launch (start us, length us, event | category | flops | bytes accessed | tf_op | source)
XLA Modules:
  0.0 31.3 jit_solution(2495251261527391698)
XLA Ops:
  0.6 0.0 copy-start.4
  0.6 0.6 %copy-done.4 = s32[1,4]{1,0:T(1,128)S(1)} copy-done((s32[1,4]{1,0:T(1,128)S(1)}, s32[1,4]{1,0:T(1,128)}, u32[]{:S(2)}) %copy-start.4) | copy-done | bytes 40
  1.3 0.0 copy-start.6
  1.3 1.4 %pack_rows.1 = (bf16[240,512]{1,0:T(8,128)(2,1)S(1)}, bf16[240,512]{1,0:T(8,128)(2,1)S(1)}) custom-call(f32[128,512]{1,0:T(8,128)} %x_ref.3, f32[128,512]{1,0:T(8,128)} %y_ref.3, f32[128,512]{1,0:T(8,128)} %o_ref.3, f32[2,128,512]{2,1,0:T(8,128)} %q_ref.3, s32[1,4]{1,0:T(1,128)S(1)} %copy-done.4), custom_call_target="tpu_custom_call" | custom-call | tf_op jit(solution)/shard_map/pack_rows/pallas_call | solution.py:681
  2.7 0.1 collective-permute-start
  2.8 3.1 %collective-permute-start.1 = (bf16[240,512]{1,0:T(8,128)(2,1)S(1)}, bf16[240,512]{1,0:T(8,128)(2,1)S(1)}, u32[]{:S(2)}, u32[]{:S(2)}) collective-permute-start(bf16[240,512]{1,0:T(8,128)(2,1)S(1)} %get-tuple-element.21), channel_id=1, source_target_pairs={{0,2},{1,3},{2,0},{3,1},{4,6},{5,7},{6,4},{7,5},{8,16},{9,17},{10,... | collective-permute-start | bytes 737288 | tf_op jit(solution)/shard_map/ppermute | solution.py:713
  5.9 0.0 copy-done.6
  5.9 0.1 convert_reduce_fusion
  6.0 0.1 fusion
  6.1 0.0 copy-start.2
  6.1 0.0 copy-start.3
  6.1 0.2 rev.3
  6.3 0.0 copy-start
  6.3 0.1 pad.4
  6.4 0.0 copy-start.1
  6.4 0.0 copy-start.5
  6.4 0.1 copy.11.table_ref
  6.6 0.5 %copy-done.2 = f32[128,512]{1,0:T(8,128)S(1)} copy-done((f32[128,512]{1,0:T(8,128)S(1)}, f32[128,512]{1,0:T(8,128)}, u32[]{:S(2)}) %copy-start.2) | copy-done | bytes 262168
  7.0 0.1 copy-done.3
  7.1 0.3 copy-done
  7.4 0.1 copy-done.1
  7.5 0.0 copy-done.5
  7.5 0.8 %local.1 = (f32[128,768]{1,0:T(8,128)S(1)}, f32[128,640]{1,0:T(8,128)S(1)}, f32[128,640]{1,0:T(8,128)S(1)}, f32[128,640]{1,0:T(8,128)S(1)}, f32[128,640]{1,0:T(8,128)S(1)}, /*index=5*/bf16[4,256,256]{2,1,0:T(8,128)(2,1)S(1)}) custom-call(f32[128,512]{1,0:T(8,128)S(1)} %copy-done.1, f32[128,512]{1,0:T(8,128)S(1)} %copy-done.2, f32[128,512]{1,0:T(8,128)S(1)} %copy-done.3, ...), custom_call_target="tpu_custom_call" | custom-call | flops 4294967296 | tf_op jit(solution)/shard_map/local/pallas_call | solution.py:681
  8.3 0.0 collective-permute-done.ra_ref
  8.3 3.9 %collective-permute-done.1.rb_ref = bf16[240,512]{1,0:T(8,128)(2,1)S(1)} collective-permute-done((bf16[240,512]{1,0:T(8,128)(2,1)S(1)}, bf16[240,512]{1,0:T(8,128)(2,1)S(1)}, u32[]{:S(2)}, u32[]{:S(2)}) %collective-permute-start.1) | collective-permute-done | bytes 245792 | tf_op jit(solution)/shard_map/ppermute | solution.py:713
  12.2 0.4 %pack_cols.1 = (bf16[448,128]{1,0:T(8,128)(2,1)S(1)}, bf16[448,128]{1,0:T(8,128)(2,1)S(1)}) custom-call(f32[128,512]{1,0:T(8,128)S(1)} %copy-done.1, f32[128,512]{1,0:T(8,128)S(1)} %copy-done.2, f32[128,512]{1,0:T(8,128)S(1)} %copy-done.3, f32[2,128,512]{2,1,0:T(8,128)S(1)} %copy-done, s32[1,4]{1,0:T(1,128)S(1)} %copy-done.5, ...), custom_call_target="tpu_custom_call" | custom-call | tf_op jit(solution)/shard_map/pack_cols/pallas_call | solution.py:681
  12.6 0.4 %collective-permute-start.2 = (bf16[448,128]{1,0:T(8,128)(2,1)S(1)}, bf16[448,128]{1,0:T(8,128)(2,1)S(1)}, u32[]{:S(2)}, u32[]{:S(2)}) collective-permute-start(bf16[448,128]{1,0:T(8,128)(2,1)S(1)} %get-tuple-element.22), channel_id=1, source_target_pairs={{0,1},{1,0},{2,3},{3,2},{4,5},{5,4},{6,7},{7,6},{8,9},{9,8},{10,11... | collective-permute-start | bytes 344072 | tf_op jit(solution)/shard_map/ppermute | solution.py:713
  13.0 2.6 %collective-permute-start.3 = (bf16[448,128]{1,0:T(8,128)(2,1)S(1)}, bf16[448,128]{1,0:T(8,128)(2,1)S(1)}, u32[]{:S(2)}, u32[]{:S(2)}) collective-permute-start(bf16[448,128]{1,0:T(8,128)(2,1)S(1)} %get-tuple-element.23), channel_id=1, source_target_pairs={{0,8},{1,2},{2,1},{3,4},{4,3},{5,6},{6,5},{7,15},{8,0},{9,10},{10,... | collective-permute-start | bytes 344072 | tf_op jit(solution)/shard_map/ppermute | solution.py:713
  15.6 5.2 %middle.1 = (f32[272,768]{1,0:T(8,128)S(1)}, f32[224,640]{1,0:T(8,128)S(1)}, f32[160,640]{1,0:T(8,128)S(1)}, f32[224,640]{1,0:T(8,128)S(1)}, f32[192,640]{1,0:T(...) custom-call(f32[128,768]{1,0:T(8,128)S(1)} %get-tuple-element.24.xw_ref, ...), custom_call_target="tpu_custom_call" | custom-call | flops 8589934592 | tf_op jit(solution)/shard_map/middle/pallas_call | solution.py:681
  20.8 0.0 collective-permute-done.2.ca_ref
  20.8 0.0 collective-permute-done.3.cb_ref
  20.8 10.3 %main.1 = (f32[128,512]{1,0:T(8,128)}, f32[128,512]{1,0:T(8,128)}) custom-call(bf16[64,1024]{1,0:T(8,128)(2,1)S(1)} %copy.11.table_ref, bf16[448,128]{1,0:T(8,128)(2,1)S(1)} %collective-permute-done.2.ca_ref, bf16[448,128]{1,0:T(8,128)(2,1)S(1)} %collective-permute-done.3.cb_ref, f32[272,768]{1,0:T(8,128)S(1)} %get-tuple-element.30.xi_ref, ...), custom_call_target="tpu_custom_call" | custom-call | tf_op jit(solution)/shard_map/main/pallas_call | solution.py:681
Async XLA Ops:
  0.6 0.7 %copy-start.4 = (s32[1,4]{1,0:T(1,128)S(1)}, s32[1,4]{1,0:T(1,128)}, u32[]{:S(2)}) copy-start(s32[1,4]{1,0:T(1,128)} %idx_ref.5) | copy-start | bytes 52
  1.3 4.6 %copy-start.6 = (bf16[64,31,31]{0,2,1:T(8,128)(2,1)S(1)}, bf16[64,31,31]{0,2,1:T(8,128)(2,1)}, u32[]{:S(2)}) copy-start(bf16[64,31,31]{0,2,1:T(8,128)(2,1)} %param.7) | copy-start | bytes 369028
  2.7 5.6 %collective-permute-start = (bf16[240,512]{1,0:T(8,128)(2,1)S(1)}, bf16[240,512]{1,0:T(8,128)(2,1)S(1)}, u32[]{:S(2)}, u32[]{:S(2)}) collective-permute-start(bf16[240,512]{1,0:T(8,128)(2,1)S(1)} %get-tuple-element.20), channel_id=1, source_target_pairs={{0,8},{1,9},{2,10},{3,11},{4,12},{5,13},{6,14},{7,15},{8,0},{9,1},... | collective-permute-start | bytes 737288 | tf_op jit(solution)/shard_map/ppermute | solution.py:713
  2.8 9.4 %collective-permute-start.1 = (bf16[240,512]{1,0:T(8,128)(2,1)S(1)}, bf16[240,512]{1,0:T(8,128)(2,1)S(1)}, u32[]{:S(2)}, u32[]{:S(2)}) collective-permute-start(bf16[240,512]{1,0:T(8,128)(2,1)S(1)} %get-tuple-element.21), channel_id=1, source_target_pairs={{0,2},{1,3},{2,0},{3,1},{4,6},{5,7},{6,4},{7,5},{8,16},{9,17},{10,... | collective-permute-start | bytes 737288 | tf_op jit(solution)/shard_map/ppermute | solution.py:713
  6.1 1.0 %copy-start.2 = (f32[128,512]{1,0:T(8,128)S(1)}, f32[128,512]{1,0:T(8,128)}, u32[]{:S(2)}) copy-start(f32[128,512]{1,0:T(8,128)} %y_ref.3) | copy-start | bytes 786436
  6.1 1.0 %copy-start.3 = (f32[128,512]{1,0:T(8,128)S(1)}, f32[128,512]{1,0:T(8,128)}, u32[]{:S(2)}) copy-start(f32[128,512]{1,0:T(8,128)} %o_ref.3) | copy-start | bytes 786436
  6.3 1.1 %copy-start = (f32[2,128,512]{2,1,0:T(8,128)S(1)}, f32[2,128,512]{2,1,0:T(8,128)}, u32[]{:S(2)}) copy-start(f32[2,128,512]{2,1,0:T(8,128)} %q_ref.3) | copy-start | bytes 1572868
  6.4 1.1 %copy-start.1 = (f32[128,512]{1,0:T(8,128)S(1)}, f32[128,512]{1,0:T(8,128)}, u32[]{:S(2)}) copy-start(f32[128,512]{1,0:T(8,128)} %x_ref.3) | copy-start | bytes 786436
  6.4 1.1 %copy-start.5 = (s32[1,4]{1,0:T(1,128)S(1)}, s32[1,4]{1,0:T(1,128)}, u32[]{:S(2)}) copy-start(s32[1,4]{1,0:T(1,128)} %idx_ref.5) | copy-start | bytes 52
  12.6 8.2 %collective-permute-start.2 = (bf16[448,128]{1,0:T(8,128)(2,1)S(1)}, bf16[448,128]{1,0:T(8,128)(2,1)S(1)}, u32[]{:S(2)}, u32[]{:S(2)}) collective-permute-start(bf16[448,128]{1,0:T(8,128)(2,1)S(1)} %get-tuple-element.22), channel_id=1, source_target_pairs={{0,1},{1,0},{2,3},{3,2},{4,5},{5,4},{6,7},{7,6},{8,9},{9,8},{10,11... | collective-permute-start | bytes 344072 | tf_op jit(solution)/shard_map/ppermute | solution.py:713
  13.0 7.8 %collective-permute-start.3 = (bf16[448,128]{1,0:T(8,128)(2,1)S(1)}, bf16[448,128]{1,0:T(8,128)(2,1)S(1)}, u32[]{:S(2)}, u32[]{:S(2)}) collective-permute-start(bf16[448,128]{1,0:T(8,128)(2,1)S(1)} %get-tuple-element.23), channel_id=1, source_target_pairs={{0,8},{1,2},{2,1},{3,4},{4,3},{5,6},{6,5},{7,15},{8,0},{9,10},{10,... | collective-permute-start | bytes 344072 | tf_op jit(solution)/shard_map/ppermute | solution.py:713
